TPU v7x, 32 devices: a whole 2x2x4 slice. The times are simulated.
32 devices in a mesh: patch: 4 (over x, core), space: 8 (over z, y).
Axes of the slice: x: 2, y: 2, z: 4, core: 2. Of those that a mesh axis runs over, the one named last changes fastest.
Arguments:
- image: bfloat16 [32, 16, 256], P('patch', 'space'), may hold values from -6 to 6
- offsets: int32 [4, 2], replicated, may hold values from 0 to 128, as said below
- conv1_weight: bfloat16 [9, 32, 3], replicated, may hold values from -1.25 to 1.25
- conv2_weight: bfloat16 [9, 32, 96], replicated, may hold values from -0.21875 to 0.21875
- norm1_gain: float32 [32], replicated, may hold values from 0.1 to 1.9
- norm1_bias: float32 [32], replicated, may hold values from -3 to 3
- norm2_gain: float32 [32], replicated, may hold values from 0.1 to 1.9
- norm2_bias: float32 [32], replicated, may hold values from -3 to 3
- head_weight: bfloat16 [3, 32], replicated, may hold values from -1 to 1
- head_bias: float32 [3], replicated, may hold values from -3 to 3
Outputs:
- volume_logits: float32 [32, 3, 16, 256], P('patch', None, 'space')
Inputs may be any that keep to these rules, and one draw needn't show every extreme that they name: offsets[p] = (oz, ox) with 0 <= oz <= 16 and 0 <= ox <= 128; some patch starts at oz = 16, some at ox = 128, some at ox = 0.
All inputs are finite; a program needn't handle non-finite values.
Results may differ from a plain program's by a relative error of at most 0.0024.
Values may be sent and summed in bfloat16 or wider, within the bound.
No kernel may reach another device: no remote copies, remote signals or barrier semaphores. Data moves between devices by JAX's collectives and lax.ppermute only.
A program may use at most 64 MiB of HBM per device.

v0:
```python
import jax
import jax.numpy as jnp
from jax import lax
from jax.sharding import PartitionSpec as P

PX = 128
PZ = 16


def padded_2(cells, sides, width):
    for axis, dim in sides:
        count = lax.axis_size(axis)
        ends = count - 1
        head = lax.slice_in_dim(cells, 0, width, axis=dim)
        tail = lax.slice_in_dim(cells, cells.shape[dim] - width, cells.shape[dim], axis=dim)
        cells = jnp.concatenate(
            [
                lax.ppermute(tail, axis, [(i, (i + 1) % count) for i in range(ends)]),
                cells,
                lax.ppermute(head, axis, [((i + 1) % count, i) for i in range(ends)]),
            ],
            axis=dim,
        )
    return cells


def gauss_value(positions, length):
    center = (length - 1) / 2.0
    deviation = length / 8.0
    offset = positions - center
    return jnp.exp(-(offset * offset) / (2.0 * deviation * deviation))


def apply_taps(padded, weights):
    depth_cells = padded.shape[2] - 2
    row_cells = padded.shape[3] - 2
    col_cells = padded.shape[4] - 2
    stacked = jnp.concatenate(
        [padded[:, :, :, :, col_shift : col_shift + col_cells] for col_shift in range(3)], axis=1
    )
    summed = jnp.zeros(
        (padded.shape[0], weights.shape[1], depth_cells, row_cells, col_cells), jnp.float32
    )
    for depth_tap in range(3):
        for row_tap in range(3):
            window = stacked[
                :, :, depth_tap : depth_tap + depth_cells, row_tap : row_tap + row_cells, :
            ]
            summed = summed + jnp.einsum(
                "oc,fczyx->fozyx",
                weights[depth_tap * 3 + row_tap],
                window,
                preferred_element_type=jnp.float32,
            )
    return summed


def convolve(features, weights):
    bordered = padded_2(features, (("space", 3),), 1)
    padded = jnp.pad(bordered, ((0, 0), (0, 0), (1, 1), (0, 0), (1, 1)))
    return apply_taps(padded, weights)


def normalize(values, channel_gain, channel_bias, cell_count):
    firsts, seconds = lax.psum(
        (jnp.sum(values, axis=(2, 3, 4)), jnp.sum(values * values, axis=(2, 3, 4))), "space"
    )
    average = firsts / cell_count
    variance = seconds / cell_count - average * average
    centered = values - average[:, :, None, None, None]
    factor = lax.rsqrt(variance + 1e-05) * channel_gain[None, :]
    shifted = centered * factor[:, :, None, None, None] + channel_bias[None, :, None, None, None]
    return jnp.where(shifted >= 0, shifted, 0.01 * shifted).astype(jnp.bfloat16)


def place_patch(contrib, corner, first_row, row_count, width_cells):
    padded = jnp.pad(
        contrib, ((row_count, row_count), (0, 0), (0, 0), (width_cells - PX, width_cells - PX))
    )
    first_slot = jnp.clip(first_row - corner[0] + row_count, 0, PZ + row_count)
    picked = lax.dynamic_slice_in_dim(padded, first_slot, row_count, 0)
    return lax.dynamic_slice_in_dim(picked, width_cells - PX - corner[1], width_cells, 3)


def local(
    image,
    offsets,
    conv1_weight,
    conv2_weight,
    norm1_gain,
    norm1_bias,
    norm2_gain,
    norm2_bias,
    head_weight,
    head_bias,
):
    groups = lax.axis_size("patch")
    group_index = lax.axis_index("patch")
    spaces = lax.axis_size("space")
    band_index = lax.axis_index("space")
    slab_rows = image.shape[0]
    band_rows = image.shape[1]
    width_cells = image.shape[2]
    patch_rows = band_rows * spaces
    per_group = offsets.shape[0] // groups
    own_corners = lax.dynamic_slice_in_dim(offsets, group_index * per_group, per_group, 0)
    shard_part = lax.all_gather(image, "patch", axis=0, tiled=True)
    row_count = shard_part.shape[0]
    padded = jnp.pad(shard_part, ((PZ, PZ), (0, 0), (0, 0)))

    def one_corner(corner):
        first_slot = jnp.clip(corner[0] + PZ, 0, row_count + PZ)
        picked = lax.dynamic_slice_in_dim(padded, first_slot, PZ, 0)
        return lax.dynamic_slice_in_dim(picked, corner[1], PX, 2)

    patches = jax.vmap(one_corner)(own_corners)
    gauss_depth = gauss_value(jnp.arange(PZ, dtype=jnp.float32), PZ)
    band_positions = (band_index * band_rows + jnp.arange(band_rows, dtype=jnp.int32)).astype(
        jnp.float32
    )
    gauss_band = gauss_value(band_positions, patch_rows)
    gauss_cols = gauss_value(jnp.arange(PX, dtype=jnp.float32), PX)
    weight_map = gauss_depth[:, None, None] * gauss_band[None, :, None] * gauss_cols[None, None, :]
    cell_count = float(PZ * patch_rows * PX)

    def one_patch(patch_cells):
        flipped = jnp.stack(
            [patch_cells, patch_cells[::-1], patch_cells[:, :, ::-1], patch_cells[::-1, :, ::-1]]
        )[:, None]
        hidden = normalize(convolve(flipped, conv1_weight), norm1_gain, norm1_bias, cell_count)
        hidden = normalize(convolve(hidden, conv2_weight), norm2_gain, norm2_bias, cell_count)
        logits = jnp.einsum(
            "kc,fczyx->fzkyx", head_weight, hidden, preferred_element_type=jnp.float32
        )
        logits = logits + head_bias[None, None, :, None, None]
        restored = (
            logits[0] + logits[1][::-1] + logits[2][:, :, :, ::-1] + logits[3][::-1, :, :, ::-1]
        )
        return restored * 0.25 * weight_map[:, None, :, :]

    contribs = lax.map(one_patch, patches)
    empty = jnp.zeros((slab_rows, contribs.shape[2], band_rows, width_cells), jnp.float32)
    shard_part = lax.all_gather(contribs, "patch", axis=0, tiled=True)

    def add_one(item_index, gathered_sum):
        corner = lax.dynamic_index_in_dim(offsets, item_index, 0, keepdims=False)
        contrib = lax.dynamic_index_in_dim(shard_part, item_index, 0, keepdims=False)
        return gathered_sum + place_patch(
            contrib, corner, group_index * slab_rows, slab_rows, width_cells
        )

    blended = lax.fori_loop(0, shard_part.shape[0], add_one, empty)
    slab_positions = group_index * slab_rows + jnp.arange(slab_rows, dtype=jnp.int32)
    rel_depth = slab_positions[None, :] - offsets[:, 0:1]
    depth_weights = jnp.where(
        (rel_depth >= 0) & (rel_depth < PZ), gauss_value(rel_depth.astype(jnp.float32), PZ), 0.0
    )
    col_positions = jnp.arange(width_cells, dtype=jnp.int32)
    rel_cols = col_positions[None, :] - offsets[:, 1:2]
    col_weights = jnp.where(
        (rel_cols >= 0) & (rel_cols < PX), gauss_value(rel_cols.astype(jnp.float32), PX), 0.0
    )
    plane = jnp.dot(
        depth_weights.T,
        col_weights,
        precision=lax.Precision.HIGHEST,
        preferred_element_type=jnp.float32,
    )
    coverage = plane[:, None, :] * gauss_band[None, :, None]
    return blended / jnp.maximum(coverage, 0.1)[:, None, :, :]


def solution(mesh):
    return jax.shard_map(
        local,
        mesh=mesh,
        in_specs=(P("patch", "space", None), P(), P(), P(), P(), P(), P(), P(), P(), P()),
        out_specs=P("patch", None, "space", None),
        check_vma=False,
    )
```

profile of v0, /device:TPU:0, one launch (start us, length us, event | category | flops | bytes accessed | tf_op | source)
XLA Modules:
  0.0 118.6 jit_solution(9886160090441819158)
XLA Ops:
  0.0 0.8 constant_dynamic-slice_fusion.1
  3.2 0.7 copy.17
  3.9 6.2 %all_gather.6 = bf16[32,2,256]{2,0,1:T(8,128)(2,1)S(1)} all-gather(bf16[8,2,256]{2,0,1:T(8,128)(2,1)S(1)} %copy.17), channel_id=1, replica_groups=mesh['patch'=4,'space'=8] {'patch'}, dimensions={0}, use_global_device_ids=true | all-gather | bytes 40960 | tf_op jit(solution)/shard_map/all_gather | solution.py:107
  11.4 3.9 %collective-permute-start = (bf16[4,1,16,1,128]{4,1,3,2,0:T(2,128)(2,1)S(1)}, bf16[4,1,16,1,128]{4,1,3,2,0:T(2,128)(2,1)S(1)}, u32[]{:S(2)}, u32[]{:S(2)}) collective-permute-start(bf16[4,1,16,1,128]{4,1,3,2,0:T(2,128)(2,1)S(1)} %get-tuple-element.281), channel_id=1, source_target_pairs={{0,1},{1,2},{2,3},{3,4},{4,5},{5,6},{6,7},{8,9},{9,10},{10,11},{11... | collective-permute-start | bytes 49160 | tf_op jit(solution)/shard_map/while/body/eval_jaxpr/ppermute | solution.py:18
  15.3 1.3 %collective-permute-start.1 = (bf16[4,1,16,1,128]{4,1,3,2,0:T(2,128)(2,1)S(1)}, bf16[4,1,16,1,128]{4,1,3,2,0:T(2,128)(2,1)S(1)}, u32[]{:S(2)}, u32[]{:S(2)}) collective-permute-start(bf16[4,1,16,1,128]{4,1,3,2,0:T(2,128)(2,1)S(1)} %get-tuple-element.282), channel_id=1, source_target_pairs={{1,0},{2,1},{3,2},{4,3},{5,4},{6,5},{7,6},{9,8},{10,9},{11,10},{12... | collective-permute-start | bytes 49160 | tf_op jit(solution)/shard_map/while/body/eval_jaxpr/ppermute | solution.py:20
  16.6 0.8 slice_bitcast_fusion.5
  17.7 3.4 %collective-permute-done.1 = bf16[4,1,16,1,128]{4,1,3,2,0:T(2,128)(2,1)S(1)} collective-permute-done((bf16[4,1,16,1,128]{4,1,3,2,0:T(2,128)(2,1)S(1)}, bf16[4,1,16,1,128]{4,1,3,2,0:T(2,128)(2,1)S(1)}, u32[]{:S(2)}, u32[]{:S(2)}) %collective-permute-start.1) | collective-permute-done | bytes 16416 | tf_op jit(solution)/shard_map/while/body/eval_jaxpr/ppermute | solution.py:20
  21.6 0.6 fusion.134
  22.2 1.2 fusion.101
  26.8 1.6 %bitcast_reduce_fusion.1 = (f32[4,32]{1,0:T(4,128)S(1)}, f32[4,32]{1,0:T(4,128)S(1)}, f32[4,16,2,128,32]{3,4,2,1,0:T(8,128)S(1)}) fusion(bf16[9,32,3]{1,2,0:T(4,128)(2,1)S(1)} %copy-done.3, f32[4,16,2,128,32]{3,4,2,1,0:T(8,128)S(1)} %fusion.89, f32[4,16,2,128,32]{3,4,2,1,0:T(8,128)S(1)} %fusion.91, f32[4,16,2,128,32]{3,4,2,1,0:T(8,128)S(1)} %fusion.93, ...), kind=kOutput, calls=%fused_computation.47 | convolution fusion | flops 9576192 | bytes 19318784 | tf_op jit(solution)/shard_map/while/body/eval_jaxpr/oc,fczyx->fozyx/dot_general | solution.py:49
  28.4 19.9 %all-reduce.7 = (f32[4,32]{1,0:T(4,128)S(1)}, f32[4,32]{1,0:T(4,128)S(1)}) all-reduce(f32[4,32]{1,0:T(4,128)S(1)} %get-tuple-element.253, f32[4,32]{1,0:T(4,128)S(1)} %get-tuple-element.252), channel_id=1, replica_groups=mesh['patch'=4,'space'=8] {'space'}, use_global_device_ids=true, to_apply=%region_3.4 | all-reduce | flops 256 | bytes 2048 | tf_op jit(solution)/shard_map/while/body/eval_jaxpr/psum | solution.py:65
  48.3 0.7 fusion.25
  49.1 1.6 %collective-permute-start.2 = (bf16[4,32,16,1,128]{4,1,3,2,0:T(8,128)(2,1)S(1)}, bf16[4,32,16,1,128]{4,1,3,2,0:T(8,128)(2,1)S(1)}, u32[]{:S(2)}, u32[]{:S(2)}) collective-permute-start(bf16[4,32,16,1,128]{4,1,3,2,0:T(8,128)(2,1)S(1)} %get-tuple-element.273), channel_id=1, source_target_pairs={{0,1},{1,2},{2,3},{3,4},{4,5},{5,6},{6,7},{8,9},{9,10},{10,11},{11... | collective-permute-start | bytes 1572872 | tf_op jit(solution)/shard_map/while/body/eval_jaxpr/ppermute | solution.py:18
  50.7 1.5 %collective-permute-start.3 = (bf16[4,32,16,1,128]{4,1,3,2,0:T(8,128)(2,1)S(1)}, bf16[4,32,16,1,128]{4,1,3,2,0:T(8,128)(2,1)S(1)}, u32[]{:S(2)}, u32[]{:S(2)}) collective-permute-start(bf16[4,32,16,1,128]{4,1,3,2,0:T(8,128)(2,1)S(1)} %get-tuple-element.274), channel_id=1, source_target_pairs={{1,0},{2,1},{3,2},{4,3},{5,4},{6,5},{7,6},{9,8},{10,9},{11,10},{12... | collective-permute-start | bytes 1572872 | tf_op jit(solution)/shard_map/while/body/eval_jaxpr/ppermute | solution.py:20
  52.4 16.5 %collective-permute-done.2 = bf16[4,32,16,1,128]{4,1,3,2,0:T(8,128)(2,1)S(1)} collective-permute-done((bf16[4,32,16,1,128]{4,1,3,2,0:T(8,128)(2,1)S(1)}, bf16[4,32,16,1,128]{4,1,3,2,0:T(8,128)(2,1)S(1)}, u32[]{:S(2)}, u32[]{:S(2)}) %collective-permute-start.2) | collective-permute-done | bytes 524320 | tf_op jit(solution)/shard_map/while/body/eval_jaxpr/ppermute | solution.py:18
  68.9 2.7 %select_maximum_fusion = bf16[4,32,18,4,130]{4,1,3,2,0:T(8,128)(2,1)S(1)} fusion(bf16[4,32,16,1,128]{4,1,3,2,0:T(8,128)(2,1)S(1)} %collective-permute-done.3, bf16[4,32,16,2,128]{4,1,3,2,0:T(8,128)(2,1)S(1)} %fusion.25, bf16[4,32,16,1,128]{4,1,3,2,0:T(8,128)(2,1)S(1)} %collective-permute-done.2), kind=kLoop, calls=%fused_computation.14 | loop fusion | flops 22763520 | bytes 4493312 | tf_op jit(solution)/shard_map/while/body/eval_jaxpr/concatenate | solution.py:16
  71.6 1.9 %fusion.132 = (bf16[4,32,18,4,128]{4,1,3,2,0:T(8,128)(2,1)S(1)}, bf16[4,32,18,4,128]{4,1,3,2,0:T(8,128)(2,1)S(1)}, bf16[4,32,18,4,128]{4,1,3,2,0:T(8,128)(2,1)S(1)}) fusion(bf16[4,32,18,4,130]{4,1,3,2,0:T(8,128)(2,1)S(1)} %select_maximum_fusion), kind=kLoop, calls=%fused_computation.176 | loop fusion | bytes 14155776 | tf_op jit(solution)/shard_map/while/body/eval_jaxpr/slice | solution.py:39
  73.5 0.8 pad_maximum_fusion
  78.8 1.5 %bitcast_reduce_fusion = (f32[4,32]{1,0:T(4,128)S(1)}, f32[4,32]{1,0:T(4,128)S(1)}, f32[4,16,2,128,32]{3,4,2,1,0:T(8,128)S(1)}) fusion(bf16[4,96,18,4,128]{4,1,3,2,0:T(8,128)(2,1)S(1)} %pad_maximum_fusion, bf16[9,32,96]{2,1,0:T(8,128)(2,1)S(1)} %copy-done.1, f32[4,16,2,128,32]{3,4,2,1,0:T(8,128)S(1)} %fusion.9, f32[4,16,2,128,32]{3,4,2,1,0:T(8,128)S(1)} %fusion.11, ...), kind=kOutput, calls=%fused_computation.41 | convolution fusion | flops 106430208 | bytes 22029312 | tf_op jit(solution)/shard_map/while/body/eval_jaxpr/oc,fczyx->fozyx/dot_general | solution.py:49
  80.3 19.6 %all-reduce.6 = (f32[4,32]{1,0:T(4,128)S(1)}, f32[4,32]{1,0:T(4,128)S(1)}) all-reduce(f32[4,32]{1,0:T(4,128)S(1)} %get-tuple-element.251, f32[4,32]{1,0:T(4,128)S(1)} %get-tuple-element.250), channel_id=1, replica_groups=mesh['patch'=4,'space'=8] {'space'}, use_global_device_ids=true, to_apply=%region_7.8 | all-reduce | flops 256 | bytes 2048 | tf_op jit(solution)/shard_map/while/body/eval_jaxpr/psum | solution.py:65
  100.0 0.6 fusion.35
  101.0 5.6 %all-gather = f32[64,3,2,128]{3,2,1,0:T(2,128)S(1)} all-gather(f32[16,3,2,128]{3,2,1,0:T(2,128)S(1)} %copy.21), channel_id=2, replica_groups=mesh['patch'=4,'space'=8] {'patch'}, dimensions={0}, use_global_device_ids=true | all-gather | bytes 245760 | tf_op jit(solution)/shard_map/all_gather | solution.py:143
  106.6 11.3 %while.23 = (s32[]{:T(128)}, f32[8,3,2,256]{3,2,1,0:T(2,128)S(1)}, f32[4,16,3,2,128]{4,3,2,1,0:T(2,128)S(1)}, s32[4,2]{0,1:T(2,128)S(1)}, s32[]{:T(128)}, /*inde...) while((s32[]{:T(128)}, f32[8,3,2,256]{3,2,1,0:T(2,128)S(1)}, ...), condition=%wide.region_9.10_spmd.clone, body=%wide.region_8.9_spmd.clone.sunk | while | flops 24589 | bytes 246061 | solution.py:152
  118.0 0.6 broadcast_divide_fusion
  (78 shorter events, 14.2 us)
Async XLA Ops:
  0.0 100.0 %copy-start = (bf16[3,32]{1,0:T(4,128)(2,1)S(1)}, bf16[3,32]{1,0:T(4,128)(2,1)}, u32[]{:S(2)}) copy-start(bf16[3,32]{1,0:T(4,128)(2,1)} %param.20) | copy-start | bytes 580
  11.3 12.1 %copy-start.3 = (bf16[9,32,3]{1,2,0:T(4,128)(2,1)S(1)}, bf16[9,32,3]{1,2,0:T(4,128)(2,1)}, u32[]{:S(2)}) copy-start(bf16[9,32,3]{1,2,0:T(4,128)(2,1)} %param.14) | copy-start | bytes 5188
  11.4 6.3 %collective-permute-start = (bf16[4,1,16,1,128]{4,1,3,2,0:T(2,128)(2,1)S(1)}, bf16[4,1,16,1,128]{4,1,3,2,0:T(2,128)(2,1)S(1)}, u32[]{:S(2)}, u32[]{:S(2)}) collective-permute-start(bf16[4,1,16,1,128]{4,1,3,2,0:T(2,128)(2,1)S(1)} %get-tuple-element.281), channel_id=1, source_target_pairs={{0,1},{1,2},{2,3},{3,4},{4,5},{5,6},{6,7},{8,9},{9,10},{10,11},{11... | collective-permute-start | bytes 49160 | tf_op jit(solution)/shard_map/while/body/eval_jaxpr/ppermute | solution.py:18
  15.3 5.8 %collective-permute-start.1 = (bf16[4,1,16,1,128]{4,1,3,2,0:T(2,128)(2,1)S(1)}, bf16[4,1,16,1,128]{4,1,3,2,0:T(2,128)(2,1)S(1)}, u32[]{:S(2)}, u32[]{:S(2)}) collective-permute-start(bf16[4,1,16,1,128]{4,1,3,2,0:T(2,128)(2,1)S(1)} %get-tuple-element.282), channel_id=1, source_target_pairs={{1,0},{2,1},{3,2},{4,3},{5,4},{6,5},{7,6},{9,8},{10,9},{11,10},{12... | collective-permute-start | bytes 49160 | tf_op jit(solution)/shard_map/while/body/eval_jaxpr/ppermute | solution.py:20
  26.8 21.5 %copy-start.4 = (f32[32]{0:T(128)S(1)}, f32[32]{0:T(128)}, u32[]{:S(2)}) copy-start(f32[32]{0:T(128)} %param.16) | copy-start | bytes 388
  26.8 21.5 %copy-start.6 = (f32[32]{0:T(128)S(1)}, f32[32]{0:T(128)}, u32[]{:S(2)}) copy-start(f32[32]{0:T(128)} %param.17) | copy-start | bytes 388
  49.1 19.8 %collective-permute-start.2 = (bf16[4,32,16,1,128]{4,1,3,2,0:T(8,128)(2,1)S(1)}, bf16[4,32,16,1,128]{4,1,3,2,0:T(8,128)(2,1)S(1)}, u32[]{:S(2)}, u32[]{:S(2)}) collective-permute-start(bf16[4,32,16,1,128]{4,1,3,2,0:T(8,128)(2,1)S(1)} %get-tuple-element.273), channel_id=1, source_target_pairs={{0,1},{1,2},{2,3},{3,4},{4,5},{5,6},{6,7},{8,9},{9,10},{10,11},{11... | collective-permute-start | bytes 1572872 | tf_op jit(solution)/shard_map/while/body/eval_jaxpr/ppermute | solution.py:18
  50.7 18.2 %collective-permute-start.3 = (bf16[4,32,16,1,128]{4,1,3,2,0:T(8,128)(2,1)S(1)}, bf16[4,32,16,1,128]{4,1,3,2,0:T(8,128)(2,1)S(1)}, u32[]{:S(2)}, u32[]{:S(2)}) collective-permute-start(bf16[4,32,16,1,128]{4,1,3,2,0:T(8,128)(2,1)S(1)} %get-tuple-element.274), channel_id=1, source_target_pairs={{1,0},{2,1},{3,2},{4,3},{5,4},{6,5},{7,6},{9,8},{10,9},{11,10},{12... | collective-permute-start | bytes 1572872 | tf_op jit(solution)/shard_map/while/body/eval_jaxpr/ppermute | solution.py:20
  73.5 0.9 copy-start.1
  78.8 21.2 %copy-start.5 = (f32[32]{0:T(128)S(1)}, f32[32]{0:T(128)}, u32[]{:S(2)}) copy-start(f32[32]{0:T(128)} %param.18) | copy-start | bytes 388
  78.8 21.2 %copy-start.7 = (f32[32]{0:T(128)S(1)}, f32[32]{0:T(128)}, u32[]{:S(2)}) copy-start(f32[32]{0:T(128)} %param.19) | copy-start | bytes 388
  78.8 21.2 %copy-start.8 = (f32[3]{0:T(128)S(1)}, f32[3]{0:T(128)}, u32[]{:S(2)}) copy-start(f32[3]{0:T(128)} %param.21) | copy-start | bytes 40
  100.0 6.7 %copy-start.2 = (s32[4,2]{0,1:T(2,128)S(1)}, s32[4,2]{0,1:T(2,128)}, u32[]{:S(2)}) copy-start(s32[4,2]{0,1:T(2,128)} %param.13) | copy-start | bytes 100
where the time goes:
time: 119 us
  blocking collectives  51.3 us (43%)
  waiting for transfers between devices  19.9 us (17%)
  matrix products  13 us (11%)
  local copies, waits for them, and re-layouts  9.01 us (8%)
  starting transfers between devices  8.18 us (7%)
  loops' own time  7.72 us (6%)
  other arithmetic  6.63 us (6%)
  between operations  2.93 us (2%)
    psum x2, blocking collectives, normalize(): lax.psum((jnp.sum(values, axis=(2, 3, 4)), jnp.sum(values * values, axis=...  39.5 us
    ppermute x2, waiting for transfers between devices, padded_2(): lax.ppermute(tail, axis, [(i, (i + 1) % count) for i in range(ends)])  16.5 us
    dot_general x18, matrix products, apply_taps(): jnp.einsum('oc,fczyx->fozyx', weights[depth_tap * 3 + row_tap], window, p...  12.1 us
    another operation x1, loops' own time, local(): blended = lax.fori_loop(0, shard_part.shape[0], add_one, empty)  7.72 us
    all_gather x1, blocking collectives, local(): shard_part = lax.all_gather(image, 'patch', axis=0, tiled=True)  6.22 us
    all_gather x1, blocking collectives, local(): shard_part = lax.all_gather(contribs, 'patch', axis=0, tiled=True)  5.6 us
    ppermute x2, starting transfers between devices, padded_2(): lax.ppermute(tail, axis, [(i, (i + 1) % count) for i in range(ends)])  5.41 us
    ppermute x2, waiting for transfers between devices, padded_2(): lax.ppermute(head, axis, [((i + 1) % count, i) for i in range(ends)])  3.37 us
  transfers between devices with their start and end apart: 4, of which 2 were waited for; matrix products, arithmetic and copies ran while one was open for 1% of the time, Pallas kernels for 0%

commit v1 on v0

v1 whole, which is shorter than its diff:
```python
import functools

import jax
import jax.numpy as jnp
from jax import lax
from jax.experimental import pallas as pl
from jax.experimental.pallas import tpu as pltpu
from jax.sharding import PartitionSpec as P

PX = 128
PZ = 16
TAPS = 3
ZG = 4
ZI = ZG + TAPS - 1
F32 = jnp.float32
BF16 = jnp.bfloat16
HI = lax.Precision.HIGHEST
CONTRACT_FIRST = (((0,), (0,)), ((), ()))
CONTRACT_LAST = (((1,), (1,)), ((), ()))
VMEM = pl.BlockSpec(memory_space=pltpu.VMEM)
SMEM = pl.BlockSpec(memory_space=pltpu.SMEM)


def iota(shape, dim):
    return lax.broadcasted_iota(jnp.int32, shape, dim)


def repeat_matrix(channels, lanes, dtype):
    shape = (channels, lanes)
    return (iota(shape, 0) == iota(shape, 1) % channels).astype(dtype)


def cut_kernel(offsets_ref, image_ref, out_ref, rows_ref):
    slab_rows, band_rows, width = image_ref.shape
    for z in range(slab_rows):
        rows_ref[z * band_rows : (z + 1) * band_rows, :] = image_ref[z].astype(F32)
    rows = rows_ref[...]
    for item in range(out_ref.shape[0]):
        shift = lax.rem(width - offsets_ref[item, 1], width)
        window = pltpu.roll(rows, shift, 1)[:, :PX].astype(BF16)
        for space in range(out_ref.shape[1]):
            out_ref[item, space] = window


def tap_rows(offsets_ref, gathered_ref, cells_ref, taps_ref, slab_rows, band_rows, spaces):
    block = slab_rows * band_rows
    devices = gathered_ref.shape[0]
    for device in range(devices):
        cells_ref[device * block : (device + 1) * block, :] = gathered_ref[device].astype(F32)
    taps_ref[...] = jnp.zeros_like(taps_ref)
    rows = band_rows * spaces
    for z in range(PZ):
        taps_ref[z, pl.ds(32 + 15, rows, stride=16), :] = jnp.ones((rows, PX), F32)
    item = lax.axis_index("patch")
    start_z = offsets_ref[item, 0]
    lane = iota((spaces, PX), 1)
    for z in range(PZ):
        deep = start_z + z
        slab = lax.div(deep, slab_rows)
        base = slab * (spaces * block) + (deep - slab * slab_rows) * band_rows
        for y in range(band_rows):
            line = cells_ref[pl.ds(base + y, spaces, stride=block), :]
            before = jnp.where(lane == 0, 0.0, pltpu.roll(line, 1, 1))
            after = jnp.where(lane == PX - 1, 0.0, pltpu.roll(line, PX - 1, 1))
            for a in range(TAPS):
                at = z + 1 - a
                if 0 <= at < PZ:
                    for c, value in enumerate((before, line, after)):
                        first = 32 + 16 * y + a * TAPS + c
                        taps_ref[at, pl.ds(first, spaces, stride=16 * band_rows), :] = value


def first_moments(taps_ref, gram_ref, weights, rows):
    cells = [taps_ref[z, 32 : 32 + 16 * rows, :].astype(BF16) for z in range(PZ)]
    cells = jnp.concatenate(cells, axis=1)
    gram_ref[...] = lax.dot_general(cells, cells, CONTRACT_LAST, preferred_element_type=F32)

    def block(y, delta):
        lane = 16 * (y + delta)
        tile = lane // 128 * 128
        value = gram_ref[16 * y : 16 * y + 16, tile : tile + 128]
        return pltpu.roll(value, (tile + 128 - lane) % 128, 1) if lane != tile else value

    def total(values):
        values = list(values)
        while len(values) > 1:
            values = [
                values[i] + values[i + 1] if i + 1 < len(values) else values[i]
                for i in range(0, len(values), 2)
            ]
        return jnp.where(iota((16, 128), 1) < 16, values[0], 0.0)

    head, tail = total([block(0, 0)]), total([block(rows - 1, 0)])
    near = total([block(y, 0) for y in range(rows)])
    next1 = 2.0 * total([block(y, 1) for y in range(rows - 1)])
    next2 = 2.0 * total([block(y, 2) for y in range(rows - 2)])
    diag = (near - tail, near, near - head)
    move = lambda value, k: pltpu.roll(value, 16 * k, 1) if k else value
    form = jnp.concatenate(
        [
            diag[0] + move(next1, 1) + move(next2, 2),
            move(diag[1], 1) + move(next1, 2),
            move(diag[2], 2),
            diag[0] + move(diag[1], 1) + move(diag[2], 2),
        ],
        axis=0,
    )[:, :48]
    product = jnp.dot(form, weights, precision=HI, preferred_element_type=F32)
    squares = jnp.sum(product[:48] * weights, axis=0, keepdims=True)
    return product[63:64], squares


def main_kernel(
    spaces,
    slab_rows,
    band_rows,
    offsets_ref,
    gathered_ref,
    w1_ref,
    w2_ref,
    gain_ref,
    bias_ref,
    conv_ref,
    stats_ref,
    cells_ref,
    taps_ref,
    gram_ref,
    wide_ref,
    w2t_ref,
    sums_ref,
):
    rows = band_rows * spaces
    channels = gain_ref.shape[1]
    hidden_rows = band_rows + TAPS - 1
    in_rows = hidden_rows + TAPS - 1
    width = 4 * hidden_rows * channels
    band = lax.axis_index("space")
    tap_rows(offsets_ref, gathered_ref, cells_ref, taps_ref, slab_rows, band_rows, spaces)

    w1 = w1_ref[...].astype(F32)
    first, second = first_moments(taps_ref, gram_ref, w1.reshape(TAPS * 16, width), rows)
    count = float(PZ * rows * PX)
    repeat = repeat_matrix(channels, width, F32)
    params = jnp.concatenate([gain_ref[...], bias_ref[...], jnp.zeros((6, channels), F32)], axis=0)
    params = jnp.dot(params, repeat, precision=HI, preferred_element_type=F32)
    mean = first / count
    variance = second / count - mean * mean
    lane_row = iota((1, width), 1) // channels % hidden_rows
    y = band * band_rows - 1 + lane_row
    inside = (y >= 0) & (y < rows)
    scale = lax.rsqrt(variance + 1e-05) * params[0:1]
    shift = jnp.where(inside, params[1:2] - mean * scale, 0.0)
    scale = jnp.where(inside, scale, 0.0)

    lane_row = iota((16, width), 1) // channels % hidden_rows
    pieces = []
    for yi in range(in_rows):
        piece = jnp.zeros((16, width), F32)
        for b in range(TAPS):
            if 0 <= yi - b < hidden_rows:
                piece = jnp.where(lane_row == yi - b, w1[b], piece)
        pieces.append(piece)
    w1_full = jnp.concatenate(pieces, axis=0).astype(BF16)

    out_lanes = ZG * band_rows * channels
    spread = repeat_matrix(channels, out_lanes, BF16)
    taps2 = [
        lax.dot_general(w2_ref[t], spread, CONTRACT_FIRST, preferred_element_type=F32)
        for t in range(TAPS * TAPS)
    ]
    group = iota((TAPS * channels, out_lanes), 1) // channels
    for zi in range(ZI):
        for yi in range(hidden_rows):
            piece = jnp.zeros((TAPS * channels, out_lanes), F32)
            for zo in range(ZG):
                for yo in range(band_rows):
                    a, b = zi - zo, yi - yo
                    if 0 <= a < TAPS and 0 <= b < TAPS:
                        piece = jnp.where(group == zo * band_rows + yo, taps2[a * TAPS + b], piece)
            piece = piece.astype(BF16)
            at = (zi * hidden_rows + yi) * channels
            for c in range(TAPS):
                w2t_ref[c, at : at + channels, :] = piece[c * channels : (c + 1) * channels]

    step = hidden_rows * channels
    groups = PZ // ZG
    empty = jnp.zeros((PX, step), BF16)
    for f in range(4):
        for g, j in ((0, 0), (groups - 1, ZI - 1)):
            at = (ZI - 1 - j if f % 2 else j) * step
            wide_ref[f, g * PX : (g + 1) * PX, at : at + step] = empty
    start = pl.multiple_of(band * (16 * band_rows), 16)
    for z in range(PZ):
        cells = taps_ref[z, pl.ds(start, in_rows * 16), :].astype(BF16)
        value = lax.dot_general(cells, w1_full, CONTRACT_FIRST, preferred_element_type=F32)
        value = value * scale + shift
        value = jnp.maximum(value, 0.01 * value).astype(BF16)
        for g in range(groups):
            j = z + 1 - ZG * g
            if 0 <= j < ZI:
                for f in range(4):
                    at = (ZI - 1 - j if f % 2 else j) * step
                    wide_ref[f, g * PX : (g + 1) * PX, at : at + step] = value[
                        :, f * step : (f + 1) * step
                    ]

    x = iota((groups * PX, out_lanes), 0) % PX
    for f in range(4):
        cells = wide_ref[f]
        parts = [
            jnp.dot(cells, w2t_ref[c], preferred_element_type=F32) for c in range(TAPS)
        ]
        before, after = (parts[2], parts[0]) if f >= 2 else (parts[0], parts[2])
        value = (
            parts[1]
            + jnp.where(x == 0, 0.0, pltpu.roll(before, 1, 0))
            + jnp.where(x == PX - 1, 0.0, pltpu.roll(after, groups * PX - 1, 0))
        )
        conv_ref[f] = value
        sums_ref[2 * f : 2 * f + 1, :] = jnp.sum(value, axis=0, keepdims=True)
        sums_ref[2 * f + 1 : 2 * f + 2, :] = jnp.sum(value * value, axis=0, keepdims=True)
    sums = sums_ref[...]
    for space in range(spaces):
        stats_ref[space] = sums


def head_kernel(
    count, band_rows, conv_ref, stats_ref, gain_ref, bias_ref, head_ref, head_bias_ref, out_ref
):
    channels = gain_ref.shape[1]
    lanes = conv_ref.shape[2]
    classes = head_ref.shape[0]
    sums = stats_ref[0]
    for space in range(1, stats_ref.shape[0]):
        sums = sums + stats_ref[space]
    reach = lanes // 2
    while reach >= channels:
        sums = sums + pltpu.roll(sums, reach, 1)
        reach //= 2
    repeat = repeat_matrix(channels, lanes, F32)
    params = jnp.concatenate([gain_ref[...], bias_ref[...], jnp.zeros((6, channels), F32)], axis=0)
    params = jnp.dot(params, repeat, precision=HI, preferred_element_type=F32)
    head = jnp.concatenate([head_ref[...].astype(F32), jnp.zeros((8 - classes, channels), F32)], 0)
    head = jnp.dot(head, repeat, precision=HI, preferred_element_type=F32)
    per_z = classes * band_rows
    shape = (ZG * per_z, lanes)
    row_z, row_k, row_y = (
        iota(shape, 0) // per_z,
        iota(shape, 0) // band_rows % classes,
        iota(shape, 0) % band_rows,
    )
    full = jnp.zeros(shape, F32)
    for k in range(classes):
        full = jnp.where(row_k == k, head[k : k + 1], full)
    lane_z = iota(shape, 1) // (band_rows * channels)
    lane_y = iota(shape, 1) // channels % band_rows
    heads = [
        jnp.where((lane_z == z) & (lane_y == row_y), full, 0.0).astype(BF16)
        for z in (row_z, ZG - 1 - row_z)
    ]
    shape = (ZG * per_z, PX)
    row_k = iota(shape, 0) // band_rows % classes
    bias = jnp.zeros(shape, F32)
    for k in range(classes):
        bias = jnp.where(row_k == k, head_bias_ref[k], bias)
    groups = conv_ref.shape[1] // PX
    totals = [None] * groups
    for f in range(4):
        mean = sums[2 * f : 2 * f + 1] / count
        variance = sums[2 * f + 1 : 2 * f + 2] / count - mean * mean
        scale = lax.rsqrt(variance + 1e-05) * params[0:1]
        shift = params[1:2] - mean * scale
        for g in range(groups):
            value = conv_ref[f, g * PX : (g + 1) * PX, :] * scale + shift
            value = jnp.maximum(value, 0.01 * value).astype(BF16)
            logits = lax.dot_general(
                heads[f % 2], value, CONTRACT_LAST, preferred_element_type=F32
            )
            totals[g] = logits if totals[g] is None else totals[g] + logits
    for g in range(groups):
        at = g * ZG * per_z
        out_ref[at : at + ZG * per_z, :] = totals[g] * 0.25 + bias


def place_kernel(spaces, offsets_ref, parts_ref, out_ref, pad_ref):
    slab_rows, classes, band_rows, width = out_ref.shape
    patch_rows = band_rows * spaces
    per_z = classes * band_rows
    count = slab_rows * per_z
    slab = lax.axis_index("patch") * slab_rows
    band = lax.axis_index("space") * band_rows
    shape = (count, width)
    z = slab + iota(shape, 0) // per_z
    x = iota(shape, 1)
    y = (band + iota(shape, 0) % band_rows).astype(F32) - (patch_rows - 1) / 2.0
    across = y * y * (1.0 / (2.0 * (patch_rows / 8.0) ** 2))
    blended = jnp.zeros(shape, F32)
    coverage = jnp.zeros(shape, F32)
    for item in range(parts_ref.shape[0]):
        pad_ref[item, count : count + PZ * per_z, :] = parts_ref[item].astype(F32)
        start_z, start_x = offsets_ref[item, 0], offsets_ref[item, 1]
        first = jnp.clip(slab - start_z, -slab_rows, PZ) * per_z + count
        part = pad_ref[item, pl.ds(first, count), :]
        part = jnp.concatenate([part, jnp.zeros((count, width - PX), F32)], axis=1)
        part = pltpu.roll(part, start_x, 1)
        rel_z, rel_x = z - start_z, x - start_x
        inside = (rel_z >= 0) & (rel_z < PZ) & (rel_x >= 0) & (rel_x < PX)
        far_z = rel_z.astype(F32) - (PZ - 1) / 2.0
        far_x = rel_x.astype(F32) - (PX - 1) / 2.0
        power = (
            across
            + far_z * far_z * (1.0 / (2.0 * (PZ / 8.0) ** 2))
            + far_x * far_x * (1.0 / (2.0 * (PX / 8.0) ** 2))
        )
        weight = jnp.where(inside, jnp.exp(-power), 0.0)
        blended = blended + jnp.where(inside, part * weight, 0.0)
        coverage = coverage + weight
    value = blended / jnp.maximum(coverage, 0.1)
    for z in range(slab_rows):
        for k in range(classes):
            at = z * per_z + k * band_rows
            out_ref[z, k] = value[at : at + band_rows]


def mirrored(weights, channels):
    taps = weights.reshape(TAPS, TAPS, channels, TAPS)
    sets = jnp.stack([taps, taps[::-1], taps[..., ::-1], taps[::-1, ..., ::-1]])
    return sets.transpose(2, 1, 4, 0, 3).reshape(TAPS, TAPS * TAPS, 4, 1, channels)


def local(
    image,
    offsets,
    conv1_weight,
    conv2_weight,
    norm1_gain,
    norm1_bias,
    norm2_gain,
    norm2_bias,
    head_weight,
    head_bias,
):
    groups = lax.axis_size("patch")
    spaces = lax.axis_size("space")
    slab_rows, band_rows, width = image.shape
    channels = norm1_gain.shape[0]
    classes = head_weight.shape[0]
    rows = band_rows * spaces
    hidden_rows = band_rows + TAPS - 1
    block = slab_rows * band_rows

    windows = pl.pallas_call(
        cut_kernel,
        out_shape=jax.ShapeDtypeStruct((groups, spaces, block, PX), BF16),
        in_specs=[SMEM, VMEM],
        out_specs=VMEM,
        scratch_shapes=[pltpu.VMEM((block, width), F32)],
        name="cut",
    )(offsets, image)
    windows = windows.reshape(groups * spaces, block, PX)
    gathered = lax.all_to_all(windows, ("patch", "space"), 0, 0, tiled=True)

    w1 = mirrored(conv1_weight, channels)
    w1 = jnp.pad(w1, ((0, 0), (0, 16 - TAPS * TAPS), (0, 0), (0, 0), (0, 0)))
    w1 = jnp.broadcast_to(w1, (TAPS, 16, 4, hidden_rows, channels))
    w1 = w1.reshape(TAPS, 16, 4 * hidden_rows * channels)
    out_lanes = ZG * band_rows * channels
    cells = PZ // ZG * PX
    conv, stats = pl.pallas_call(
        functools.partial(main_kernel, spaces, slab_rows, band_rows),
        out_shape=(
            jax.ShapeDtypeStruct((4, cells, out_lanes), F32),
            jax.ShapeDtypeStruct((spaces, 8, out_lanes), F32),
        ),
        in_specs=[SMEM] + [VMEM] * 5,
        out_specs=(VMEM, VMEM),
        scratch_shapes=[
            pltpu.VMEM((groups * spaces * block, PX), F32),
            pltpu.VMEM((PZ, (rows + 4) * 16, PX), F32),
            pltpu.VMEM((rows * 16, rows * 16), F32),
            pltpu.VMEM((4, cells, ZI * hidden_rows * channels), BF16),
            pltpu.VMEM((TAPS, ZI * hidden_rows * channels, out_lanes), BF16),
            pltpu.VMEM((8, out_lanes), F32),
        ],
        name="main",
    )(
        offsets,
        gathered,
        w1,
        conv2_weight,
        norm1_gain.reshape(1, channels),
        norm1_bias.reshape(1, channels),
    )
    stats = lax.all_to_all(stats, "space", 0, 0, tiled=True)
    averaged = pl.pallas_call(
        functools.partial(head_kernel, float(PZ * rows * PX), band_rows),
        out_shape=jax.ShapeDtypeStruct((PZ * classes * band_rows, PX), F32),
        in_specs=[VMEM] * 5 + [SMEM],
        out_specs=VMEM,
        name="head",
    )(
        conv,
        stats,
        norm2_gain.reshape(1, channels),
        norm2_bias.reshape(1, channels),
        head_weight,
        head_bias,
    )
    parts = lax.all_gather(averaged, "patch", axis=0, tiled=False)
    return pl.pallas_call(
        functools.partial(place_kernel, spaces),
        out_shape=jax.ShapeDtypeStruct((slab_rows, classes, band_rows, width), F32),
        in_specs=[SMEM, VMEM],
        out_specs=VMEM,
        scratch_shapes=[
            pltpu.VMEM((groups, (2 * slab_rows + PZ) * classes * band_rows, PX), F32)
        ],
        name="place",
    )(offsets, parts)


def solution(mesh):
    return jax.shard_map(
        local,
        mesh=mesh,
        in_specs=(P("patch", "space", None), P(), P(), P(), P(), P(), P(), P(), P(), P()),
        out_specs=P("patch", None, "space", None),
        check_vma=False,
    )
```

time: 119 us -> 49.6 us (0.42)
  blocking collectives: 51.3 us -> 17.4 us
  waiting for transfers between devices: 19.9 us -> 3.96 us
  Pallas kernels: 0 us -> 14.3 us
  matrix products: 13 us -> 0 us
  loops' own time: 7.72 us -> 0 us
  other arithmetic: 6.63 us -> 0.74 us
  local copies, waits for them, and re-layouts: 9.01 us -> 5.07 us
  between operations: 2.93 us -> 0.04 us
    psum x2 -> x0, blocking collectives: 39.5 us -> none  [normalize(): lax.psum((jnp.sum(values, axis=(2, 3, 4)), jnp.sum(values * values, axis=...]
    ppermute x4 -> x0, waiting for transfers between devices: 19.9 us -> none  [the longest x2 16.5 us: padded_2(): lax.ppermute(tail, axis, [(i, (i + 1) % count) for i in range(ends)])]
    pallas_call x0 -> x4, Pallas kernels: none -> 14.3 us  [the longest x1 8.14 us: local(): pl.pallas_call(functools.partial(main_kernel, spaces, slab_rows, band_row...]
    dot_general x20 -> x0, matrix products: 13 us -> none  [the longest x18 12.1 us: apply_taps(): jnp.einsum('oc,fczyx->fozyx', weights[depth_tap * 3 + row_tap], window, p...]
    all_to_all x0 -> x1, blocking collectives: none -> 10.9 us  [local(): stats = lax.all_to_all(stats, 'space', 0, 0, tiled=True)]
    ppermute x4 -> x0, starting transfers between devices: 8.18 us -> none  [the longest x2 5.41 us: padded_2(): lax.ppermute(tail, axis, [(i, (i + 1) % count) for i in range(ends)])]
    another operation x1 -> x0, loops' own time: 7.72 us -> none  [local(): blended = lax.fori_loop(0, shard_part.shape[0], add_one, empty)]
    all_to_all x0 -> x1, starting transfers between devices: none -> 7.33 us  [local(): gathered = lax.all_to_all(windows, ('patch', 'space'), 0, 0, tiled=True)]
  transfers between devices with their start and end apart: 4 -> 1, of which waited for: 2 -> 1; matrix products, arithmetic and copies ran while one was open for 1% -> 8% of each run, Pallas kernels for 0% -> 0%
where the time goes in v1:
time: 49.6 us; the launch traced here: 48.9 us
  blocking collectives  17.4 us (35%)
  Pallas kernels  14.3 us (29%)
  starting transfers between devices  7.33 us (15%)
  local copies, waits for them, and re-layouts  5.07 us (10%)
  waiting for transfers between devices  3.96 us (8%)
  other arithmetic  0.74 us (1%)
    all_to_all x1, blocking collectives, local(): stats = lax.all_to_all(stats, 'space', 0, 0, tiled=True)  10.9 us
    pallas_call x1, Pallas kernels, local(): pl.pallas_call(functools.partial(main_kernel, spaces, slab_rows, band_row...  8.14 us
    all_to_all x1, starting transfers between devices, local(): gathered = lax.all_to_all(windows, ('patch', 'space'), 0, 0, tiled=True)  7.33 us
    all_gather x1, blocking collectives, local(): parts = lax.all_gather(averaged, 'patch', axis=0, tiled=False)  6.59 us
    all_to_all x1, waiting for transfers between devices, local(): gathered = lax.all_to_all(windows, ('patch', 'space'), 0, 0, tiled=True)  3.96 us
    pallas_call x1, Pallas kernels, local(): pl.pallas_call(functools.partial(head_kernel, float(PZ * rows * PX), band...  2.96 us
    unnamed x3, local copies, waits for them, and re-layouts  2 us
    pallas_call x1, Pallas kernels, local(): pl.pallas_call(functools.partial(place_kernel, spaces), out_shape=jax.Sha...  1.73 us
  transfers between devices with their start and end apart: 1, of which 1 were waited for; matrix products, arithmetic and copies ran while one was open for 8% of the time, Pallas kernels for 0%

profile of v1, /device:TPU:0, one launch (start us, length us, event | category | flops | bytes accessed | tf_op | source)
XLA Modules:
  0.0 48.9 jit_solution(8035537948109831909)
XLA Ops:
  0.0 1.4 %copy.24.offsets_ref = s32[4,2]{1,0:T(4,128)} copy(s32[4,2]{0,1:T(2,128)} %param.11) | data formatting | bytes 64 | tf_op args[1]
  1.4 1.4 %cut.1 = bf16[4,8,16,128]{3,2,1,0:T(8,128)(2,1)} custom-call(s32[4,2]{1,0:T(4,128)} %copy.24.offsets_ref, bf16[8,2,256]{2,1,0:T(2,128)(2,1)} %image_ref.1), custom_call_target="tpu_custom_call" | custom-call | tf_op jit(solution)/shard_map/cut/pallas_call | solution.py:352
  2.8 7.3 %all-to-all-start = ((bf16[32,16,128]{2,1,0:T(8,128)(2,1)}), bf16[32,16,128]{2,1,0:T(8,128)(2,1)S(1)}, u32[]{:S(2)}, u32[]{:S(2)}) async-start(bf16[32,16,128]{2,1,0:T(8,128)(2,1)} %bitcast.18), calls=%async_computation | async-start | bytes 262144 | tf_op jit(solution)/shard_map/all_to_all | solution.py:361
  10.1 0.7 %reverse_bitcast_fusion = bf16[1,3,3,32,3]{3,4,2,1,0:T(4,128)(2,1)S(1)} fusion(bf16[3,3,32,3]{2,3,1,0:T(4,128)(2,1)} %bitcast.19), kind=kLoop, calls=%fused_computation.2 | loop fusion | bytes 3456 | tf_op jit(solution)/shard_map/stack | solution.py:327
  10.8 0.7 %rev.11 = bf16[3,3,32,3]{2,3,1,0:T(4,128)(2,1)S(1)} reverse(bf16[3,3,32,3]{2,3,1,0:T(4,128)(2,1)} %bitcast.20), dimensions={0,3} | reverse | bytes 3456 | tf_op jit(solution)/shard_map/rev | solution.py:327
  11.6 0.7 %rev.10 = bf16[3,3,32,3]{2,3,1,0:T(4,128)(2,1)S(1)} reverse(bf16[3,3,32,3]{2,3,1,0:T(4,128)(2,1)} %bitcast.21), dimensions={3} | reverse | bytes 3456 | tf_op jit(solution)/shard_map/rev | solution.py:327
  12.3 0.7 %maximum_bitcast_fusion = bf16[3,3,3,4,32]{4,2,0,1,3:T(4,128)(2,1)S(1)} fusion(bf16[1,3,3,32,3]{3,4,2,1,0:T(4,128)(2,1)S(1)} %bitcast.24, bf16[1,3,3,32,3]{3,4,2,1,0:T(4,128)(2,1)S(1)} %bitcast.25, bf16[1,3,3,32,3]{3,4,2,1,0:T(4,128)(2,1)S(1)} %reverse_bitcast_fusion, bf16[1,3,3,32,3]{3,4,2,1,0:T(4,128)(2,1)} %bitcast.22), kind=kLoop, calls=%fused_computation.1 | loop fusion | flops 10368 | bytes 13824 | tf_op jit(solution)/shard_map/transpose | solution.py:328
  13.1 0.1 broadcast_in_dim.8
  13.2 0.8 %reshape.27.w1_ref = bf16[3,16,512]{2,1,0:T(8,128)(2,1)} reshape(bf16[3,16,4,4,32]{4,3,2,1,0:T(4,128)(2,1)S(1)} %broadcast_in_dim.8) | data formatting | bytes 98304 | tf_op jit(solution)/shard_map/reshape | solution.py:366
  14.0 4.0 %all-to-all-done.gathered_ref = bf16[32,16,128]{2,1,0:T(8,128)(2,1)S(1)} async-done(((bf16[32,16,128]{2,1,0:T(8,128)(2,1)}), bf16[32,16,128]{2,1,0:T(8,128)(2,1)S(1)}, u32[]{:S(2)}, u32[]{:S(2)}) %all-to-all-start) | async-done | bytes 131104 | tf_op jit(solution)/shard_map/all_to_all | solution.py:361
  17.9 0.0 copy-start
  17.9 0.6 %copy-done = bf16[32,16,128]{2,1,0:T(8,128)(2,1)} copy-done((bf16[32,16,128]{2,1,0:T(8,128)(2,1)}, bf16[32,16,128]{2,1,0:T(8,128)(2,1)S(1)}, u32[]{:S(2)}) %copy-start) | copy-done | bytes 131096
  18.6 8.1 %main.1 = (f32[4,512,256]{2,1,0:T(8,128)}, f32[8,8,256]{2,1,0:T(8,128)}) custom-call(s32[4,2]{1,0:T(4,128)} %copy.24.offsets_ref, bf16[32,16,128]{2,1,0:T(8,128)(2,1)} %copy-done, bf16[3,16,512]{2,1,0:T(8,128)(2,1)} %reshape.27.w1_ref, bf16[9,32,96]{2,1,0:T(8,128)(2,1)} %w2_ref.1, f32[1,32]{1,0:T(1,128)} %bitcast.26, f32[1,32]{1,0:T(1,128)} %bitcast.27), custom_call_target="tpu_custom_call" | custom-call | tf_op jit(solution)/shard_map/main/pallas_call | solution.py:369
  26.7 10.9 %all_to_all.10.stats_ref = f32[8,8,256]{2,1,0:T(8,128)} all-to-all(f32[8,8,256]{2,1,0:T(8,128)} %get-tuple-element.8), channel_id=1, replica_groups=mesh['patch'=4,'space'=8] {'space'}, dimensions={0} | all-to-all | bytes 131072 | tf_op jit(solution)/shard_map/all_to_all | solution.py:394
  37.6 3.0 %head.1 = f32[96,128]{1,0:T(8,128)} custom-call(f32[4,512,256]{2,1,0:T(8,128)} %get-tuple-element.7.conv_ref, f32[8,8,256]{2,1,0:T(8,128)} %all_to_all.10.stats_ref, f32[1,32]{1,0:T(1,128)} %bitcast.28, f32[1,32]{1,0:T(1,128)} %bitcast.29, bf16[3,32]{1,0:T(4,128)(2,1)} %head_ref.1, f32[3]{0:T(128)} %head_bias_ref.1), custom_call_target="tpu_custom_call" | custom-call | tf_op jit(solution)/shard_map/head/pallas_call | solution.py:395
  40.6 6.6 %all-gather = f32[384,128]{1,0:T(8,128)} all-gather(f32[96,128]{1,0:T(8,128)} %head.1), channel_id=2, replica_groups=mesh['patch'=4,'space'=8] {'patch'}, dimensions={0}, use_global_device_ids=true | all-gather | bytes 245760 | tf_op jit(solution)/shard_map/all_gather | solution.py:409
  47.1 1.7 %place.1 = f32[8,3,2,256]{3,2,1,0:T(2,128)} custom-call(s32[4,2]{1,0:T(4,128)} %copy.24.offsets_ref, f32[4,96,128]{2,1,0:T(8,128)} %bitcast.17), custom_call_target="tpu_custom_call" | custom-call | tf_op jit(solution)/shard_map/place/pallas_call | solution.py:410
  (2 shorter events, 0.0 us)
Async XLA Ops:
  2.8 15.1 %all-to-all-start = ((bf16[32,16,128]{2,1,0:T(8,128)(2,1)}), bf16[32,16,128]{2,1,0:T(8,128)(2,1)S(1)}, u32[]{:S(2)}, u32[]{:S(2)}) async-start(bf16[32,16,128]{2,1,0:T(8,128)(2,1)} %bitcast.18), calls=%async_computation | async-start | bytes 262144 | tf_op jit(solution)/shard_map/all_to_all | solution.py:361
  17.9 0.6 %copy-start = (bf16[32,16,128]{2,1,0:T(8,128)(2,1)}, bf16[32,16,128]{2,1,0:T(8,128)(2,1)S(1)}, u32[]{:S(2)}) copy-start(bf16[32,16,128]{2,1,0:T(8,128)(2,1)S(1)} %all-to-all-done.gathered_ref) | copy-start | bytes 393220

commit v2 on v1

--- a/solution.py
+++ b/solution.py
@@ -1,4 +1,5 @@
 import functools
+import math
 
 import jax
 import jax.numpy as jnp
@@ -36,7 +37,7 @@
         rows_ref[z * band_rows : (z + 1) * band_rows, :] = image_ref[z].astype(F32)
     rows = rows_ref[...]
     for item in range(out_ref.shape[0]):
-        shift = lax.rem(width - offsets_ref[item, 1], width)
+        shift = lax.rem(width - offsets_ref[1, item], width)
         window = pltpu.roll(rows, shift, 1)[:, :PX].astype(BF16)
         for space in range(out_ref.shape[1]):
             out_ref[item, space] = window
@@ -52,7 +53,7 @@
     for z in range(PZ):
         taps_ref[z, pl.ds(32 + 15, rows, stride=16), :] = jnp.ones((rows, PX), F32)
     item = lax.axis_index("patch")
-    start_z = offsets_ref[item, 0]
+    start_z = offsets_ref[0, item]
     lane = iota((spaces, PX), 1)
     for z in range(PZ):
         deep = start_z + z
@@ -110,79 +111,151 @@
     return product[63:64], squares
 
 
+def prep_kernel(
+    band_rows,
+    w1_ref,
+    w2_ref,
+    gain1_ref,
+    bias1_ref,
+    gain2_ref,
+    bias2_ref,
+    head_ref,
+    head_bias_ref,
+    flat_ref,
+    full_ref,
+    wide_ref,
+    params1_ref,
+    params2_ref,
+    heads_ref,
+    bias_ref,
+):
+    channels = gain1_ref.shape[1]
+    classes = head_ref.shape[0]
+    hidden_rows = band_rows + TAPS - 1
+    in_rows = hidden_rows + TAPS - 1
+
+    width = flat_ref.shape[1]
+    repeat = repeat_matrix(channels, width, BF16)
+    taps = [
+        jnp.dot(w1_ref[t], repeat, preferred_element_type=F32) for t in range(TAPS * TAPS)
+    ]
+    mirror = iota((1, width), 1) // (hidden_rows * channels)
+    flat_ref[...] = jnp.zeros_like(flat_ref)
+    for b in range(TAPS):
+        for a in range(TAPS):
+            one, two = taps[a * TAPS + b], taps[(TAPS - 1 - a) * TAPS + b]
+            for c in range(TAPS):
+                d = TAPS - 1 - c
+                row = jnp.where(
+                    mirror < 2,
+                    jnp.where(mirror == 0, one[c : c + 1], two[c : c + 1]),
+                    jnp.where(mirror == 2, one[d : d + 1], two[d : d + 1]),
+                )
+                at = 16 * b + a * TAPS + c
+                flat_ref[at : at + 1, :] = row
+    lane_row = iota((16, width), 1) // channels % hidden_rows
+    for yi in range(in_rows):
+        piece = jnp.zeros((16, width), F32)
+        for b in range(TAPS):
+            if 0 <= yi - b < hidden_rows:
+                piece = jnp.where(lane_row == yi - b, flat_ref[16 * b : 16 * b + 16, :], piece)
+        full_ref[16 * yi : 16 * yi + 16, :] = piece.astype(BF16)
+
+    lanes = ZG * band_rows * channels
+    spread = repeat_matrix(channels, lanes, BF16)
+    taps = [
+        lax.dot_general(w2_ref[t], spread, CONTRACT_FIRST, preferred_element_type=F32)
+        for t in range(TAPS * TAPS)
+    ]
+    group = iota((TAPS * channels, lanes), 1) // channels
+    for zi in range(ZI):
+        for yi in range(hidden_rows):
+            piece = jnp.zeros((TAPS * channels, lanes), F32)
+            for zo in range(ZG):
+                for yo in range(band_rows):
+                    a, b = zi - zo, yi - yo
+                    if 0 <= a < TAPS and 0 <= b < TAPS:
+                        piece = jnp.where(group == zo * band_rows + yo, taps[a * TAPS + b], piece)
+            piece = piece.astype(BF16)
+            at = (zi * hidden_rows + yi) * channels
+            for c in range(TAPS):
+                wide_ref[c, at : at + channels, :] = piece[c * channels : (c + 1) * channels]
+
+    rest = jnp.zeros((8 - classes - 4, channels), F32)
+    rows = jnp.concatenate(
+        [
+            gain1_ref[...],
+            bias1_ref[...],
+            gain2_ref[...],
+            bias2_ref[...],
+            head_ref[...].astype(F32),
+            rest,
+        ],
+        axis=0,
+    )
+    spread = repeat_matrix(channels, width, F32)
+    rows = jnp.dot(rows, spread, precision=HI, preferred_element_type=F32)
+    params1_ref[...] = rows
+    params2_ref[...] = jnp.concatenate([rows[2:4, :lanes], rows[:6, :lanes]], axis=0)
+
+    per_z = classes * band_rows
+    shape = (ZG * per_z, lanes)
+    row_z = iota(shape, 0) // per_z
+    row_k = iota(shape, 0) // band_rows % classes
+    row_y = iota(shape, 0) % band_rows
+    full = jnp.zeros(shape, F32)
+    for k in range(classes):
+        full = jnp.where(row_k == k, rows[4 + k : 5 + k, :lanes], full)
+    lane_z = iota(shape, 1) // (band_rows * channels)
+    lane_y = iota(shape, 1) // channels % band_rows
+    for f, z in enumerate((row_z, ZG - 1 - row_z)):
+        heads_ref[f] = jnp.where((lane_z == z) & (lane_y == row_y), full, 0.0).astype(BF16)
+    row_k = iota(bias_ref.shape, 0) // band_rows % classes
+    bias = jnp.zeros(bias_ref.shape, F32)
+    for k in range(classes):
+        bias = jnp.where(row_k == k, head_bias_ref[k], bias)
+    bias_ref[...] = bias
+
+
 def main_kernel(
     spaces,
     slab_rows,
     band_rows,
     offsets_ref,
     gathered_ref,
-    w1_ref,
-    w2_ref,
-    gain_ref,
-    bias_ref,
+    flat_ref,
+    full_ref,
+    w2t_ref,
+    params_ref,
     conv_ref,
     stats_ref,
     cells_ref,
     taps_ref,
     gram_ref,
     wide_ref,
-    w2t_ref,
     sums_ref,
 ):
     rows = band_rows * spaces
-    channels = gain_ref.shape[1]
     hidden_rows = band_rows + TAPS - 1
     in_rows = hidden_rows + TAPS - 1
-    width = 4 * hidden_rows * channels
+    width = flat_ref.shape[1]
+    step = width // 4
+    channels = step // hidden_rows
     band = lax.axis_index("space")
     tap_rows(offsets_ref, gathered_ref, cells_ref, taps_ref, slab_rows, band_rows, spaces)
 
-    w1 = w1_ref[...].astype(F32)
-    first, second = first_moments(taps_ref, gram_ref, w1.reshape(TAPS * 16, width), rows)
+    first, second = first_moments(taps_ref, gram_ref, flat_ref[...], rows)
     count = float(PZ * rows * PX)
-    repeat = repeat_matrix(channels, width, F32)
-    params = jnp.concatenate([gain_ref[...], bias_ref[...], jnp.zeros((6, channels), F32)], axis=0)
-    params = jnp.dot(params, repeat, precision=HI, preferred_element_type=F32)
     mean = first / count
     variance = second / count - mean * mean
     lane_row = iota((1, width), 1) // channels % hidden_rows
     y = band * band_rows - 1 + lane_row
     inside = (y >= 0) & (y < rows)
-    scale = lax.rsqrt(variance + 1e-05) * params[0:1]
-    shift = jnp.where(inside, params[1:2] - mean * scale, 0.0)
+    scale = lax.rsqrt(variance + 1e-05) * params_ref[0:1]
+    shift = jnp.where(inside, params_ref[1:2] - mean * scale, 0.0)
     scale = jnp.where(inside, scale, 0.0)
 
-    lane_row = iota((16, width), 1) // channels % hidden_rows
-    pieces = []
-    for yi in range(in_rows):
-        piece = jnp.zeros((16, width), F32)
-        for b in range(TAPS):
-            if 0 <= yi - b < hidden_rows:
-                piece = jnp.where(lane_row == yi - b, w1[b], piece)
-        pieces.append(piece)
-    w1_full = jnp.concatenate(pieces, axis=0).astype(BF16)
-
-    out_lanes = ZG * band_rows * channels
-    spread = repeat_matrix(channels, out_lanes, BF16)
-    taps2 = [
-        lax.dot_general(w2_ref[t], spread, CONTRACT_FIRST, preferred_element_type=F32)
-        for t in range(TAPS * TAPS)
-    ]
-    group = iota((TAPS * channels, out_lanes), 1) // channels
-    for zi in range(ZI):
-        for yi in range(hidden_rows):
-            piece = jnp.zeros((TAPS * channels, out_lanes), F32)
-            for zo in range(ZG):
-                for yo in range(band_rows):
-                    a, b = zi - zo, yi - yo
-                    if 0 <= a < TAPS and 0 <= b < TAPS:
-                        piece = jnp.where(group == zo * band_rows + yo, taps2[a * TAPS + b], piece)
-            piece = piece.astype(BF16)
-            at = (zi * hidden_rows + yi) * channels
-            for c in range(TAPS):
-                w2t_ref[c, at : at + channels, :] = piece[c * channels : (c + 1) * channels]
-
-    step = hidden_rows * channels
+    out_lanes = conv_ref.shape[2]
     groups = PZ // ZG
     empty = jnp.zeros((PX, step), BF16)
     for f in range(4):
@@ -190,9 +263,10 @@
             at = (ZI - 1 - j if f % 2 else j) * step
             wide_ref[f, g * PX : (g + 1) * PX, at : at + step] = empty
     start = pl.multiple_of(band * (16 * band_rows), 16)
+    weights = full_ref[...]
     for z in range(PZ):
         cells = taps_ref[z, pl.ds(start, in_rows * 16), :].astype(BF16)
-        value = lax.dot_general(cells, w1_full, CONTRACT_FIRST, preferred_element_type=F32)
+        value = lax.dot_general(cells, weights, CONTRACT_FIRST, preferred_element_type=F32)
         value = value * scale + shift
         value = jnp.maximum(value, 0.01 * value).astype(BF16)
         for g in range(groups):
@@ -224,12 +298,9 @@
         stats_ref[space] = sums
 
 
-def head_kernel(
-    count, band_rows, conv_ref, stats_ref, gain_ref, bias_ref, head_ref, head_bias_ref, out_ref
-):
-    channels = gain_ref.shape[1]
+def head_kernel(count, channels, conv_ref, stats_ref, params_ref, heads_ref, bias_ref, out_ref):
     lanes = conv_ref.shape[2]
-    classes = head_ref.shape[0]
+    per_group = heads_ref.shape[1]
     sums = stats_ref[0]
     for space in range(1, stats_ref.shape[0]):
         sums = sums + stats_ref[space]
@@ -237,49 +308,22 @@
     while reach >= channels:
         sums = sums + pltpu.roll(sums, reach, 1)
         reach //= 2
-    repeat = repeat_matrix(channels, lanes, F32)
-    params = jnp.concatenate([gain_ref[...], bias_ref[...], jnp.zeros((6, channels), F32)], axis=0)
-    params = jnp.dot(params, repeat, precision=HI, preferred_element_type=F32)
-    head = jnp.concatenate([head_ref[...].astype(F32), jnp.zeros((8 - classes, channels), F32)], 0)
-    head = jnp.dot(head, repeat, precision=HI, preferred_element_type=F32)
-    per_z = classes * band_rows
-    shape = (ZG * per_z, lanes)
-    row_z, row_k, row_y = (
-        iota(shape, 0) // per_z,
-        iota(shape, 0) // band_rows % classes,
-        iota(shape, 0) % band_rows,
-    )
-    full = jnp.zeros(shape, F32)
-    for k in range(classes):
-        full = jnp.where(row_k == k, head[k : k + 1], full)
-    lane_z = iota(shape, 1) // (band_rows * channels)
-    lane_y = iota(shape, 1) // channels % band_rows
-    heads = [
-        jnp.where((lane_z == z) & (lane_y == row_y), full, 0.0).astype(BF16)
-        for z in (row_z, ZG - 1 - row_z)
-    ]
-    shape = (ZG * per_z, PX)
-    row_k = iota(shape, 0) // band_rows % classes
-    bias = jnp.zeros(shape, F32)
-    for k in range(classes):
-        bias = jnp.where(row_k == k, head_bias_ref[k], bias)
     groups = conv_ref.shape[1] // PX
     totals = [None] * groups
     for f in range(4):
         mean = sums[2 * f : 2 * f + 1] / count
         variance = sums[2 * f + 1 : 2 * f + 2] / count - mean * mean
-        scale = lax.rsqrt(variance + 1e-05) * params[0:1]
-        shift = params[1:2] - mean * scale
+        scale = lax.rsqrt(variance + 1e-05) * params_ref[0:1]
+        shift = params_ref[1:2] - mean * scale
         for g in range(groups):
             value = conv_ref[f, g * PX : (g + 1) * PX, :] * scale + shift
             value = jnp.maximum(value, 0.01 * value).astype(BF16)
             logits = lax.dot_general(
-                heads[f % 2], value, CONTRACT_LAST, preferred_element_type=F32
+                heads_ref[f % 2], value, CONTRACT_LAST, preferred_element_type=F32
             )
             totals[g] = logits if totals[g] is None else totals[g] + logits
     for g in range(groups):
-        at = g * ZG * per_z
-        out_ref[at : at + ZG * per_z, :] = totals[g] * 0.25 + bias
+        out_ref[g * per_group : (g + 1) * per_group, :] = totals[g] * 0.25 + bias_ref[...]
 
 
 def place_kernel(spaces, offsets_ref, parts_ref, out_ref, pad_ref):
@@ -298,7 +342,7 @@
     coverage = jnp.zeros(shape, F32)
     for item in range(parts_ref.shape[0]):
         pad_ref[item, count : count + PZ * per_z, :] = parts_ref[item].astype(F32)
-        start_z, start_x = offsets_ref[item, 0], offsets_ref[item, 1]
+        start_z, start_x = offsets_ref[0, item], offsets_ref[1, item]
         first = jnp.clip(slab - start_z, -slab_rows, PZ) * per_z + count
         part = pad_ref[item, pl.ds(first, count), :]
         part = jnp.concatenate([part, jnp.zeros((count, width - PX), F32)], axis=1)
@@ -322,10 +366,12 @@
             out_ref[z, k] = value[at : at + band_rows]
 
 
-def mirrored(weights, channels):
-    taps = weights.reshape(TAPS, TAPS, channels, TAPS)
-    sets = jnp.stack([taps, taps[::-1], taps[..., ::-1], taps[::-1, ..., ::-1]])
-    return sets.transpose(2, 1, 4, 0, 3).reshape(TAPS, TAPS * TAPS, 4, 1, channels)
+def in_vmem(value):
+    return pltpu.with_memory_space_constraint(value, pltpu.VMEM)
+
+
+def in_hbm(value):
+    return pltpu.with_memory_space_constraint(value, pltpu.HBM)
 
 
 def local(
@@ -347,7 +393,14 @@
     classes = head_weight.shape[0]
     rows = band_rows * spaces
     hidden_rows = band_rows + TAPS - 1
+    in_rows = hidden_rows + TAPS - 1
     block = slab_rows * band_rows
+    lanes1 = 4 * hidden_rows * channels
+    lanes2 = ZG * band_rows * channels
+    depth2 = ZI * hidden_rows * channels
+    cells = PZ // ZG * PX
+    per_z = classes * band_rows
+    corners = in_hbm(offsets.T)
 
     windows = pl.pallas_call(
         cut_kernel,
@@ -356,67 +409,80 @@
         out_specs=VMEM,
         scratch_shapes=[pltpu.VMEM((block, width), F32)],
         name="cut",
-    )(offsets, image)
+    )(corners, image)
     windows = windows.reshape(groups * spaces, block, PX)
     gathered = lax.all_to_all(windows, ("patch", "space"), 0, 0, tiled=True)
 
-    w1 = mirrored(conv1_weight, channels)
-    w1 = jnp.pad(w1, ((0, 0), (0, 16 - TAPS * TAPS), (0, 0), (0, 0), (0, 0)))
-    w1 = jnp.broadcast_to(w1, (TAPS, 16, 4, hidden_rows, channels))
-    w1 = w1.reshape(TAPS, 16, 4 * hidden_rows * channels)
-    out_lanes = ZG * band_rows * channels
-    cells = PZ // ZG * PX
+    flat, full, w2t, params1, params2, heads, bias = pl.pallas_call(
+        functools.partial(prep_kernel, band_rows),
+        out_shape=(
+            pltpu.VMEM((TAPS * 16, lanes1), F32),
+            pltpu.VMEM((in_rows * 16, lanes1), BF16),
+            pltpu.VMEM((TAPS, depth2, lanes2), BF16),
+            pltpu.VMEM((8, lanes1), F32),
+            pltpu.VMEM((8, lanes2), F32),
+            pltpu.VMEM((2, ZG * per_z, lanes2), BF16),
+            pltpu.VMEM((ZG * per_z, PX), F32),
+        ),
+        in_specs=[VMEM] * 7 + [SMEM],
+        out_specs=(VMEM,) * 7,
+        name="prep",
+    )(
+        in_hbm(conv1_weight.transpose(0, 2, 1)),
+        in_hbm(conv2_weight),
+        in_hbm(norm1_gain.reshape(1, channels)),
+        in_hbm(norm1_bias.reshape(1, channels)),
+        in_hbm(norm2_gain.reshape(1, channels)),
+        in_hbm(norm2_bias.reshape(1, channels)),
+        in_hbm(head_weight),
+        in_hbm(head_bias),
+    )
+    scratch = (
+        ((groups * spaces * block, PX), F32),
+        ((PZ, (rows + 4) * 16, PX), F32),
+        ((rows * 16, rows * 16), F32),
+        ((4, cells, depth2), BF16),
+        ((8, lanes2), F32),
+    )
+    size = sum(math.prod(shape) * jnp.dtype(kind).itemsize for shape, kind in scratch)
     conv, stats = pl.pallas_call(
         functools.partial(main_kernel, spaces, slab_rows, band_rows),
         out_shape=(
-            jax.ShapeDtypeStruct((4, cells, out_lanes), F32),
-            jax.ShapeDtypeStruct((spaces, 8, out_lanes), F32),
+            pltpu.VMEM((4, cells, lanes2), F32),
+            pltpu.VMEM((spaces, 8, lanes2), F32),
         ),
         in_specs=[SMEM] + [VMEM] * 5,
         out_specs=(VMEM, VMEM),
-        scratch_shapes=[
-            pltpu.VMEM((groups * spaces * block, PX), F32),
-            pltpu.VMEM((PZ, (rows + 4) * 16, PX), F32),
-            pltpu.VMEM((rows * 16, rows * 16), F32),
-            pltpu.VMEM((4, cells, ZI * hidden_rows * channels), BF16),
-            pltpu.VMEM((TAPS, ZI * hidden_rows * channels, out_lanes), BF16),
-            pltpu.VMEM((8, out_lanes), F32),
-        ],
+        scratch_shapes=[pltpu.VMEM(shape, kind) for shape, kind in scratch],
+        compiler_params=pltpu.CompilerParams(vmem_limit_bytes=min(2 * size + (16 << 20), 52 << 20)),
         name="main",
     )(
-        offsets,
-        gathered,
-        w1,
-        conv2_weight,
-        norm1_gain.reshape(1, channels),
-        norm1_bias.reshape(1, channels),
+        corners,
+        in_vmem(gathered),
+        in_vmem(flat),
+        in_vmem(full),
+        in_vmem(w2t),
+        in_vmem(params1),
     )
     stats = lax.all_to_all(stats, "space", 0, 0, tiled=True)
     averaged = pl.pallas_call(
-        functools.partial(head_kernel, float(PZ * rows * PX), band_rows),
-        out_shape=jax.ShapeDtypeStruct((PZ * classes * band_rows, PX), F32),
-        in_specs=[VMEM] * 5 + [SMEM],
+        functools.partial(head_kernel, float(PZ * rows * PX), channels),
+        out_shape=pltpu.VMEM((PZ * per_z, PX), F32),
+        in_specs=[VMEM] * 5,
         out_specs=VMEM,
+        compiler_params=pltpu.CompilerParams(vmem_limit_bytes=8 << 20),
         name="head",
-    )(
-        conv,
-        stats,
-        norm2_gain.reshape(1, channels),
-        norm2_bias.reshape(1, channels),
-        head_weight,
-        head_bias,
-    )
+    )(in_vmem(conv), in_vmem(stats), in_vmem(params2), in_vmem(heads), in_vmem(bias))
     parts = lax.all_gather(averaged, "patch", axis=0, tiled=False)
     return pl.pallas_call(
         functools.partial(place_kernel, spaces),
         out_shape=jax.ShapeDtypeStruct((slab_rows, classes, band_rows, width), F32),
         in_specs=[SMEM, VMEM],
         out_specs=VMEM,
-        scratch_shapes=[
-            pltpu.VMEM((groups, (2 * slab_rows + PZ) * classes * band_rows, PX), F32)
-        ],
+        scratch_shapes=[pltpu.VMEM((groups, (2 * slab_rows + PZ) * per_z, PX), F32)],
+        compiler_params=pltpu.CompilerParams(vmem_limit_bytes=8 << 20),
         name="place",
-    )(offsets, parts)
+    )(corners, in_vmem(parts))
 
 
 def solution(mesh):

time: 49.6 us -> 40.9 us (0.82)
  local copies, waits for them, and re-layouts: 5.07 us -> 0 us
  Pallas kernels: 14.3 us -> 11.3 us
  waiting for transfers between devices: 3.96 us -> 6.37 us
  blocking collectives: 17.4 us -> 15.5 us
  other arithmetic: 0.74 us -> 0 us
    all_to_all x1, waiting for transfers between devices: 3.96 us -> 6.37 us  [local(): gathered = lax.all_to_all(windows, ('patch', 'space'), 0, 0, tiled=True)]
    unnamed x3 -> x0, local copies, waits for them, and re-layouts: 2 us -> none
    pallas_call x1, Pallas kernels: 8.14 us -> 6.28 us  [local(): pl.pallas_call(functools.partial(main_kernel, spaces, slab_rows, band_row...]
    rev x2 -> x0, local copies, waits for them, and re-layouts: 1.46 us -> none  [mirrored(): sets = jnp.stack([taps, taps[::-1], taps[..., ::-1], taps[::-1, ..., ::-1]])]
    all_gather x1, blocking collectives: 6.59 us -> 5.59 us  [local(): parts = lax.all_gather(averaged, 'patch', axis=0, tiled=False)]
    all_to_all x1, blocking collectives: 10.9 us -> 9.92 us  [local(): stats = lax.all_to_all(stats, 'space', 0, 0, tiled=True)]
    pallas_call x1 -> x2, Pallas kernels: 2.96 us -> 2.07 us  [the longest x1 1.43 us: local(): pl.pallas_call(functools.partial(prep_kernel, band_rows), out_shape=(pltp...]
    reshape x1 -> x0, local copies, waits for them, and re-layouts: 0.81 us -> none  [local(): w1 = w1.reshape(TAPS, 16, 4 * hidden_rows * channels)]
  transfers between devices with their start and end apart: 1 -> 1, of which waited for: 1 -> 1; matrix products, arithmetic and copies ran while one was open for 8% -> 0% of each run, Pallas kernels for 0% -> 4%
where the time goes in v2:
time: 40.9 us; the launch traced here: 40.5 us
  blocking collectives  15.5 us (38%)
  Pallas kernels  11.3 us (28%)
  starting transfers between devices  7.33 us (18%)
  waiting for transfers between devices  6.37 us (16%)
    all_to_all x1, blocking collectives, local(): stats = lax.all_to_all(stats, 'space', 0, 0, tiled=True)  9.92 us
    all_to_all x1, starting transfers between devices, local(): gathered = lax.all_to_all(windows, ('patch', 'space'), 0, 0, tiled=True)  7.33 us
    all_to_all x1, waiting for transfers between devices, local(): gathered = lax.all_to_all(windows, ('patch', 'space'), 0, 0, tiled=True)  6.37 us
    pallas_call x1, Pallas kernels, local(): pl.pallas_call(functools.partial(main_kernel, spaces, slab_rows, band_row...  6.28 us
    all_gather x1, blocking collectives, local(): parts = lax.all_gather(averaged, 'patch', axis=0, tiled=False)  5.59 us
    pallas_call x1, Pallas kernels, local(): pl.pallas_call(functools.partial(place_kernel, spaces), out_shape=jax.Sha...  1.48 us
    pallas_call x1, Pallas kernels, local(): pl.pallas_call(cut_kernel, out_shape=jax.ShapeDtypeStruct((groups, spaces...  1.44 us
    pallas_call x1, Pallas kernels, local(): pl.pallas_call(functools.partial(prep_kernel, band_rows), out_shape=(pltp...  1.43 us
  transfers between devices with their start and end apart: 1, of which 1 were waited for; matrix products, arithmetic and copies ran while one was open for 0% of the time, Pallas kernels for 4%

profile of v2, /device:TPU:0, one launch (start us, length us, event | category | flops | bytes accessed | tf_op | source)
XLA Modules:
  0.0 40.5 jit_solution(17673804407764770419)
XLA Ops:
  0.0 1.4 %cut.1 = bf16[4,8,16,128]{3,2,1,0:T(8,128)(2,1)} custom-call(s32[2,4]{1,0:T(2,128)} %bitcast.11, bf16[8,2,256]{2,1,0:T(2,128)(2,1)} %image_ref.1), custom_call_target="tpu_custom_call" | custom-call | tf_op jit(solution)/shard_map/cut/pallas_call | solution.py:405
  1.4 7.3 %all-to-all-start = ((bf16[32,16,128]{2,1,0:T(8,128)(2,1)}), bf16[32,16,128]{2,1,0:T(8,128)(2,1)S(1)}, u32[]{:S(2)}, u32[]{:S(2)}) async-start(bf16[32,16,128]{2,1,0:T(8,128)(2,1)} %bitcast.9), calls=%async_computation | async-start | bytes 262144 | tf_op jit(solution)/shard_map/all_to_all | solution.py:414
  8.8 1.4 %prep.1 = (f32[48,512]{1,0:T(8,128)S(1)}, bf16[96,512]{1,0:T(8,128)(2,1)S(1)}, bf16[3,768,256]{2,1,0:T(8,128)(2,1)S(1)}, f32[8,512]{1,0:T(8,128)S(1)}, f32[8,256...) custom-call(bf16[9,3,32]{2,1,0:T(4,128)(2,1)} %bitcast.10, bf16[9,32,96]{2,1,0:T(8,128)(2,1)} %w2_ref.1, ...), custom_call_target="tpu_custom_call" | custom-call | tf_op jit(solution)/shard_map/prep/pallas_call | solution.py:416
  10.2 6.4 %all-to-all-done.gathered_ref = bf16[32,16,128]{2,1,0:T(8,128)(2,1)S(1)} async-done(((bf16[32,16,128]{2,1,0:T(8,128)(2,1)}), bf16[32,16,128]{2,1,0:T(8,128)(2,1)S(1)}, u32[]{:S(2)}, u32[]{:S(2)}) %all-to-all-start) | async-done | bytes 131104 | tf_op jit(solution)/shard_map/all_to_all | solution.py:414
  16.6 6.3 %main.1 = (f32[4,512,256]{2,1,0:T(8,128)S(1)}, f32[8,8,256]{2,1,0:T(8,128)S(1)}) custom-call(s32[2,4]{1,0:T(2,128)} %bitcast.12, bf16[32,16,128]{2,1,0:T(8,128)(2,1)S(1)} %all-to-all-done.gathered_ref, f32[48,512]{1,0:T(8,128)S(1)} %get-tuple-element.14.flat_ref, bf16[96,512]{1,0:T(8,128)(2,1)S(1)} %get-tuple-element.15.full_ref, ...), custom_call_target="tpu_custom_call" | custom-call | tf_op jit(solution)/shard_map/main/pallas_call | solution.py:448
  22.9 9.9 %all_to_all.10.stats_ref = f32[8,8,256]{2,1,0:T(8,128)S(1)} all-to-all(f32[8,8,256]{2,1,0:T(8,128)S(1)} %get-tuple-element.19), channel_id=1, replica_groups=mesh['patch'=4,'space'=8] {'space'}, dimensions={0} | all-to-all | bytes 131072 | tf_op jit(solution)/shard_map/all_to_all | solution.py:467
  32.8 0.6 %head.1 = f32[96,128]{1,0:T(8,128)S(1)} custom-call(f32[4,512,256]{2,1,0:T(8,128)S(1)} %get-tuple-element.18.conv_ref, f32[8,8,256]{2,1,0:T(8,128)S(1)} %all_to_all.10.stats_ref, f32[8,256]{1,0:T(8,128)S(1)} %get-tuple-element.20.params_ref, bf16[2,24,256]{2,1,0:T(8,128)(2,1)S(1)} %get-tuple-element.21.heads_ref, f32[24,128]{1,0:T(8,128)S(1)} %get-tuple-element.22.bias_ref), custom_call_target="tpu_custom_call" | custom-call | tf_op jit(solution)/shard_map/head/pallas_call | solution.py:468
  33.4 5.6 %all-gather = f32[384,128]{1,0:T(8,128)S(1)} all-gather(f32[96,128]{1,0:T(8,128)S(1)} %head.1), channel_id=2, replica_groups=mesh['patch'=4,'space'=8] {'patch'}, dimensions={0}, use_global_device_ids=true | all-gather | bytes 245760 | tf_op jit(solution)/shard_map/all_gather | solution.py:476
  39.0 1.5 %place.1 = f32[8,3,2,256]{3,2,1,0:T(2,128)} custom-call(s32[2,4]{1,0:T(2,128)} %bitcast.13, f32[4,96,128]{2,1,0:T(8,128)S(1)} %bitcast.8), custom_call_target="tpu_custom_call" | custom-call | tf_op jit(solution)/shard_map/place/pallas_call | solution.py:477
Async XLA Ops:
  1.4 15.1 %all-to-all-start = ((bf16[32,16,128]{2,1,0:T(8,128)(2,1)}), bf16[32,16,128]{2,1,0:T(8,128)(2,1)S(1)}, u32[]{:S(2)}, u32[]{:S(2)}) async-start(bf16[32,16,128]{2,1,0:T(8,128)(2,1)} %bitcast.9), calls=%async_computation | async-start | bytes 262144 | tf_op jit(solution)/shard_map/all_to_all | solution.py:414

commit v3 on v2

v3 whole, which is shorter than its diff:
```python
import functools
import math

import jax
import jax.numpy as jnp
from jax import lax
from jax.experimental import pallas as pl
from jax.experimental.pallas import tpu as pltpu
from jax.sharding import PartitionSpec as P

PX = 128
PZ = 16
TAPS = 3
ZG = 4
ZI = ZG + TAPS - 1
F32 = jnp.float32
BF16 = jnp.bfloat16
HI = lax.Precision.HIGHEST
CONTRACT_FIRST = (((0,), (0,)), ((), ()))
CONTRACT_LAST = (((1,), (1,)), ((), ()))
VMEM = pl.BlockSpec(memory_space=pltpu.VMEM)
SMEM = pl.BlockSpec(memory_space=pltpu.SMEM)


def iota(shape, dim):
    return lax.broadcasted_iota(jnp.int32, shape, dim)


def repeat_matrix(channels, lanes, dtype):
    shape = (channels, lanes)
    return (iota(shape, 0) == iota(shape, 1) % channels).astype(dtype)


def cut_kernel(offsets_ref, image_ref, out_ref, rows_ref):
    slab_rows, band_rows, width = image_ref.shape
    for z in range(slab_rows):
        rows_ref[z * band_rows : (z + 1) * band_rows, :] = image_ref[z].astype(F32)
    rows = rows_ref[...]
    items = offsets_ref.shape[1]
    spaces = out_ref.shape[0] // items
    for item in range(items):
        shift = lax.rem(width - offsets_ref[1, item], width)
        window = pltpu.roll(rows, shift, 1)[:, :PX].astype(BF16)
        for space in range(spaces):
            out_ref[item * spaces + space] = window


def prep_kernel(
    spaces,
    slab_rows,
    band_rows,
    offsets_ref,
    w1_ref,
    w2_ref,
    gain1_ref,
    bias1_ref,
    gain2_ref,
    bias2_ref,
    head_ref,
    head_bias_ref,
    every_ref,
    own_ref,
    wide_ref,
    params_ref,
    heads_ref,
    bias_ref,
    weights_ref,
    corner_ref,
    flat_ref,
):
    channels = gain1_ref.shape[1]
    classes = head_ref.shape[0]
    rows = band_rows * spaces
    hidden_rows = band_rows + TAPS - 1
    step = 4 * channels
    band = lax.axis_index("space")
    patch = lax.axis_index("patch")

    repeat = repeat_matrix(channels, step, BF16)
    taps = [
        jnp.dot(w1_ref[t], repeat, preferred_element_type=F32) for t in range(TAPS * TAPS)
    ]
    mirror = iota((1, step), 1) // channels
    flat_ref[...] = jnp.zeros_like(flat_ref)
    for b in range(TAPS):
        for a in range(TAPS):
            one, two = taps[a * TAPS + b], taps[(TAPS - 1 - a) * TAPS + b]
            for c in range(TAPS):
                d = TAPS - 1 - c
                row = jnp.where(
                    mirror < 2,
                    jnp.where(mirror == 0, one[c : c + 1], two[c : c + 1]),
                    jnp.where(mirror == 2, one[d : d + 1], two[d : d + 1]),
                )
                at = 16 * b + a * TAPS + c
                flat_ref[at : at + 1, :] = row
    flat = flat_ref[...]

    def row_of(shape):
        r = iota(shape, 0)
        return r % spaces * band_rows + r // spaces

    zeros = jnp.zeros((16, step), BF16)
    for y in range(rows):
        delta = row_of((rows, step)) - (y - 1)
        masks = [delta == b for b in range(TAPS)]
        for slot in range(TAPS * TAPS):
            piece = jnp.zeros((rows, step), F32)
            for b in range(TAPS):
                piece = jnp.where(masks[b], flat[16 * b + slot : 16 * b + slot + 1], piece)
            every_ref[slot * rows : (slot + 1) * rows, y * step : (y + 1) * step] = piece.astype(
                BF16
            )
        every_ref[TAPS * TAPS * rows :, y * step : (y + 1) * step] = zeros
    lanes = own_ref.shape[1]
    shape = (step, lanes)
    lane = iota(shape, 1)
    spread = iota(shape, 0) == lane // (hidden_rows * channels) * channels + lane % channels
    spread = jnp.dot(flat.astype(BF16), spread.astype(BF16), preferred_element_type=F32)
    shape = (rows, lanes)
    delta = row_of(shape) - iota(shape, 1) // channels % hidden_rows - (band * band_rows - 2)
    masks = [delta == b for b in range(TAPS)]
    for slot in range(TAPS * TAPS):
        piece = jnp.zeros(shape, F32)
        for b in range(TAPS):
            piece = jnp.where(masks[b], spread[16 * b + slot : 16 * b + slot + 1], piece)
        own_ref[slot * rows : (slot + 1) * rows, :] = piece.astype(BF16)
    own_ref[TAPS * TAPS * rows :, :] = jnp.zeros((16, lanes), BF16)

    lanes = ZG * band_rows * channels
    spread = repeat_matrix(channels, lanes, BF16)
    taps = [
        lax.dot_general(w2_ref[t], spread, CONTRACT_FIRST, preferred_element_type=F32)
        for t in range(TAPS * TAPS)
    ]
    group = iota((TAPS * channels, lanes), 1) // channels
    for zi in range(ZI):
        for yi in range(hidden_rows):
            piece = jnp.zeros((TAPS * channels, lanes), F32)
            for zo in range(ZG):
                for yo in range(band_rows):
                    a, b = zi - zo, yi - yo
                    if 0 <= a < TAPS and 0 <= b < TAPS:
                        piece = jnp.where(group == zo * band_rows + yo, taps[a * TAPS + b], piece)
            piece = piece.astype(BF16)
            at = (zi * hidden_rows + yi) * channels
            for c in range(TAPS):
                wide_ref[c, at : at + channels, :] = piece[c * channels : (c + 1) * channels]

    table = jnp.concatenate(
        [
            gain1_ref[...],
            bias1_ref[...],
            gain2_ref[...],
            bias2_ref[...],
            head_ref[...].astype(F32),
            jnp.zeros((8 - classes - 4, channels), F32),
        ],
        axis=0,
    )
    spread = repeat_matrix(channels, lanes, F32)
    table = jnp.dot(table, spread, precision=HI, preferred_element_type=F32)
    params_ref[...] = table[:, :step]

    per_z = classes * band_rows
    shape = (ZG * per_z, lanes)
    row_z = iota(shape, 0) // per_z
    row_k = iota(shape, 0) // band_rows % classes
    row_y = iota(shape, 0) % band_rows
    full = jnp.zeros(shape, F32)
    for k in range(classes):
        full = jnp.where(row_k == k, table[4 + k : 5 + k], full)
    lane_z = iota(shape, 1) // (band_rows * channels)
    lane_y = iota(shape, 1) // channels % band_rows
    for f, z in enumerate((row_z, ZG - 1 - row_z)):
        heads_ref[f] = jnp.where((lane_z == z) & (lane_y == row_y), full, 0.0).astype(BF16)
    row_k = iota(bias_ref.shape, 0) // band_rows % classes
    bias = jnp.zeros(bias_ref.shape, F32)
    for k in range(classes):
        bias = jnp.where(row_k == k, head_bias_ref[k], bias)
    bias_ref[...] = bias

    items, count, width = weights_ref.shape
    shape = (count, width)
    slab = patch * slab_rows
    z = slab + iota(shape, 0) // per_z
    x = iota(shape, 1)
    y = (band * band_rows + iota(shape, 0) % band_rows).astype(F32) - (rows - 1) / 2.0
    across = y * y * (1.0 / (2.0 * (rows / 8.0) ** 2))
    shape = corner_ref.shape
    corner_row, corner_lane = iota(shape, 0), iota(shape, 1)
    own_z = jnp.where(corner_lane == 0, offsets_ref[0, patch], 0)
    corners = jnp.where(corner_row == items, own_z, 0)
    coverage = jnp.zeros((count, width), F32)
    weights = []
    for k in range(items):
        item = jnp.bitwise_xor(patch, k)
        start_z, start_x = offsets_ref[0, item], offsets_ref[1, item]
        first = jnp.clip(slab - start_z, -slab_rows, PZ) * per_z + count
        values = jnp.where(corner_lane == 0, first, start_x)
        corners = jnp.where((corner_row == k) & (corner_lane < 2), values, corners)
        rel_z, rel_x = z - start_z, x - start_x
        inside = (rel_z >= 0) & (rel_z < PZ) & (rel_x >= 0) & (rel_x < PX)
        far_z = rel_z.astype(F32) - (PZ - 1) / 2.0
        far_x = rel_x.astype(F32) - (PX - 1) / 2.0
        power = (
            across
            + far_z * far_z * (1.0 / (2.0 * (PZ / 8.0) ** 2))
            + far_x * far_x * (1.0 / (2.0 * (PX / 8.0) ** 2))
        )
        weight = jnp.where(inside, jnp.exp(-power), 0.0)
        weights.append(weight)
        coverage = coverage + weight
    share = 1.0 / jnp.maximum(coverage, 0.1)
    for k in range(items):
        weights_ref[k] = weights[k] * share
    corner_ref[...] = corners


def tap_rows(start_z, gathered_ref, cells_ref, taps_ref, slab_rows, band_rows, spaces):
    block = slab_rows * band_rows
    for device in range(gathered_ref.shape[0]):
        cells_ref[device * block : (device + 1) * block, :] = gathered_ref[device].astype(F32)
    rows = band_rows * spaces
    lane = iota((spaces, PX), 1)
    empty = jnp.zeros((rows, PX), F32)
    for c in range(TAPS):
        taps_ref[0, c * rows : (c + 1) * rows, :] = empty
        at = (TAPS * (TAPS - 1) + c) * rows
        taps_ref[PZ - 1, at : at + rows, :] = empty
    ones = jnp.ones((16, PX), F32)
    for z in range(PZ):
        taps_ref[z, TAPS * TAPS * rows :, :] = ones
        deep = start_z + z
        slab = lax.div(deep, slab_rows)
        base = slab * (spaces * block) + (deep - slab * slab_rows) * band_rows
        for y in range(band_rows):
            line = cells_ref[pl.ds(base + y, spaces, stride=block), :]
            before = jnp.where(lane == 0, 0.0, pltpu.roll(line, 1, 1))
            after = jnp.where(lane == PX - 1, 0.0, pltpu.roll(line, PX - 1, 1))
            for a in range(TAPS):
                at = z + 1 - a
                if 0 <= at < PZ:
                    for c, value in enumerate((before, line, after)):
                        first = (a * TAPS + c) * rows + y * spaces
                        taps_ref[at, first : first + spaces, :] = value


def first_moments(taps_ref, every_ref, rows, step):
    cells = [taps_ref[z].astype(BF16) for z in range(PZ)]
    cells = jnp.concatenate(cells, axis=1)
    gram = lax.dot_general(cells, cells, CONTRACT_LAST, preferred_element_type=F32)
    high = gram.astype(BF16)
    left = gram - high.astype(F32)
    middle = left.astype(BF16)
    low = (left - middle.astype(F32)).astype(BF16)
    first = jnp.zeros((1, step), F32)
    second = jnp.zeros((1, step), F32)
    wide = 4 * step
    for at in range(0, rows * step, wide):
        weights = every_ref[:, at : at + wide]
        product = (
            jnp.dot(high, weights, preferred_element_type=F32)
            + jnp.dot(middle, weights, preferred_element_type=F32)
            + jnp.dot(low, weights, preferred_element_type=F32)
        )
        squares = jnp.sum(product * weights.astype(F32), axis=0, keepdims=True)
        ones = TAPS * TAPS * rows
        for lane in range(0, wide, step):
            first = first + product[ones : ones + 1, lane : lane + step]
            second = second + squares[:, lane : lane + step]
    return first, second


def spread_mirror(value, f, channels):
    value = jnp.where(iota(value.shape, 1) // channels == f, value, 0.0)
    reach = channels
    while reach < value.shape[1]:
        value = value + pltpu.roll(value, reach, 1)
        reach *= 2
    return value


def main_kernel(
    spaces,
    slab_rows,
    band_rows,
    channels,
    gathered_ref,
    corner_ref,
    every_ref,
    own_ref,
    w2t_ref,
    params_ref,
    conv_ref,
    stats_ref,
    cells_ref,
    taps_ref,
    wide_ref,
    sums_ref,
):
    rows = band_rows * spaces
    hidden_rows = band_rows + TAPS - 1
    step = hidden_rows * channels
    band = lax.axis_index("space")
    start_z = corner_ref[lax.axis_size("patch"), 0]
    tap_rows(start_z, gathered_ref, cells_ref, taps_ref, slab_rows, band_rows, spaces)

    first, second = first_moments(taps_ref, every_ref, rows, step)
    count = float(PZ * rows * PX)
    mean = first / count
    variance = second / count - mean * mean
    scale = lax.rsqrt(variance + 1e-05) * params_ref[0:1]
    shift = params_ref[1:2] - mean * scale
    table = jnp.concatenate([scale, shift, jnp.zeros((6, step), F32)], axis=0)
    y = band * band_rows - 1 + iota((8, step), 1) // channels
    inside = (y >= 0) & (y < rows)
    table = jnp.concatenate(
        [jnp.where(inside, spread_mirror(table, f, channels), 0.0) for f in range(4)], axis=1
    )
    scale, shift = table[0:1], table[1:2]

    out_lanes = conv_ref.shape[2]
    groups = PZ // ZG
    empty = jnp.zeros((PX, step), BF16)
    for f in range(4):
        for g, j in ((0, 0), (groups - 1, ZI - 1)):
            at = (ZI - 1 - j if f % 2 else j) * step
            wide_ref[f, g * PX : (g + 1) * PX, at : at + step] = empty
    weights = own_ref[...]
    for z in range(PZ):
        cells = taps_ref[z].astype(BF16)
        value = lax.dot_general(cells, weights, CONTRACT_FIRST, preferred_element_type=F32)
        value = value * scale + shift
        value = jnp.maximum(value, 0.01 * value).astype(BF16)
        for g in range(groups):
            j = z + 1 - ZG * g
            if 0 <= j < ZI:
                for f in range(4):
                    at = (ZI - 1 - j if f % 2 else j) * step
                    wide_ref[f, g * PX : (g + 1) * PX, at : at + step] = value[
                        :, f * step : (f + 1) * step
                    ]

    x = iota((groups * PX, out_lanes), 0) % PX
    for f in range(4):
        cells = wide_ref[f]
        parts = [
            jnp.dot(cells, w2t_ref[c], preferred_element_type=F32) for c in range(TAPS)
        ]
        before, after = (parts[2], parts[0]) if f >= 2 else (parts[0], parts[2])
        value = (
            parts[1]
            + jnp.where(x == 0, 0.0, pltpu.roll(before, 1, 0))
            + jnp.where(x == PX - 1, 0.0, pltpu.roll(after, groups * PX - 1, 0))
        )
        conv_ref[f] = value
        sums_ref[f : f + 1, :] = jnp.sum(value, axis=0, keepdims=True)
        sums_ref[f + 4 : f + 5, :] = jnp.sum(value * value, axis=0, keepdims=True)
    sums = sums_ref[...]
    lanes = 4 * channels
    sums = sum(sums[:, at : at + lanes] for at in range(0, out_lanes, lanes))
    reach = lanes // 2
    while reach >= channels:
        sums = sums + pltpu.roll(sums, reach, 1)
        reach //= 2
    mirror = iota((1, lanes), 1) // channels
    for kind in range(2):
        row = sums[4 * kind : 4 * kind + 1]
        for f in range(1, 4):
            row = jnp.where(mirror == f, sums[4 * kind + f : 4 * kind + f + 1], row)
        for space in range(spaces):
            stats_ref[space, kind : kind + 1, :] = row


def head_kernel(count, channels, conv_ref, stats_ref, params_ref, heads_ref, bias_ref, out_ref):
    lanes = conv_ref.shape[2]
    per_group = heads_ref.shape[1]
    sums = stats_ref[0]
    for space in range(1, stats_ref.shape[0]):
        sums = sums + stats_ref[space]
    mean = sums[0:1] / count
    variance = sums[1:2] / count - mean * mean
    scale = lax.rsqrt(variance + 1e-05) * params_ref[2:3]
    shift = params_ref[3:4] - mean * scale
    table = jnp.concatenate([scale, shift, jnp.zeros((6, 4 * channels), F32)], axis=0)
    groups = conv_ref.shape[1] // PX
    totals = [None] * groups
    for f in range(4):
        own = spread_mirror(table, f, channels)
        own = jnp.concatenate([own] * (lanes // own.shape[1]), axis=1)
        for g in range(groups):
            value = conv_ref[f, g * PX : (g + 1) * PX, :] * own[0:1] + own[1:2]
            value = jnp.maximum(value, 0.01 * value).astype(BF16)
            logits = lax.dot_general(
                heads_ref[f % 2], value, CONTRACT_LAST, preferred_element_type=F32
            )
            totals[g] = logits if totals[g] is None else totals[g] + logits
    for g in range(groups):
        out_ref[g * per_group : (g + 1) * per_group, :] = (
            totals[g] * 0.25 + bias_ref[...]
        ).astype(out_ref.dtype)


def place_kernel(items, corner_ref, weights_ref, *refs):
    parts, (out_ref, pad_ref) = refs[:items], refs[items:]
    slab_rows, classes, band_rows, width = out_ref.shape
    per_z = classes * band_rows
    count = slab_rows * per_z
    blended = jnp.zeros((count, width), F32)
    for k in range(items):
        pad_ref[k, count : count + PZ * per_z, :] = parts[k][...].astype(F32)
        part = pad_ref[k, pl.ds(corner_ref[k, 0], count), :]
        part = jnp.concatenate([part, jnp.zeros((count, width - PX), F32)], axis=1)
        part = pltpu.roll(part, corner_ref[k, 1], 1)
        weight = weights_ref[k]
        blended = blended + jnp.where(weight > 0, part * weight, 0.0)
    for z in range(slab_rows):
        for k in range(classes):
            at = z * per_z + k * band_rows
            out_ref[z, k] = blended[at : at + band_rows]


def in_vmem(value):
    return pltpu.with_memory_space_constraint(value, pltpu.VMEM)


def in_hbm(value):
    return pltpu.with_memory_space_constraint(value, pltpu.HBM)


def local(
    image,
    offsets,
    conv1_weight,
    conv2_weight,
    norm1_gain,
    norm1_bias,
    norm2_gain,
    norm2_bias,
    head_weight,
    head_bias,
):
    groups = lax.axis_size("patch")
    spaces = lax.axis_size("space")
    slab_rows, band_rows, width = image.shape
    channels = norm1_gain.shape[0]
    classes = head_weight.shape[0]
    rows = band_rows * spaces
    hidden_rows = band_rows + TAPS - 1
    block = slab_rows * band_rows
    step = 4 * channels
    lanes1 = 4 * hidden_rows * channels
    lanes2 = ZG * band_rows * channels
    depth1 = TAPS * TAPS * rows + 16
    depth2 = ZI * hidden_rows * channels
    cells = PZ // ZG * PX
    per_z = classes * band_rows
    corners = in_hbm(offsets.T)

    windows = pl.pallas_call(
        cut_kernel,
        out_shape=pltpu.VMEM((groups * spaces, block, PX), BF16),
        in_specs=[SMEM, VMEM],
        out_specs=VMEM,
        scratch_shapes=[pltpu.VMEM((block, width), F32)],
        name="cut",
    )(corners, image)
    gathered = lax.all_to_all(in_vmem(windows), ("patch", "space"), 0, 0, tiled=True)

    every, own, w2t, params, heads, bias, weights, corner = pl.pallas_call(
        functools.partial(prep_kernel, spaces, slab_rows, band_rows),
        out_shape=(
            pltpu.VMEM((depth1, rows * step), BF16),
            pltpu.VMEM((depth1, lanes1), BF16),
            pltpu.VMEM((TAPS, depth2, lanes2), BF16),
            pltpu.VMEM((8, step), F32),
            pltpu.VMEM((2, ZG * per_z, lanes2), BF16),
            pltpu.VMEM((ZG * per_z, PX), F32),
            pltpu.VMEM((groups, slab_rows * per_z, width), F32),
            pltpu.VMEM(((groups + 8) // 8 * 8, 128), jnp.int32),
        ),
        in_specs=[SMEM] + [VMEM] * 7 + [SMEM],
        out_specs=(VMEM,) * 8,
        scratch_shapes=[pltpu.VMEM((TAPS * 16, step), F32)],
        compiler_params=pltpu.CompilerParams(vmem_limit_bytes=16 << 20),
        name="prep",
    )(
        corners,
        in_hbm(conv1_weight.transpose(0, 2, 1)),
        in_hbm(conv2_weight),
        in_hbm(norm1_gain.reshape(1, channels)),
        in_hbm(norm1_bias.reshape(1, channels)),
        in_hbm(norm2_gain.reshape(1, channels)),
        in_hbm(norm2_bias.reshape(1, channels)),
        in_hbm(head_weight),
        in_hbm(head_bias),
    )
    scratch = (
        ((groups * spaces * block, PX), F32),
        ((PZ, depth1, PX), F32),
        ((4, cells, depth2), BF16),
        ((8, lanes2), F32),
    )
    size = sum(math.prod(shape) * jnp.dtype(kind).itemsize for shape, kind in scratch)
    conv, stats = pl.pallas_call(
        functools.partial(main_kernel, spaces, slab_rows, band_rows, channels),
        out_shape=(
            pltpu.VMEM((4, cells, lanes2), F32),
            pltpu.VMEM((spaces, 2, step), F32),
        ),
        in_specs=[VMEM] * 6,
        out_specs=(VMEM, VMEM),
        scratch_shapes=[pltpu.VMEM(shape, kind) for shape, kind in scratch],
        compiler_params=pltpu.CompilerParams(vmem_limit_bytes=min(2 * size + (16 << 20), 40 << 20)),
        name="main",
    )(
        in_vmem(gathered),
        in_vmem(corner),
        in_vmem(every),
        in_vmem(own),
        in_vmem(w2t),
        in_vmem(params),
    )
    stats = lax.all_to_all(stats, "space", 0, 0, tiled=True)
    averaged = pl.pallas_call(
        functools.partial(head_kernel, float(PZ * rows * PX), channels),
        out_shape=pltpu.VMEM((PZ * per_z, PX), BF16),
        in_specs=[VMEM] * 5,
        out_specs=VMEM,
        compiler_params=pltpu.CompilerParams(vmem_limit_bytes=8 << 20),
        name="head",
    )(in_vmem(conv), in_vmem(stats), in_vmem(params), in_vmem(heads), in_vmem(bias))
    parts = [averaged] + [
        lax.ppermute(averaged, "patch", [(i, i ^ k) for i in range(groups)])
        for k in range(1, groups)
    ]
    return pl.pallas_call(
        functools.partial(place_kernel, groups),
        out_shape=jax.ShapeDtypeStruct((slab_rows, classes, band_rows, width), F32),
        in_specs=[VMEM] * (2 + groups),
        out_specs=VMEM,
        scratch_shapes=[pltpu.VMEM((groups, (2 * slab_rows + PZ) * per_z, PX), F32)],
        compiler_params=pltpu.CompilerParams(vmem_limit_bytes=8 << 20),
        name="place",
    )(in_vmem(corner), in_vmem(weights), *[in_vmem(part) for part in parts])


def solution(mesh):
    return jax.shard_map(
        local,
        mesh=mesh,
        in_specs=(P("patch", "space", None), P(), P(), P(), P(), P(), P(), P(), P(), P()),
        out_specs=P("patch", None, "space", None),
        check_vma=False,
    )
```

time: 40.9 us -> 37.4 us (0.914)
  blocking collectives: 15.5 us -> 9.53 us
  starting transfers between devices: 7.33 us -> 9.22 us
  waiting for transfers between devices: 6.37 us -> 8.07 us
  Pallas kernels: 11.3 us -> 10.3 us
    all_gather x1 -> x0, blocking collectives: 5.59 us -> none  [local(): parts = lax.all_gather(averaged, 'patch', axis=0, tiled=False)]
    ppermute x0 -> x3, waiting for transfers between devices: none -> 2.05 us  [local(): lax.ppermute(averaged, 'patch', [(i, i ^ k) for i in range(groups)])]
    ppermute x0 -> x3, starting transfers between devices: none -> 1.9 us  [local(): lax.ppermute(averaged, 'patch', [(i, i ^ k) for i in range(groups)])]
    pallas_call x1, Pallas kernels: 6.28 us -> 5.54 us  [local(): pl.pallas_call(functools.partial(main_kernel, spaces, slab_rows, band_row...]
  transfers between devices with their start and end apart: 1 -> 4, of which waited for: 1 -> 3; matrix products, arithmetic and copies ran while one was open for 0% -> 0% of each run, Pallas kernels for 4% -> 5%
where the time goes in v3:
time: 37.4 us; the launch traced here: 37.1 us
  Pallas kernels  10.3 us (28%)
  blocking collectives  9.53 us (25%)
  starting transfers between devices  9.22 us (25%)
  waiting for transfers between devices  8.07 us (22%)
    all_to_all x1, blocking collectives, local(): stats = lax.all_to_all(stats, 'space', 0, 0, tiled=True)  9.53 us
    all_to_all x1, starting transfers between devices, local(): lax.all_to_all(in_vmem(windows), ('patch', 'space'), 0, 0, tiled=True)  7.33 us
    all_to_all x1, waiting for transfers between devices, local(): lax.all_to_all(in_vmem(windows), ('patch', 'space'), 0, 0, tiled=True)  6.02 us
    pallas_call x1, Pallas kernels, local(): pl.pallas_call(functools.partial(main_kernel, spaces, slab_rows, band_row...  5.54 us
    ppermute x3, waiting for transfers between devices, local(): lax.ppermute(averaged, 'patch', [(i, i ^ k) for i in range(groups)])  2.05 us
    ppermute x3, starting transfers between devices, local(): lax.ppermute(averaged, 'patch', [(i, i ^ k) for i in range(groups)])  1.9 us
    pallas_call x1, Pallas kernels, local(): pl.pallas_call(functools.partial(prep_kernel, spaces, slab_rows, band_row...  1.78 us
    pallas_call x1, Pallas kernels, local(): pl.pallas_call(cut_kernel, out_shape=pltpu.VMEM((groups * spaces, block,...  1.45 us
  transfers between devices with their start and end apart: 4, of which 3 were waited for; matrix products, arithmetic and copies ran while one was open for 0% of the time, Pallas kernels for 5%

profile of v3, /device:TPU:0, one launch (start us, length us, event | category | flops | bytes accessed | tf_op | source)
XLA Modules:
  0.0 37.1 jit_solution(4600619906353823206)
XLA Ops:
  0.0 1.4 %cut.1 = bf16[32,16,128]{2,1,0:T(8,128)(2,1)} custom-call(s32[2,4]{1,0:T(2,128)} %bitcast.7, bf16[8,2,256]{2,1,0:T(2,128)(2,1)} %image_ref.1), custom_call_target="tpu_custom_call" | custom-call | tf_op jit(solution)/shard_map/cut/pallas_call | solution.py:461
  1.4 7.3 %all-to-all-start = ((bf16[32,16,128]{2,1,0:T(8,128)(2,1)}), bf16[32,16,128]{2,1,0:T(8,128)(2,1)S(1)}, u32[]{:S(2)}, u32[]{:S(2)}) async-start(bf16[32,16,128]{2,1,0:T(8,128)(2,1)} %cut.1), calls=%async_computation | async-start | bytes 262144 | tf_op jit(solution)/shard_map/all_to_all | solution.py:469
  8.8 1.8 %prep.1 = (bf16[160,2048]{1,0:T(8,128)(2,1)S(1)}, bf16[160,512]{1,0:T(8,128)(2,1)S(1)}, bf16[3,768,256]{2,1,0:T(8,128)(2,1)S(1)}, f32[8,128]{1,0:T(8,128)S(1)}, ...) custom-call(s32[2,4]{1,0:T(2,128)} %bitcast.8, ...), custom_call_target="tpu_custom_call" | custom-call | tf_op jit(solution)/shard_map/prep/pallas_call | solution.py:471
  10.6 6.0 %all-to-all-done.gathered_ref = bf16[32,16,128]{2,1,0:T(8,128)(2,1)S(1)} async-done(((bf16[32,16,128]{2,1,0:T(8,128)(2,1)}), bf16[32,16,128]{2,1,0:T(8,128)(2,1)S(1)}, u32[]{:S(2)}, u32[]{:S(2)}) %all-to-all-start) | async-done | bytes 131104 | tf_op jit(solution)/shard_map/all_to_all | solution.py:469
  16.6 5.5 %main.1 = (f32[4,512,256]{2,1,0:T(8,128)S(1)}, f32[8,2,128]{2,1,0:T(2,128)S(1)}) custom-call(bf16[32,16,128]{2,1,0:T(8,128)(2,1)S(1)} %all-to-all-done.gathered_ref, s32[8,128]{1,0:T(8,128)S(1)} %get-tuple-element.15.corner_ref, bf16[160,2048]{1,0:T(8,128)(2,1)S(1)} %get-tuple-element.17.every_ref, bf16[160,512]{1,0:T(8,128)(2,1)S(1)} %get-tuple-element.18.own_ref, ...), custom_call_target="tpu_custom_call" | custom-call | tf_op jit(solution)/shard_map/main/pallas_call | solution.py:506
  22.1 9.5 %all_to_all.10.stats_ref = f32[8,2,128]{2,1,0:T(2,128)S(1)} all-to-all(f32[8,2,128]{2,1,0:T(2,128)S(1)} %get-tuple-element.22), channel_id=1, replica_groups=mesh['patch'=4,'space'=8] {'space'}, dimensions={0} | all-to-all | bytes 16384 | tf_op jit(solution)/shard_map/all_to_all | solution.py:525
  31.7 0.7 %head.1.refs_0_ = bf16[96,128]{1,0:T(8,128)(2,1)S(1)} custom-call(f32[4,512,256]{2,1,0:T(8,128)S(1)} %get-tuple-element.21.conv_ref, f32[8,2,128]{2,1,0:T(2,128)S(1)} %all_to_all.10.stats_ref, f32[8,128]{1,0:T(8,128)S(1)} %get-tuple-element.20.params_ref, bf16[2,24,256]{2,1,0:T(8,128)(2,1)S(1)} %get-tuple-element.23.heads_ref, ...), custom_call_target="tpu_custom_call" | custom-call | tf_op jit(solution)/shard_map/head/pallas_call | solution.py:526
  32.3 0.0 collective-permute-start.2
  32.4 0.7 %collective-permute-start.1 = (bf16[96,128]{1,0:T(8,128)(2,1)S(1)}, bf16[96,128]{1,0:T(8,128)(2,1)S(1)}, u32[]{:S(2)}, u32[]{:S(2)}) collective-permute-start(bf16[96,128]{1,0:T(8,128)(2,1)S(1)} %head.1.refs_0_), channel_id=1, source_target_pairs={{0,16},{8,24},{16,0},{24,8},{1,17},{9,25},{17,1},{25,9},{2,18},{10... | collective-permute-start | bytes 73736 | tf_op jit(solution)/shard_map/ppermute | solution.py:535
  33.0 1.2 %collective-permute-start = (bf16[96,128]{1,0:T(8,128)(2,1)S(1)}, bf16[96,128]{1,0:T(8,128)(2,1)S(1)}, u32[]{:S(2)}, u32[]{:S(2)}) collective-permute-start(bf16[96,128]{1,0:T(8,128)(2,1)S(1)} %head.1.refs_0_), channel_id=1, source_target_pairs={{0,8},{8,0},{16,24},{24,16},{1,9},{9,1},{17,25},{25,17},{2,10},{10... | collective-permute-start | bytes 73736 | tf_op jit(solution)/shard_map/ppermute | solution.py:535
  34.2 1.4 %collective-permute-done.2.refs_3_ = bf16[96,128]{1,0:T(8,128)(2,1)S(1)} collective-permute-done((bf16[96,128]{1,0:T(8,128)(2,1)S(1)}, bf16[96,128]{1,0:T(8,128)(2,1)S(1)}, u32[]{:S(2)}, u32[]{:S(2)}) %collective-permute-start.2) | collective-permute-done | bytes 24608 | tf_op jit(solution)/shard_map/ppermute | solution.py:535
  35.6 0.7 %collective-permute-done.1.refs_2_ = bf16[96,128]{1,0:T(8,128)(2,1)S(1)} collective-permute-done((bf16[96,128]{1,0:T(8,128)(2,1)S(1)}, bf16[96,128]{1,0:T(8,128)(2,1)S(1)}, u32[]{:S(2)}, u32[]{:S(2)}) %collective-permute-start.1) | collective-permute-done | bytes 24608 | tf_op jit(solution)/shard_map/ppermute | solution.py:535
  36.3 0.0 collective-permute-done.refs_1_
  36.3 0.8 %place.1 = f32[8,3,2,256]{3,2,1,0:T(2,128)} custom-call(s32[8,128]{1,0:T(8,128)S(1)} %get-tuple-element.15.corner_ref, f32[4,48,256]{2,1,0:T(8,128)S(1)} %get-tuple-element.16.weights_ref, bf16[96,128]{1,0:T(8,128)(2,1)S(1)} %head.1.refs_0_, bf16[96,128]{1,0:T(8,128)(2,1)S(1)} %collective-permute-done.refs_1_, ...), custom_call_target="tpu_custom_call" | custom-call | tf_op jit(solution)/shard_map/place/pallas_call | solution.py:538
Async XLA Ops:
  1.4 15.1 %all-to-all-start = ((bf16[32,16,128]{2,1,0:T(8,128)(2,1)}), bf16[32,16,128]{2,1,0:T(8,128)(2,1)S(1)}, u32[]{:S(2)}, u32[]{:S(2)}) async-start(bf16[32,16,128]{2,1,0:T(8,128)(2,1)} %cut.1), calls=%async_computation | async-start | bytes 262144 | tf_op jit(solution)/shard_map/all_to_all | solution.py:469
  32.3 3.3 %collective-permute-start.2 = (bf16[96,128]{1,0:T(8,128)(2,1)S(1)}, bf16[96,128]{1,0:T(8,128)(2,1)S(1)}, u32[]{:S(2)}, u32[]{:S(2)}) collective-permute-start(bf16[96,128]{1,0:T(8,128)(2,1)S(1)} %head.1.refs_0_), channel_id=1, source_target_pairs={{0,24},{8,16},{16,8},{24,0},{1,25},{9,17},{17,9},{25,1},{2,26},{10... | collective-permute-start | bytes 73736 | tf_op jit(solution)/shard_map/ppermute | solution.py:535
  32.4 3.9 %collective-permute-start.1 = (bf16[96,128]{1,0:T(8,128)(2,1)S(1)}, bf16[96,128]{1,0:T(8,128)(2,1)S(1)}, u32[]{:S(2)}, u32[]{:S(2)}) collective-permute-start(bf16[96,128]{1,0:T(8,128)(2,1)S(1)} %head.1.refs_0_), channel_id=1, source_target_pairs={{0,16},{8,24},{16,0},{24,8},{1,17},{9,25},{17,1},{25,9},{2,18},{10... | collective-permute-start | bytes 73736 | tf_op jit(solution)/shard_map/ppermute | solution.py:535
  33.0 3.2 %collective-permute-start = (bf16[96,128]{1,0:T(8,128)(2,1)S(1)}, bf16[96,128]{1,0:T(8,128)(2,1)S(1)}, u32[]{:S(2)}, u32[]{:S(2)}) collective-permute-start(bf16[96,128]{1,0:T(8,128)(2,1)S(1)} %head.1.refs_0_), channel_id=1, source_target_pairs={{0,8},{8,0},{16,24},{24,16},{1,9},{9,1},{17,25},{25,17},{2,10},{10... | collective-permute-start | bytes 73736 | tf_op jit(solution)/shard_map/ppermute | solution.py:535

commit v4 on v3

--- a/solution.py
+++ b/solution.py
@@ -13,6 +13,8 @@
 TAPS = 3
 ZG = 4
 ZI = ZG + TAPS - 1
+SLOTS = 16
+LINE = TAPS * (PZ + 2) + 1
 F32 = jnp.float32
 BF16 = jnp.bfloat16
 HI = lax.Precision.HIGHEST
@@ -58,15 +60,15 @@
     bias2_ref,
     head_ref,
     head_bias_ref,
-    every_ref,
-    own_ref,
+    flat_ref,
+    full_ref,
     wide_ref,
     params_ref,
     heads_ref,
     bias_ref,
     weights_ref,
     corner_ref,
-    flat_ref,
+    narrow_ref,
 ):
     channels = gain1_ref.shape[1]
     classes = head_ref.shape[0]
@@ -81,7 +83,7 @@
         jnp.dot(w1_ref[t], repeat, preferred_element_type=F32) for t in range(TAPS * TAPS)
     ]
     mirror = iota((1, step), 1) // channels
-    flat_ref[...] = jnp.zeros_like(flat_ref)
+    narrow_ref[...] = jnp.zeros_like(narrow_ref)
     for b in range(TAPS):
         for a in range(TAPS):
             one, two = taps[a * TAPS + b], taps[(TAPS - 1 - a) * TAPS + b]
@@ -92,40 +94,23 @@
                     jnp.where(mirror == 0, one[c : c + 1], two[c : c + 1]),
                     jnp.where(mirror == 2, one[d : d + 1], two[d : d + 1]),
                 )
-                at = 16 * b + a * TAPS + c
-                flat_ref[at : at + 1, :] = row
-    flat = flat_ref[...]
-
-    def row_of(shape):
-        r = iota(shape, 0)
-        return r % spaces * band_rows + r // spaces
-
-    zeros = jnp.zeros((16, step), BF16)
-    for y in range(rows):
-        delta = row_of((rows, step)) - (y - 1)
-        masks = [delta == b for b in range(TAPS)]
-        for slot in range(TAPS * TAPS):
-            piece = jnp.zeros((rows, step), F32)
-            for b in range(TAPS):
-                piece = jnp.where(masks[b], flat[16 * b + slot : 16 * b + slot + 1], piece)
-            every_ref[slot * rows : (slot + 1) * rows, y * step : (y + 1) * step] = piece.astype(
-                BF16
-            )
-        every_ref[TAPS * TAPS * rows :, y * step : (y + 1) * step] = zeros
-    lanes = own_ref.shape[1]
+                at = SLOTS * b + a * TAPS + c
+                narrow_ref[at : at + 1, :] = row
+    lanes = flat_ref.shape[1]
     shape = (step, lanes)
     lane = iota(shape, 1)
     spread = iota(shape, 0) == lane // (hidden_rows * channels) * channels + lane % channels
-    spread = jnp.dot(flat.astype(BF16), spread.astype(BF16), preferred_element_type=F32)
-    shape = (rows, lanes)
-    delta = row_of(shape) - iota(shape, 1) // channels % hidden_rows - (band * band_rows - 2)
-    masks = [delta == b for b in range(TAPS)]
-    for slot in range(TAPS * TAPS):
-        piece = jnp.zeros(shape, F32)
+    flat = jnp.dot(
+        narrow_ref[...].astype(BF16), spread.astype(BF16), preferred_element_type=F32
+    )
+    flat_ref[...] = flat
+    lane_row = iota((SLOTS, lanes), 1) // channels % hidden_rows
+    for yi in range(hidden_rows + TAPS - 1):
+        piece = jnp.zeros((SLOTS, lanes), F32)
         for b in range(TAPS):
-            piece = jnp.where(masks[b], spread[16 * b + slot : 16 * b + slot + 1], piece)
-        own_ref[slot * rows : (slot + 1) * rows, :] = piece.astype(BF16)
-    own_ref[TAPS * TAPS * rows :, :] = jnp.zeros((16, lanes), BF16)
+            if 0 <= yi - b < hidden_rows:
+                piece = jnp.where(lane_row == yi - b, flat[SLOTS * b : SLOTS * b + SLOTS], piece)
+        full_ref[SLOTS * yi : SLOTS * yi + SLOTS, :] = piece.astype(BF16)
 
     lanes = ZG * band_rows * channels
     spread = repeat_matrix(channels, lanes, BF16)
@@ -158,9 +143,10 @@
         ],
         axis=0,
     )
-    spread = repeat_matrix(channels, lanes, F32)
+    spread = repeat_matrix(channels, params_ref.shape[1], F32)
     table = jnp.dot(table, spread, precision=HI, preferred_element_type=F32)
-    params_ref[...] = table[:, :step]
+    params_ref[...] = table
+    table = table[:, :lanes]
 
     per_z = classes * band_rows
     shape = (ZG * per_z, lanes)
@@ -217,59 +203,89 @@
     corner_ref[...] = corners
 
 
-def tap_rows(start_z, gathered_ref, cells_ref, taps_ref, slab_rows, band_rows, spaces):
+def line_rows(start_z, gathered_ref, cells_ref, lines_ref, slab_rows, band_rows, spaces):
     block = slab_rows * band_rows
+    pitch = block + 1
     for device in range(gathered_ref.shape[0]):
-        cells_ref[device * block : (device + 1) * block, :] = gathered_ref[device].astype(F32)
-    rows = band_rows * spaces
+        cells_ref[device * pitch : device * pitch + block, :] = gathered_ref[device].astype(F32)
     lane = iota((spaces, PX), 1)
-    empty = jnp.zeros((rows, PX), F32)
-    for c in range(TAPS):
-        taps_ref[0, c * rows : (c + 1) * rows, :] = empty
-        at = (TAPS * (TAPS - 1) + c) * rows
-        taps_ref[PZ - 1, at : at + rows, :] = empty
-    ones = jnp.ones((16, PX), F32)
+    empty = jnp.zeros((spaces, PX), F32)
+    edge = jnp.zeros((LINE, PX), F32)
+    last = band_rows * (spaces + 2) * LINE
+    lines_ref[last : last + SLOTS, :] = edge[:SLOTS]
+    for y in range(band_rows):
+        base = y * (spaces + 2) * LINE
+        lines_ref[base : base + LINE, :] = edge
+        lines_ref[base + (spaces + 1) * LINE : base + (spaces + 2) * LINE, :] = edge
+        base = base + LINE
+        for k in (0, 1, 2, LINE - 4, LINE - 3, LINE - 2, LINE - 1):
+            lines_ref[pl.ds(base + k, spaces, stride=LINE), :] = empty
     for z in range(PZ):
-        taps_ref[z, TAPS * TAPS * rows :, :] = ones
         deep = start_z + z
         slab = lax.div(deep, slab_rows)
-        base = slab * (spaces * block) + (deep - slab * slab_rows) * band_rows
+        first = slab * (spaces * pitch) + (deep - slab * slab_rows) * band_rows
         for y in range(band_rows):
-            line = cells_ref[pl.ds(base + y, spaces, stride=block), :]
+            line = cells_ref[pl.ds(first + y, spaces, stride=pitch), :]
             before = jnp.where(lane == 0, 0.0, pltpu.roll(line, 1, 1))
             after = jnp.where(lane == PX - 1, 0.0, pltpu.roll(line, PX - 1, 1))
-            for a in range(TAPS):
-                at = z + 1 - a
-                if 0 <= at < PZ:
-                    for c, value in enumerate((before, line, after)):
-                        first = (a * TAPS + c) * rows + y * spaces
-                        taps_ref[at, first : first + spaces, :] = value
-
-
-def first_moments(taps_ref, every_ref, rows, step):
-    cells = [taps_ref[z].astype(BF16) for z in range(PZ)]
+            base = (y * (spaces + 2) + 1) * LINE + TAPS * (z + 1)
+            for c, value in enumerate((before, line, after)):
+                lines_ref[pl.ds(base + c, spaces, stride=LINE), :] = value
+
+
+def tree_sum(values):
+    values = list(values)
+    while len(values) > 1:
+        values = [
+            values[i] + values[i + 1] if i + 1 < len(values) else values[i]
+            for i in range(0, len(values), 2)
+        ]
+    return values[0]
+
+
+def first_moments(lines_ref, gram_ref, weights, band_rows, spaces):
+    rows = band_rows * spaces
+    cells = []
+    sums = [None] * rows
+    for z in range(PZ):
+        column = []
+        for y in range(rows):
+            at = (y % band_rows * (spaces + 2) + y // band_rows + 1) * LINE + TAPS * z
+            value = lines_ref[at : at + SLOTS, :]
+            sums[y] = value if sums[y] is None else sums[y] + value
+            column.append(value.astype(BF16))
+        cells.append(jnp.concatenate(column, axis=0))
     cells = jnp.concatenate(cells, axis=1)
-    gram = lax.dot_general(cells, cells, CONTRACT_LAST, preferred_element_type=F32)
-    high = gram.astype(BF16)
-    left = gram - high.astype(F32)
-    middle = left.astype(BF16)
-    low = (left - middle.astype(F32)).astype(BF16)
-    first = jnp.zeros((1, step), F32)
-    second = jnp.zeros((1, step), F32)
-    wide = 4 * step
-    for at in range(0, rows * step, wide):
-        weights = every_ref[:, at : at + wide]
-        product = (
-            jnp.dot(high, weights, preferred_element_type=F32)
-            + jnp.dot(middle, weights, preferred_element_type=F32)
-            + jnp.dot(low, weights, preferred_element_type=F32)
-        )
-        squares = jnp.sum(product * weights.astype(F32), axis=0, keepdims=True)
-        ones = TAPS * TAPS * rows
-        for lane in range(0, wide, step):
-            first = first + product[ones : ones + 1, lane : lane + step]
-            second = second + squares[:, lane : lane + step]
-    return first, second
+    gram_ref[...] = lax.dot_general(cells, cells, CONTRACT_LAST, preferred_element_type=F32)
+
+    def block(y, delta):
+        lane = SLOTS * (y + delta)
+        tile = lane // 128 * 128
+        value = gram_ref[SLOTS * y : SLOTS * y + SLOTS, tile : tile + 128]
+        return pltpu.roll(value, (tile + 128 - lane) % 128, 1) if lane != tile else value
+
+    def total(values):
+        return jnp.where(iota((SLOTS, 128), 1) < SLOTS, tree_sum(values), 0.0)
+
+    head, tail = total([block(0, 0)]), total([block(rows - 1, 0)])
+    near = total([block(y, 0) for y in range(rows)])
+    next1 = 2.0 * total([block(y, 1) for y in range(rows - 1)])
+    next2 = 2.0 * total([block(y, 2) for y in range(rows - 2)])
+    move = lambda value, k: pltpu.roll(value, SLOTS * k, 1)
+    form = jnp.concatenate(
+        [
+            near - tail + move(next1, 1) + move(next2, 2),
+            move(near, 1) + move(next1, 2),
+            move(near - head, 2),
+        ],
+        axis=0,
+    )[:, : TAPS * SLOTS]
+    product = jnp.dot(form, weights, precision=HI, preferred_element_type=F32)
+    squares = jnp.sum(product * weights, axis=0, keepdims=True)
+    every = tree_sum(sums)
+    column = jnp.concatenate([every - sums[rows - 1], every, every - sums[0]], axis=0)
+    column = jnp.sum(column, axis=1, keepdims=True)
+    return jnp.sum(column * weights, axis=0, keepdims=True), squares
 
 
 def spread_mirror(value, f, channels):
@@ -288,14 +304,15 @@
     channels,
     gathered_ref,
     corner_ref,
-    every_ref,
-    own_ref,
+    flat_ref,
+    full_ref,
     w2t_ref,
     params_ref,
     conv_ref,
     stats_ref,
     cells_ref,
-    taps_ref,
+    lines_ref,
+    gram_ref,
     wide_ref,
     sums_ref,
 ):
@@ -304,21 +321,18 @@
     step = hidden_rows * channels
     band = lax.axis_index("space")
     start_z = corner_ref[lax.axis_size("patch"), 0]
-    tap_rows(start_z, gathered_ref, cells_ref, taps_ref, slab_rows, band_rows, spaces)
-
-    first, second = first_moments(taps_ref, every_ref, rows, step)
+    line_rows(start_z, gathered_ref, cells_ref, lines_ref, slab_rows, band_rows, spaces)
+
+    first, second = first_moments(lines_ref, gram_ref, flat_ref[...], band_rows, spaces)
     count = float(PZ * rows * PX)
     mean = first / count
     variance = second / count - mean * mean
+    lane_row = iota(mean.shape, 1) // channels % hidden_rows
+    y = band * band_rows - 1 + lane_row
+    inside = (y >= 0) & (y < rows)
     scale = lax.rsqrt(variance + 1e-05) * params_ref[0:1]
-    shift = params_ref[1:2] - mean * scale
-    table = jnp.concatenate([scale, shift, jnp.zeros((6, step), F32)], axis=0)
-    y = band * band_rows - 1 + iota((8, step), 1) // channels
-    inside = (y >= 0) & (y < rows)
-    table = jnp.concatenate(
-        [jnp.where(inside, spread_mirror(table, f, channels), 0.0) for f in range(4)], axis=1
-    )
-    scale, shift = table[0:1], table[1:2]
+    shift = jnp.where(inside, params_ref[1:2] - mean * scale, 0.0)
+    scale = jnp.where(inside, scale, 0.0)
 
     out_lanes = conv_ref.shape[2]
     groups = PZ // ZG
@@ -327,9 +341,13 @@
         for g, j in ((0, 0), (groups - 1, ZI - 1)):
             at = (ZI - 1 - j if f % 2 else j) * step
             wide_ref[f, g * PX : (g + 1) * PX, at : at + step] = empty
-    weights = own_ref[...]
+    weights = full_ref[...]
     for z in range(PZ):
-        cells = taps_ref[z].astype(BF16)
+        cells = []
+        for yi in range(hidden_rows + TAPS - 1):
+            at = (yi % band_rows * (spaces + 2) + yi // band_rows + band) * LINE + TAPS * z
+            cells.append(lines_ref[pl.ds(at, SLOTS), :].astype(BF16))
+        cells = jnp.concatenate(cells, axis=0)
         value = lax.dot_general(cells, weights, CONTRACT_FIRST, preferred_element_type=F32)
         value = value * scale + shift
         value = jnp.maximum(value, 0.01 * value).astype(BF16)
@@ -381,8 +399,8 @@
         sums = sums + stats_ref[space]
     mean = sums[0:1] / count
     variance = sums[1:2] / count - mean * mean
-    scale = lax.rsqrt(variance + 1e-05) * params_ref[2:3]
-    shift = params_ref[3:4] - mean * scale
+    scale = lax.rsqrt(variance + 1e-05) * params_ref[2:3, : 4 * channels]
+    shift = params_ref[3:4, : 4 * channels] - mean * scale
     table = jnp.concatenate([scale, shift, jnp.zeros((6, 4 * channels), F32)], axis=0)
     groups = conv_ref.shape[1] // PX
     totals = [None] * groups
@@ -452,7 +470,6 @@
     step = 4 * channels
     lanes1 = 4 * hidden_rows * channels
     lanes2 = ZG * band_rows * channels
-    depth1 = TAPS * TAPS * rows + 16
     depth2 = ZI * hidden_rows * channels
     cells = PZ // ZG * PX
     per_z = classes * band_rows
@@ -468,13 +485,13 @@
     )(corners, image)
     gathered = lax.all_to_all(in_vmem(windows), ("patch", "space"), 0, 0, tiled=True)
 
-    every, own, w2t, params, heads, bias, weights, corner = pl.pallas_call(
+    flat, full, w2t, params, heads, bias, weights, corner = pl.pallas_call(
         functools.partial(prep_kernel, spaces, slab_rows, band_rows),
         out_shape=(
-            pltpu.VMEM((depth1, rows * step), BF16),
-            pltpu.VMEM((depth1, lanes1), BF16),
+            pltpu.VMEM((TAPS * SLOTS, lanes1), F32),
+            pltpu.VMEM(((hidden_rows + TAPS - 1) * SLOTS, lanes1), BF16),
             pltpu.VMEM((TAPS, depth2, lanes2), BF16),
-            pltpu.VMEM((8, step), F32),
+            pltpu.VMEM((8, lanes1), F32),
             pltpu.VMEM((2, ZG * per_z, lanes2), BF16),
             pltpu.VMEM((ZG * per_z, PX), F32),
             pltpu.VMEM((groups, slab_rows * per_z, width), F32),
@@ -482,7 +499,7 @@
         ),
         in_specs=[SMEM] + [VMEM] * 7 + [SMEM],
         out_specs=(VMEM,) * 8,
-        scratch_shapes=[pltpu.VMEM((TAPS * 16, step), F32)],
+        scratch_shapes=[pltpu.VMEM((TAPS * SLOTS, step), F32)],
         compiler_params=pltpu.CompilerParams(vmem_limit_bytes=16 << 20),
         name="prep",
     )(
@@ -497,8 +514,9 @@
         in_hbm(head_bias),
     )
     scratch = (
-        ((groups * spaces * block, PX), F32),
-        ((PZ, depth1, PX), F32),
+        ((groups * spaces * (block + 1), PX), F32),
+        ((band_rows * (spaces + 2) * LINE + SLOTS, PX), F32),
+        ((rows * SLOTS, rows * SLOTS), F32),
         ((4, cells, depth2), BF16),
         ((8, lanes2), F32),
     )
@@ -517,8 +535,8 @@
     )(
         in_vmem(gathered),
         in_vmem(corner),
-        in_vmem(every),
-        in_vmem(own),
+        in_vmem(flat),
+        in_vmem(full),
         in_vmem(w2t),
         in_vmem(params),
     )

time: 37.4 us -> 36.7 us (0.981)
  Pallas kernels: 10.3 us -> 9.45 us
    pallas_call x1, Pallas kernels: 5.54 us -> 4.88 us  [local(): pl.pallas_call(functools.partial(main_kernel, spaces, slab_rows, band_row...]
  transfers between devices with their start and end apart: 4 -> 4, of which waited for: 3 -> 3; matrix products, arithmetic and copies ran while one was open for 0% -> 0% of each run, Pallas kernels for 5% -> 4%
where the time goes in v4:
time: 36.7 us; the launch traced here: 36.4 us
  blocking collectives  9.53 us (26%)
  Pallas kernels  9.45 us (26%)
  starting transfers between devices  9.22 us (25%)
  waiting for transfers between devices  8.21 us (22%)
    all_to_all x1, blocking collectives, local(): stats = lax.all_to_all(stats, 'space', 0, 0, tiled=True)  9.53 us
    all_to_all x1, starting transfers between devices, local(): lax.all_to_all(in_vmem(windows), ('patch', 'space'), 0, 0, tiled=True)  7.33 us
    all_to_all x1, waiting for transfers between devices, local(): lax.all_to_all(in_vmem(windows), ('patch', 'space'), 0, 0, tiled=True)  6.16 us
    pallas_call x1, Pallas kernels, local(): pl.pallas_call(functools.partial(main_kernel, spaces, slab_rows, band_row...  4.88 us
    ppermute x3, waiting for transfers between devices, local(): lax.ppermute(averaged, 'patch', [(i, i ^ k) for i in range(groups)])  2.05 us
    ppermute x3, starting transfers between devices, local(): lax.ppermute(averaged, 'patch', [(i, i ^ k) for i in range(groups)])  1.9 us
    pallas_call x1, Pallas kernels, local(): pl.pallas_call(functools.partial(prep_kernel, spaces, slab_rows, band_row...  1.64 us
    pallas_call x1, Pallas kernels, local(): pl.pallas_call(cut_kernel, out_shape=pltpu.VMEM((groups * spaces, block,...  1.45 us
  transfers between devices with their start and end apart: 4, of which 3 were waited for; matrix products, arithmetic and copies ran while one was open for 0% of the time, Pallas kernels for 4%

profile of v4, /device:TPU:0, one launch (start us, length us, event | category | flops | bytes accessed | tf_op | source)
XLA Modules:
  0.0 36.4 jit_solution(14637657691765416186)
XLA Ops:
  0.0 1.4 %cut.1 = bf16[32,16,128]{2,1,0:T(8,128)(2,1)} custom-call(s32[2,4]{1,0:T(2,128)} %bitcast.7, bf16[8,2,256]{2,1,0:T(2,128)(2,1)} %image_ref.1), custom_call_target="tpu_custom_call" | custom-call | tf_op jit(solution)/shard_map/cut/pallas_call | solution.py:478
  1.4 7.3 %all-to-all-start = ((bf16[32,16,128]{2,1,0:T(8,128)(2,1)}), bf16[32,16,128]{2,1,0:T(8,128)(2,1)S(1)}, u32[]{:S(2)}, u32[]{:S(2)}) async-start(bf16[32,16,128]{2,1,0:T(8,128)(2,1)} %cut.1), calls=%async_computation | async-start | bytes 262144 | tf_op jit(solution)/shard_map/all_to_all | solution.py:486
  8.8 1.6 %prep.1 = (f32[48,512]{1,0:T(8,128)S(1)}, bf16[96,512]{1,0:T(8,128)(2,1)S(1)}, bf16[3,768,256]{2,1,0:T(8,128)(2,1)S(1)}, f32[8,512]{1,0:T(8,128)S(1)}, bf16[2,24...) custom-call(s32[2,4]{1,0:T(2,128)} %bitcast.8, ...), custom_call_target="tpu_custom_call" | custom-call | tf_op jit(solution)/shard_map/prep/pallas_call | solution.py:488
  10.4 6.2 %all-to-all-done.gathered_ref = bf16[32,16,128]{2,1,0:T(8,128)(2,1)S(1)} async-done(((bf16[32,16,128]{2,1,0:T(8,128)(2,1)}), bf16[32,16,128]{2,1,0:T(8,128)(2,1)S(1)}, u32[]{:S(2)}, u32[]{:S(2)}) %all-to-all-start) | async-done | bytes 131104 | tf_op jit(solution)/shard_map/all_to_all | solution.py:486
  16.6 4.9 %main.1 = (f32[4,512,256]{2,1,0:T(8,128)S(1)}, f32[8,2,128]{2,1,0:T(2,128)S(1)}) custom-call(bf16[32,16,128]{2,1,0:T(8,128)(2,1)S(1)} %all-to-all-done.gathered_ref, s32[8,128]{1,0:T(8,128)S(1)} %get-tuple-element.15.corner_ref, f32[48,512]{1,0:T(8,128)S(1)} %get-tuple-element.17.flat_ref, bf16[96,512]{1,0:T(8,128)(2,1)S(1)} %get-tuple-element.18.full_ref, ...), custom_call_target="tpu_custom_call" | custom-call | tf_op jit(solution)/shard_map/main/pallas_call | solution.py:524
  21.5 9.5 %all_to_all.10.stats_ref = f32[8,2,128]{2,1,0:T(2,128)S(1)} all-to-all(f32[8,2,128]{2,1,0:T(2,128)S(1)} %get-tuple-element.22), channel_id=1, replica_groups=mesh['patch'=4,'space'=8] {'space'}, dimensions={0} | all-to-all | bytes 16384 | tf_op jit(solution)/shard_map/all_to_all | solution.py:543
  31.0 0.6 %head.1.refs_0_ = bf16[96,128]{1,0:T(8,128)(2,1)S(1)} custom-call(f32[4,512,256]{2,1,0:T(8,128)S(1)} %get-tuple-element.21.conv_ref, f32[8,2,128]{2,1,0:T(2,128)S(1)} %all_to_all.10.stats_ref, f32[8,512]{1,0:T(8,128)S(1)} %get-tuple-element.20.params_ref, bf16[2,24,256]{2,1,0:T(8,128)(2,1)S(1)} %get-tuple-element.23.heads_ref, ...), custom_call_target="tpu_custom_call" | custom-call | tf_op jit(solution)/shard_map/head/pallas_call | solution.py:544
  31.6 0.0 collective-permute-start.2
  31.7 0.7 %collective-permute-start.1 = (bf16[96,128]{1,0:T(8,128)(2,1)S(1)}, bf16[96,128]{1,0:T(8,128)(2,1)S(1)}, u32[]{:S(2)}, u32[]{:S(2)}) collective-permute-start(bf16[96,128]{1,0:T(8,128)(2,1)S(1)} %head.1.refs_0_), channel_id=1, source_target_pairs={{0,16},{8,24},{16,0},{24,8},{1,17},{9,25},{17,1},{25,9},{2,18},{10... | collective-permute-start | bytes 73736 | tf_op jit(solution)/shard_map/ppermute | solution.py:553
  32.4 1.2 %collective-permute-start = (bf16[96,128]{1,0:T(8,128)(2,1)S(1)}, bf16[96,128]{1,0:T(8,128)(2,1)S(1)}, u32[]{:S(2)}, u32[]{:S(2)}) collective-permute-start(bf16[96,128]{1,0:T(8,128)(2,1)S(1)} %head.1.refs_0_), channel_id=1, source_target_pairs={{0,8},{8,0},{16,24},{24,16},{1,9},{9,1},{17,25},{25,17},{2,10},{10... | collective-permute-start | bytes 73736 | tf_op jit(solution)/shard_map/ppermute | solution.py:553
  33.6 1.4 %collective-permute-done.2.refs_3_ = bf16[96,128]{1,0:T(8,128)(2,1)S(1)} collective-permute-done((bf16[96,128]{1,0:T(8,128)(2,1)S(1)}, bf16[96,128]{1,0:T(8,128)(2,1)S(1)}, u32[]{:S(2)}, u32[]{:S(2)}) %collective-permute-start.2) | collective-permute-done | bytes 24608 | tf_op jit(solution)/shard_map/ppermute | solution.py:553
  34.9 0.7 %collective-permute-done.1.refs_2_ = bf16[96,128]{1,0:T(8,128)(2,1)S(1)} collective-permute-done((bf16[96,128]{1,0:T(8,128)(2,1)S(1)}, bf16[96,128]{1,0:T(8,128)(2,1)S(1)}, u32[]{:S(2)}, u32[]{:S(2)}) %collective-permute-start.1) | collective-permute-done | bytes 24608 | tf_op jit(solution)/shard_map/ppermute | solution.py:553
  35.6 0.0 collective-permute-done.refs_1_
  35.6 0.8 %place.1 = f32[8,3,2,256]{3,2,1,0:T(2,128)} custom-call(s32[8,128]{1,0:T(8,128)S(1)} %get-tuple-element.15.corner_ref, f32[4,48,256]{2,1,0:T(8,128)S(1)} %get-tuple-element.16.weights_ref, bf16[96,128]{1,0:T(8,128)(2,1)S(1)} %head.1.refs_0_, bf16[96,128]{1,0:T(8,128)(2,1)S(1)} %collective-permute-done.refs_1_, ...), custom_call_target="tpu_custom_call" | custom-call | tf_op jit(solution)/shard_map/place/pallas_call | solution.py:556
Async XLA Ops:
  1.4 15.1 %all-to-all-start = ((bf16[32,16,128]{2,1,0:T(8,128)(2,1)}), bf16[32,16,128]{2,1,0:T(8,128)(2,1)S(1)}, u32[]{:S(2)}, u32[]{:S(2)}) async-start(bf16[32,16,128]{2,1,0:T(8,128)(2,1)} %cut.1), calls=%async_computation | async-start | bytes 262144 | tf_op jit(solution)/shard_map/all_to_all | solution.py:486
  31.6 3.3 %collective-permute-start.2 = (bf16[96,128]{1,0:T(8,128)(2,1)S(1)}, bf16[96,128]{1,0:T(8,128)(2,1)S(1)}, u32[]{:S(2)}, u32[]{:S(2)}) collective-permute-start(bf16[96,128]{1,0:T(8,128)(2,1)S(1)} %head.1.refs_0_), channel_id=1, source_target_pairs={{0,24},{8,16},{16,8},{24,0},{1,25},{9,17},{17,9},{25,1},{2,26},{10... | collective-permute-start | bytes 73736 | tf_op jit(solution)/shard_map/ppermute | solution.py:553
  31.7 3.9 %collective-permute-start.1 = (bf16[96,128]{1,0:T(8,128)(2,1)S(1)}, bf16[96,128]{1,0:T(8,128)(2,1)S(1)}, u32[]{:S(2)}, u32[]{:S(2)}) collective-permute-start(bf16[96,128]{1,0:T(8,128)(2,1)S(1)} %head.1.refs_0_), channel_id=1, source_target_pairs={{0,16},{8,24},{16,0},{24,8},{1,17},{9,25},{17,1},{25,9},{2,18},{10... | collective-permute-start | bytes 73736 | tf_op jit(solution)/shard_map/ppermute | solution.py:553
  32.4 3.2 %collective-permute-start = (bf16[96,128]{1,0:T(8,128)(2,1)S(1)}, bf16[96,128]{1,0:T(8,128)(2,1)S(1)}, u32[]{:S(2)}, u32[]{:S(2)}) collective-permute-start(bf16[96,128]{1,0:T(8,128)(2,1)S(1)} %head.1.refs_0_), channel_id=1, source_target_pairs={{0,8},{8,0},{16,24},{24,16},{1,9},{9,1},{17,25},{25,17},{2,10},{10... | collective-permute-start | bytes 73736 | tf_op jit(solution)/shard_map/ppermute | solution.py:553

commit v5 on v4

--- a/solution.py
+++ b/solution.py
@@ -63,6 +63,7 @@
     flat_ref,
     full_ref,
     wide_ref,
+    pair_ref,
     params_ref,
     heads_ref,
     bias_ref,
@@ -118,19 +119,30 @@
         lax.dot_general(w2_ref[t], spread, CONTRACT_FIRST, preferred_element_type=F32)
         for t in range(TAPS * TAPS)
     ]
-    group = iota((TAPS * channels, lanes), 1) // channels
+    half = lanes // 2
+    group = iota((channels, lanes), 1) // channels
+    outer = TAPS - 1
     for zi in range(ZI):
         for yi in range(hidden_rows):
-            piece = jnp.zeros((TAPS * channels, lanes), F32)
+            at = (zi * hidden_rows + yi) * channels
+            piece = jnp.zeros((channels, lanes), F32)
+            pair = jnp.zeros((channels, lanes), F32)
             for zo in range(ZG):
                 for yo in range(band_rows):
                     a, b = zi - zo, yi - yo
                     if 0 <= a < TAPS and 0 <= b < TAPS:
-                        piece = jnp.where(group == zo * band_rows + yo, taps[a * TAPS + b], piece)
-            piece = piece.astype(BF16)
-            at = (zi * hidden_rows + yi) * channels
-            for c in range(TAPS):
-                wide_ref[c, at : at + channels, :] = piece[c * channels : (c + 1) * channels]
+                        to = zo * band_rows + yo
+                        tap = taps[a * TAPS + b]
+                        piece = jnp.where(group == to, tap[outer * channels :], piece)
+                        if zo < ZG // 2:
+                            pair = jnp.where(group == to, tap[:channels], pair)
+                            to = to + half // channels
+                            pair = jnp.where(
+                                group == to, tap[channels : 2 * channels], pair
+                            )
+            wide_ref[at : at + channels, :] = piece.astype(BF16)
+            if zi < ZI - ZG // 2:
+                pair_ref[at : at + channels, :] = pair.astype(BF16)
 
     table = jnp.concatenate(
         [
@@ -245,32 +257,48 @@
 
 def first_moments(lines_ref, gram_ref, weights, band_rows, spaces):
     rows = band_rows * spaces
+    chunks = gram_ref.shape[0]
+    size = rows // chunks
+    ahead = TAPS - 1
     cells = []
     sums = [None] * rows
-    for z in range(PZ):
-        column = []
-        for y in range(rows):
+    for y in range(rows + ahead):
+        line = []
+        for z in range(PZ):
             at = (y % band_rows * (spaces + 2) + y // band_rows + 1) * LINE + TAPS * z
             value = lines_ref[at : at + SLOTS, :]
-            sums[y] = value if sums[y] is None else sums[y] + value
-            column.append(value.astype(BF16))
-        cells.append(jnp.concatenate(column, axis=0))
-    cells = jnp.concatenate(cells, axis=1)
-    gram_ref[...] = lax.dot_general(cells, cells, CONTRACT_LAST, preferred_element_type=F32)
-
-    def block(y, delta):
+            line.append(value.astype(BF16))
+            if y < rows:
+                sums[y] = value if sums[y] is None else sums[y] + value
+        cells.append(jnp.concatenate(line, axis=1))
+    for chunk in range(chunks):
+        left = jnp.concatenate(cells[chunk * size : (chunk + 1) * size], axis=0)
+        right = jnp.concatenate(cells[chunk * size : (chunk + 1) * size + ahead], axis=0)
+        gram_ref[chunk] = lax.dot_general(
+            left, right, CONTRACT_LAST, preferred_element_type=F32
+        )
+
+    def block(y, delta, chosen):
         lane = SLOTS * (y + delta)
         tile = lane // 128 * 128
-        value = gram_ref[SLOTS * y : SLOTS * y + SLOTS, tile : tile + 128]
+        end = min(tile + 128, gram_ref.shape[2])
+        value = tree_sum(
+            [gram_ref[chunk, SLOTS * y : SLOTS * (y + 1), tile:end] for chunk in chosen]
+        )
+        if end < tile + 128:
+            value = jnp.concatenate(
+                [value, jnp.zeros((SLOTS, tile + 128 - end), F32)], axis=1
+            )
         return pltpu.roll(value, (tile + 128 - lane) % 128, 1) if lane != tile else value
 
     def total(values):
         return jnp.where(iota((SLOTS, 128), 1) < SLOTS, tree_sum(values), 0.0)
 
-    head, tail = total([block(0, 0)]), total([block(rows - 1, 0)])
-    near = total([block(y, 0) for y in range(rows)])
-    next1 = 2.0 * total([block(y, 1) for y in range(rows - 1)])
-    next2 = 2.0 * total([block(y, 2) for y in range(rows - 2)])
+    every = range(chunks)
+    head, tail = total([block(0, 0, [0])]), total([block(size - 1, 0, [chunks - 1])])
+    near = total([block(y, 0, every) for y in range(size)])
+    next1 = 2.0 * total([block(y, 1, every) for y in range(size)])
+    next2 = 2.0 * total([block(y, 2, every) for y in range(size)])
     move = lambda value, k: pltpu.roll(value, SLOTS * k, 1)
     form = jnp.concatenate(
         [
@@ -280,7 +308,17 @@
         ],
         axis=0,
     )[:, : TAPS * SLOTS]
-    product = jnp.dot(form, weights, precision=HI, preferred_element_type=F32)
+    high = form.astype(BF16)
+    left = form - high.astype(F32)
+    middle = left.astype(BF16)
+    low = (left - middle.astype(F32)).astype(BF16)
+    product = jnp.dot(
+        jnp.concatenate([high, middle, low], axis=0),
+        weights.astype(BF16),
+        preferred_element_type=F32,
+    )
+    size = TAPS * SLOTS
+    product = product[:size] + (product[size : 2 * size] + product[2 * size :])
     squares = jnp.sum(product * weights, axis=0, keepdims=True)
     every = tree_sum(sums)
     column = jnp.concatenate([every - sums[rows - 1], every, every - sums[0]], axis=0)
@@ -307,6 +345,7 @@
     flat_ref,
     full_ref,
     w2t_ref,
+    w2p_ref,
     params_ref,
     conv_ref,
     stats_ref,
@@ -314,7 +353,6 @@
     lines_ref,
     gram_ref,
     wide_ref,
-    sums_ref,
 ):
     rows = band_rows * spaces
     hidden_rows = band_rows + TAPS - 1
@@ -335,47 +373,74 @@
     scale = jnp.where(inside, scale, 0.0)
 
     out_lanes = conv_ref.shape[2]
+    half = out_lanes // 2
     groups = PZ // ZG
     empty = jnp.zeros((PX, step), BF16)
     for f in range(4):
         for g, j in ((0, 0), (groups - 1, ZI - 1)):
             at = (ZI - 1 - j if f % 2 else j) * step
-            wide_ref[f, g * PX : (g + 1) * PX, at : at + step] = empty
+            wide_ref[g, f * PX : (f + 1) * PX, at : at + step] = empty
     weights = full_ref[...]
-    for z in range(PZ):
+
+    def hidden(cells_z):
         cells = []
         for yi in range(hidden_rows + TAPS - 1):
-            at = (yi % band_rows * (spaces + 2) + yi // band_rows + band) * LINE + TAPS * z
-            cells.append(lines_ref[pl.ds(at, SLOTS), :].astype(BF16))
+            base = (yi % band_rows * (spaces + 2) + yi // band_rows + band) * LINE
+            line = [
+                lines_ref[pl.ds(base + TAPS * z, SLOTS), :].astype(BF16) for z in cells_z
+            ]
+            cells.append(jnp.concatenate(line, axis=1))
         cells = jnp.concatenate(cells, axis=0)
-        value = lax.dot_general(cells, weights, CONTRACT_FIRST, preferred_element_type=F32)
-        value = value * scale + shift
-        value = jnp.maximum(value, 0.01 * value).astype(BF16)
-        for g in range(groups):
-            j = z + 1 - ZG * g
-            if 0 <= j < ZI:
-                for f in range(4):
-                    at = (ZI - 1 - j if f % 2 else j) * step
-                    wide_ref[f, g * PX : (g + 1) * PX, at : at + step] = value[
-                        :, f * step : (f + 1) * step
-                    ]
-
-    x = iota((groups * PX, out_lanes), 0) % PX
-    for f in range(4):
-        cells = wide_ref[f]
-        parts = [
-            jnp.dot(cells, w2t_ref[c], preferred_element_type=F32) for c in range(TAPS)
+        values = lax.dot_general(cells, weights, CONTRACT_FIRST, preferred_element_type=F32)
+        for k, z in enumerate(cells_z):
+            value = values[k * PX : (k + 1) * PX] * scale + shift
+            value = jnp.maximum(value, 0.01 * value).astype(BF16)
+            for g in range(groups):
+                j = z + 1 - ZG * g
+                if 0 <= j < ZI:
+                    for f in range(4):
+                        at = (ZI - 1 - j if f % 2 else j) * step
+                        wide_ref[g, f * PX : (f + 1) * PX, at : at + step] = value[
+                            :, f * step : (f + 1) * step
+                        ]
+
+    x = iota((2 * PX, out_lanes), 0) % PX
+    totals = [[None] * 4, [None] * 4]
+    done = 0
+    for g in range(groups):
+        upto = min(ZG * g + ZG + 1, PZ)
+        hidden(range(done, upto))
+        done = upto
+        cells = wide_ref[g]
+        last = jnp.dot(cells, w2t_ref[...], preferred_element_type=F32)
+        pairs = [
+            jnp.dot(
+                cells[:, at : at + w2p_ref.shape[0]], w2p_ref[...], preferred_element_type=F32
+            )
+            for at in (0, ZG // 2 * step)
         ]
-        before, after = (parts[2], parts[0]) if f >= 2 else (parts[0], parts[2])
-        value = (
-            parts[1]
-            + jnp.where(x == 0, 0.0, pltpu.roll(before, 1, 0))
-            + jnp.where(x == PX - 1, 0.0, pltpu.roll(after, groups * PX - 1, 0))
+        first, middle = (
+            jnp.concatenate([pair[:, at : at + half] for pair in pairs], axis=1)
+            for at in (0, half)
         )
-        conv_ref[f] = value
-        sums_ref[f : f + 1, :] = jnp.sum(value, axis=0, keepdims=True)
-        sums_ref[f + 4 : f + 5, :] = jnp.sum(value * value, axis=0, keepdims=True)
-    sums = sums_ref[...]
+        for flip in range(2):
+            at = flip * 2 * PX
+            before, after = (last, first) if flip else (first, last)
+            value = (
+                middle[at : at + 2 * PX]
+                + jnp.where(x == 0, 0.0, pltpu.roll(before[at : at + 2 * PX], 1, 0))
+                + jnp.where(
+                    x == PX - 1, 0.0, pltpu.roll(after[at : at + 2 * PX], 2 * PX - 1, 0)
+                )
+            )
+            conv_ref[g, at : at + 2 * PX, :] = value
+            for f in (2 * flip, 2 * flip + 1):
+                part = value[f * PX - at : (f + 1) * PX - at]
+                for kind, item in enumerate((part, part * part)):
+                    item = jnp.sum(item, axis=0, keepdims=True)
+                    old = totals[kind][f]
+                    totals[kind][f] = item if old is None else old + item
+    sums = jnp.concatenate(totals[0] + totals[1], axis=0)
     lanes = 4 * channels
     sums = sum(sums[:, at : at + lanes] for at in range(0, out_lanes, lanes))
     reach = lanes // 2
@@ -402,13 +467,13 @@
     scale = lax.rsqrt(variance + 1e-05) * params_ref[2:3, : 4 * channels]
     shift = params_ref[3:4, : 4 * channels] - mean * scale
     table = jnp.concatenate([scale, shift, jnp.zeros((6, 4 * channels), F32)], axis=0)
-    groups = conv_ref.shape[1] // PX
+    groups = conv_ref.shape[0]
     totals = [None] * groups
     for f in range(4):
         own = spread_mirror(table, f, channels)
         own = jnp.concatenate([own] * (lanes // own.shape[1]), axis=1)
         for g in range(groups):
-            value = conv_ref[f, g * PX : (g + 1) * PX, :] * own[0:1] + own[1:2]
+            value = conv_ref[g, f * PX : (f + 1) * PX, :] * own[0:1] + own[1:2]
             value = jnp.maximum(value, 0.01 * value).astype(BF16)
             logits = lax.dot_general(
                 heads_ref[f % 2], value, CONTRACT_LAST, preferred_element_type=F32
@@ -471,7 +536,7 @@
     lanes1 = 4 * hidden_rows * channels
     lanes2 = ZG * band_rows * channels
     depth2 = ZI * hidden_rows * channels
-    cells = PZ // ZG * PX
+    depth3 = (ZI - ZG // 2) * hidden_rows * channels
     per_z = classes * band_rows
     corners = in_hbm(offsets.T)
 
@@ -485,12 +550,13 @@
     )(corners, image)
     gathered = lax.all_to_all(in_vmem(windows), ("patch", "space"), 0, 0, tiled=True)
 
-    flat, full, w2t, params, heads, bias, weights, corner = pl.pallas_call(
+    flat, full, w2t, w2p, params, heads, bias, weights, corner = pl.pallas_call(
         functools.partial(prep_kernel, spaces, slab_rows, band_rows),
         out_shape=(
             pltpu.VMEM((TAPS * SLOTS, lanes1), F32),
             pltpu.VMEM(((hidden_rows + TAPS - 1) * SLOTS, lanes1), BF16),
-            pltpu.VMEM((TAPS, depth2, lanes2), BF16),
+            pltpu.VMEM((depth2, lanes2), BF16),
+            pltpu.VMEM((depth3, lanes2), BF16),
             pltpu.VMEM((8, lanes1), F32),
             pltpu.VMEM((2, ZG * per_z, lanes2), BF16),
             pltpu.VMEM((ZG * per_z, PX), F32),
@@ -498,7 +564,7 @@
             pltpu.VMEM(((groups + 8) // 8 * 8, 128), jnp.int32),
         ),
         in_specs=[SMEM] + [VMEM] * 7 + [SMEM],
-        out_specs=(VMEM,) * 8,
+        out_specs=(VMEM,) * 9,
         scratch_shapes=[pltpu.VMEM((TAPS * SLOTS, step), F32)],
         compiler_params=pltpu.CompilerParams(vmem_limit_bytes=16 << 20),
         name="prep",
@@ -513,21 +579,21 @@
         in_hbm(head_weight),
         in_hbm(head_bias),
     )
+    chunks = max(rows // 8, 1)
     scratch = (
         ((groups * spaces * (block + 1), PX), F32),
         ((band_rows * (spaces + 2) * LINE + SLOTS, PX), F32),
-        ((rows * SLOTS, rows * SLOTS), F32),
-        ((4, cells, depth2), BF16),
-        ((8, lanes2), F32),
+        ((chunks, rows // chunks * SLOTS, (rows // chunks + TAPS - 1) * SLOTS), F32),
+        ((PZ // ZG, 4 * PX, depth2), BF16),
     )
     size = sum(math.prod(shape) * jnp.dtype(kind).itemsize for shape, kind in scratch)
     conv, stats = pl.pallas_call(
         functools.partial(main_kernel, spaces, slab_rows, band_rows, channels),
         out_shape=(
-            pltpu.VMEM((4, cells, lanes2), F32),
+            pltpu.VMEM((PZ // ZG, 4 * PX, lanes2), F32),
             pltpu.VMEM((spaces, 2, step), F32),
         ),
-        in_specs=[VMEM] * 6,
+        in_specs=[VMEM] * 7,
         out_specs=(VMEM, VMEM),
         scratch_shapes=[pltpu.VMEM(shape, kind) for shape, kind in scratch],
         compiler_params=pltpu.CompilerParams(vmem_limit_bytes=min(2 * size + (16 << 20), 40 << 20)),
@@ -538,6 +604,7 @@
         in_vmem(flat),
         in_vmem(full),
         in_vmem(w2t),
+        in_vmem(w2p),
         in_vmem(params),
     )
     stats = lax.all_to_all(stats, "space", 0, 0, tiled=True)

time: 36.7 us -> 35.9 us (0.978)
  Pallas kernels: 9.45 us -> 8.55 us
    pallas_call x1, Pallas kernels: 4.88 us -> 4.08 us  [local(): pl.pallas_call(functools.partial(main_kernel, spaces, slab_rows, band_row...]
where the time goes in v5:
time: 35.9 us; the launch traced here: 35.6 us
  blocking collectives  9.53 us (27%)
  starting transfers between devices  9.22 us (26%)
  Pallas kernels  8.55 us (24%)
  waiting for transfers between devices  8.31 us (23%)
    all_to_all x1, blocking collectives, local(): stats = lax.all_to_all(stats, 'space', 0, 0, tiled=True)  9.53 us
    all_to_all x1, starting transfers between devices, local(): lax.all_to_all(in_vmem(windows), ('patch', 'space'), 0, 0, tiled=True)  7.33 us
    all_to_all x1, waiting for transfers between devices, local(): lax.all_to_all(in_vmem(windows), ('patch', 'space'), 0, 0, tiled=True)  6.26 us
    pallas_call x1, Pallas kernels, local(): pl.pallas_call(functools.partial(main_kernel, spaces, slab_rows, band_row...  4.08 us
    ppermute x3, waiting for transfers between devices, local(): lax.ppermute(averaged, 'patch', [(i, i ^ k) for i in range(groups)])  2.05 us
    ppermute x3, starting transfers between devices, local(): lax.ppermute(averaged, 'patch', [(i, i ^ k) for i in range(groups)])  1.9 us
    pallas_call x1, Pallas kernels, local(): pl.pallas_call(functools.partial(prep_kernel, spaces, slab_rows, band_row...  1.54 us
    pallas_call x1, Pallas kernels, local(): pl.pallas_call(cut_kernel, out_shape=pltpu.VMEM((groups * spaces, block,...  1.45 us
  transfers between devices with their start and end apart: 4, of which 3 were waited for; matrix products, arithmetic and copies ran while one was open for 0% of the time, Pallas kernels for 4%

profile of v5, /device:TPU:0, one launch (start us, length us, event | category | flops | bytes accessed | tf_op | source)
XLA Modules:
  0.0 35.6 jit_solution(8000716760146786687)
XLA Ops:
  0.0 1.4 %cut.1 = bf16[32,16,128]{2,1,0:T(8,128)(2,1)} custom-call(s32[2,4]{1,0:T(2,128)} %bitcast.7, bf16[8,2,256]{2,1,0:T(2,128)(2,1)} %image_ref.1), custom_call_target="tpu_custom_call" | custom-call | tf_op jit(solution)/shard_map/cut/pallas_call | solution.py:543
  1.4 7.3 %all-to-all-start = ((bf16[32,16,128]{2,1,0:T(8,128)(2,1)}), bf16[32,16,128]{2,1,0:T(8,128)(2,1)S(1)}, u32[]{:S(2)}, u32[]{:S(2)}) async-start(bf16[32,16,128]{2,1,0:T(8,128)(2,1)} %cut.1), calls=%async_computation | async-start | bytes 262144 | tf_op jit(solution)/shard_map/all_to_all | solution.py:551
  8.8 1.5 %prep.1 = (f32[48,512]{1,0:T(8,128)S(1)}, bf16[96,512]{1,0:T(8,128)(2,1)S(1)}, bf16[768,256]{1,0:T(8,128)(2,1)S(1)}, bf16[512,256]{1,0:T(8,128)(2,1)S(1)}, f32[8...) custom-call(s32[2,4]{1,0:T(2,128)} %bitcast.8, ...), custom_call_target="tpu_custom_call" | custom-call | tf_op jit(solution)/shard_map/prep/pallas_call | solution.py:553
  10.3 6.3 %all-to-all-done.gathered_ref = bf16[32,16,128]{2,1,0:T(8,128)(2,1)S(1)} async-done(((bf16[32,16,128]{2,1,0:T(8,128)(2,1)}), bf16[32,16,128]{2,1,0:T(8,128)(2,1)S(1)}, u32[]{:S(2)}, u32[]{:S(2)}) %all-to-all-start) | async-done | bytes 131104 | tf_op jit(solution)/shard_map/all_to_all | solution.py:551
  16.6 4.1 %main.1 = (f32[4,512,256]{2,1,0:T(8,128)S(1)}, f32[8,2,128]{2,1,0:T(2,128)S(1)}) custom-call(bf16[32,16,128]{2,1,0:T(8,128)(2,1)S(1)} %all-to-all-done.gathered_ref, s32[8,128]{1,0:T(8,128)S(1)} %get-tuple-element.16.corner_ref, f32[48,512]{1,0:T(8,128)S(1)} %get-tuple-element.18.flat_ref, bf16[96,512]{1,0:T(8,128)(2,1)S(1)} %get-tuple-element.19.full_ref, ...), custom_call_target="tpu_custom_call" | custom-call | tf_op jit(solution)/shard_map/main/pallas_call | solution.py:590
  20.7 9.5 %all_to_all.10.stats_ref = f32[8,2,128]{2,1,0:T(2,128)S(1)} all-to-all(f32[8,2,128]{2,1,0:T(2,128)S(1)} %get-tuple-element.24), channel_id=1, replica_groups=mesh['patch'=4,'space'=8] {'space'}, dimensions={0} | all-to-all | bytes 16384 | tf_op jit(solution)/shard_map/all_to_all | solution.py:610
  30.2 0.6 %head.1.refs_0_ = bf16[96,128]{1,0:T(8,128)(2,1)S(1)} custom-call(f32[4,512,256]{2,1,0:T(8,128)S(1)} %get-tuple-element.23.conv_ref, f32[8,2,128]{2,1,0:T(2,128)S(1)} %all_to_all.10.stats_ref, f32[8,512]{1,0:T(8,128)S(1)} %get-tuple-element.22.params_ref, bf16[2,24,256]{2,1,0:T(8,128)(2,1)S(1)} %get-tuple-element.25.heads_ref, ...), custom_call_target="tpu_custom_call" | custom-call | tf_op jit(solution)/shard_map/head/pallas_call | solution.py:611
  30.8 0.0 collective-permute-start.2
  30.9 0.7 %collective-permute-start.1 = (bf16[96,128]{1,0:T(8,128)(2,1)S(1)}, bf16[96,128]{1,0:T(8,128)(2,1)S(1)}, u32[]{:S(2)}, u32[]{:S(2)}) collective-permute-start(bf16[96,128]{1,0:T(8,128)(2,1)S(1)} %head.1.refs_0_), channel_id=1, source_target_pairs={{0,16},{8,24},{16,0},{24,8},{1,17},{9,25},{17,1},{25,9},{2,18},{10... | collective-permute-start | bytes 73736 | tf_op jit(solution)/shard_map/ppermute | solution.py:620
  31.6 1.2 %collective-permute-start = (bf16[96,128]{1,0:T(8,128)(2,1)S(1)}, bf16[96,128]{1,0:T(8,128)(2,1)S(1)}, u32[]{:S(2)}, u32[]{:S(2)}) collective-permute-start(bf16[96,128]{1,0:T(8,128)(2,1)S(1)} %head.1.refs_0_), channel_id=1, source_target_pairs={{0,8},{8,0},{16,24},{24,16},{1,9},{9,1},{17,25},{25,17},{2,10},{10... | collective-permute-start | bytes 73736 | tf_op jit(solution)/shard_map/ppermute | solution.py:620
  32.8 1.4 %collective-permute-done.2.refs_3_ = bf16[96,128]{1,0:T(8,128)(2,1)S(1)} collective-permute-done((bf16[96,128]{1,0:T(8,128)(2,1)S(1)}, bf16[96,128]{1,0:T(8,128)(2,1)S(1)}, u32[]{:S(2)}, u32[]{:S(2)}) %collective-permute-start.2) | collective-permute-done | bytes 24608 | tf_op jit(solution)/shard_map/ppermute | solution.py:620
  34.1 0.7 %collective-permute-done.1.refs_2_ = bf16[96,128]{1,0:T(8,128)(2,1)S(1)} collective-permute-done((bf16[96,128]{1,0:T(8,128)(2,1)S(1)}, bf16[96,128]{1,0:T(8,128)(2,1)S(1)}, u32[]{:S(2)}, u32[]{:S(2)}) %collective-permute-start.1) | collective-permute-done | bytes 24608 | tf_op jit(solution)/shard_map/ppermute | solution.py:620
  34.8 0.0 collective-permute-done.refs_1_
  34.8 0.8 %place.1 = f32[8,3,2,256]{3,2,1,0:T(2,128)} custom-call(s32[8,128]{1,0:T(8,128)S(1)} %get-tuple-element.16.corner_ref, f32[4,48,256]{2,1,0:T(8,128)S(1)} %get-tuple-element.17.weights_ref, bf16[96,128]{1,0:T(8,128)(2,1)S(1)} %head.1.refs_0_, bf16[96,128]{1,0:T(8,128)(2,1)S(1)} %collective-permute-done.refs_1_, ...), custom_call_target="tpu_custom_call" | custom-call | tf_op jit(solution)/shard_map/place/pallas_call | solution.py:623
Async XLA Ops:
  1.4 15.1 %all-to-all-start = ((bf16[32,16,128]{2,1,0:T(8,128)(2,1)}), bf16[32,16,128]{2,1,0:T(8,128)(2,1)S(1)}, u32[]{:S(2)}, u32[]{:S(2)}) async-start(bf16[32,16,128]{2,1,0:T(8,128)(2,1)} %cut.1), calls=%async_computation | async-start | bytes 262144 | tf_op jit(solution)/shard_map/all_to_all | solution.py:551
  30.8 3.3 %collective-permute-start.2 = (bf16[96,128]{1,0:T(8,128)(2,1)S(1)}, bf16[96,128]{1,0:T(8,128)(2,1)S(1)}, u32[]{:S(2)}, u32[]{:S(2)}) collective-permute-start(bf16[96,128]{1,0:T(8,128)(2,1)S(1)} %head.1.refs_0_), channel_id=1, source_target_pairs={{0,24},{8,16},{16,8},{24,0},{1,25},{9,17},{17,9},{25,1},{2,26},{10... | collective-permute-start | bytes 73736 | tf_op jit(solution)/shard_map/ppermute | solution.py:620
  30.9 3.9 %collective-permute-start.1 = (bf16[96,128]{1,0:T(8,128)(2,1)S(1)}, bf16[96,128]{1,0:T(8,128)(2,1)S(1)}, u32[]{:S(2)}, u32[]{:S(2)}) collective-permute-start(bf16[96,128]{1,0:T(8,128)(2,1)S(1)} %head.1.refs_0_), channel_id=1, source_target_pairs={{0,16},{8,24},{16,0},{24,8},{1,17},{9,25},{17,1},{25,9},{2,18},{10... | collective-permute-start | bytes 73736 | tf_op jit(solution)/shard_map/ppermute | solution.py:620
  31.6 3.2 %collective-permute-start = (bf16[96,128]{1,0:T(8,128)(2,1)S(1)}, bf16[96,128]{1,0:T(8,128)(2,1)S(1)}, u32[]{:S(2)}, u32[]{:S(2)}) collective-permute-start(bf16[96,128]{1,0:T(8,128)(2,1)S(1)} %head.1.refs_0_), channel_id=1, source_target_pairs={{0,8},{8,0},{16,24},{24,16},{1,9},{9,1},{17,25},{25,17},{2,10},{10... | collective-permute-start | bytes 73736 | tf_op jit(solution)/shard_map/ppermute | solution.py:620

commit v6 on v5

--- a/solution.py
+++ b/solution.py
@@ -406,11 +406,11 @@
 
     x = iota((2 * PX, out_lanes), 0) % PX
     totals = [[None] * 4, [None] * 4]
-    done = 0
+    ends = [0] + [min(ZG * g + ZG + 1, PZ) for g in range(groups)]
+    hidden(range(ends[0], ends[1]))
     for g in range(groups):
-        upto = min(ZG * g + ZG + 1, PZ)
-        hidden(range(done, upto))
-        done = upto
+        if g + 1 < groups:
+            hidden(range(ends[g + 1], ends[g + 2]))
         cells = wide_ref[g]
         last = jnp.dot(cells, w2t_ref[...], preferred_element_type=F32)
         pairs = [

time: 35.9 us -> 35.7 us (level)
  no operation moved by 1% of the time
where the time goes in v6:
time: 35.7 us; the launch traced here: 35.4 us
  blocking collectives  9.53 us (27%)
  starting transfers between devices  9.22 us (26%)
  waiting for transfers between devices  8.31 us (23%)
  Pallas kernels  8.29 us (23%)
    all_to_all x1, blocking collectives, local(): stats = lax.all_to_all(stats, 'space', 0, 0, tiled=True)  9.53 us
    all_to_all x1, starting transfers between devices, local(): lax.all_to_all(in_vmem(windows), ('patch', 'space'), 0, 0, tiled=True)  7.33 us
    all_to_all x1, waiting for transfers between devices, local(): lax.all_to_all(in_vmem(windows), ('patch', 'space'), 0, 0, tiled=True)  6.26 us
    pallas_call x1, Pallas kernels, local(): pl.pallas_call(functools.partial(main_kernel, spaces, slab_rows, band_row...  3.82 us
    ppermute x3, waiting for transfers between devices, local(): lax.ppermute(averaged, 'patch', [(i, i ^ k) for i in range(groups)])  2.05 us
    ppermute x3, starting transfers between devices, local(): lax.ppermute(averaged, 'patch', [(i, i ^ k) for i in range(groups)])  1.9 us
    pallas_call x1, Pallas kernels, local(): pl.pallas_call(functools.partial(prep_kernel, spaces, slab_rows, band_row...  1.54 us
    pallas_call x1, Pallas kernels, local(): pl.pallas_call(cut_kernel, out_shape=pltpu.VMEM((groups * spaces, block,...  1.45 us
  transfers between devices with their start and end apart: 4, of which 3 were waited for; matrix products, arithmetic and copies ran while one was open for 0% of the time, Pallas kernels for 4%

profile of v6, /device:TPU:0, one launch (start us, length us, event | category | flops | bytes accessed | tf_op | source)
XLA Modules:
  0.0 35.4 jit_solution(3087116629558958291)
XLA Ops:
  0.0 1.4 %cut.1 = bf16[32,16,128]{2,1,0:T(8,128)(2,1)} custom-call(s32[2,4]{1,0:T(2,128)} %bitcast.7, bf16[8,2,256]{2,1,0:T(2,128)(2,1)} %image_ref.1), custom_call_target="tpu_custom_call" | custom-call | tf_op jit(solution)/shard_map/cut/pallas_call | solution.py:543
  1.4 7.3 %all-to-all-start = ((bf16[32,16,128]{2,1,0:T(8,128)(2,1)}), bf16[32,16,128]{2,1,0:T(8,128)(2,1)S(1)}, u32[]{:S(2)}, u32[]{:S(2)}) async-start(bf16[32,16,128]{2,1,0:T(8,128)(2,1)} %cut.1), calls=%async_computation | async-start | bytes 262144 | tf_op jit(solution)/shard_map/all_to_all | solution.py:551
  8.8 1.5 %prep.1 = (f32[48,512]{1,0:T(8,128)S(1)}, bf16[96,512]{1,0:T(8,128)(2,1)S(1)}, bf16[768,256]{1,0:T(8,128)(2,1)S(1)}, bf16[512,256]{1,0:T(8,128)(2,1)S(1)}, f32[8...) custom-call(s32[2,4]{1,0:T(2,128)} %bitcast.8, ...), custom_call_target="tpu_custom_call" | custom-call | tf_op jit(solution)/shard_map/prep/pallas_call | solution.py:553
  10.3 6.3 %all-to-all-done.gathered_ref = bf16[32,16,128]{2,1,0:T(8,128)(2,1)S(1)} async-done(((bf16[32,16,128]{2,1,0:T(8,128)(2,1)}), bf16[32,16,128]{2,1,0:T(8,128)(2,1)S(1)}, u32[]{:S(2)}, u32[]{:S(2)}) %all-to-all-start) | async-done | bytes 131104 | tf_op jit(solution)/shard_map/all_to_all | solution.py:551
  16.6 3.8 %main.1 = (f32[4,512,256]{2,1,0:T(8,128)S(1)}, f32[8,2,128]{2,1,0:T(2,128)S(1)}) custom-call(bf16[32,16,128]{2,1,0:T(8,128)(2,1)S(1)} %all-to-all-done.gathered_ref, s32[8,128]{1,0:T(8,128)S(1)} %get-tuple-element.16.corner_ref, f32[48,512]{1,0:T(8,128)S(1)} %get-tuple-element.18.flat_ref, bf16[96,512]{1,0:T(8,128)(2,1)S(1)} %get-tuple-element.19.full_ref, ...), custom_call_target="tpu_custom_call" | custom-call | tf_op jit(solution)/shard_map/main/pallas_call | solution.py:590
  20.4 9.5 %all_to_all.10.stats_ref = f32[8,2,128]{2,1,0:T(2,128)S(1)} all-to-all(f32[8,2,128]{2,1,0:T(2,128)S(1)} %get-tuple-element.24), channel_id=1, replica_groups=mesh['patch'=4,'space'=8] {'space'}, dimensions={0} | all-to-all | bytes 16384 | tf_op jit(solution)/shard_map/all_to_all | solution.py:610
  29.9 0.6 %head.1.refs_0_ = bf16[96,128]{1,0:T(8,128)(2,1)S(1)} custom-call(f32[4,512,256]{2,1,0:T(8,128)S(1)} %get-tuple-element.23.conv_ref, f32[8,2,128]{2,1,0:T(2,128)S(1)} %all_to_all.10.stats_ref, f32[8,512]{1,0:T(8,128)S(1)} %get-tuple-element.22.params_ref, bf16[2,24,256]{2,1,0:T(8,128)(2,1)S(1)} %get-tuple-element.25.heads_ref, ...), custom_call_target="tpu_custom_call" | custom-call | tf_op jit(solution)/shard_map/head/pallas_call | solution.py:611
  30.6 0.0 collective-permute-start.2
  30.6 0.7 %collective-permute-start.1 = (bf16[96,128]{1,0:T(8,128)(2,1)S(1)}, bf16[96,128]{1,0:T(8,128)(2,1)S(1)}, u32[]{:S(2)}, u32[]{:S(2)}) collective-permute-start(bf16[96,128]{1,0:T(8,128)(2,1)S(1)} %head.1.refs_0_), channel_id=1, source_target_pairs={{0,16},{8,24},{16,0},{24,8},{1,17},{9,25},{17,1},{25,9},{2,18},{10... | collective-permute-start | bytes 73736 | tf_op jit(solution)/shard_map/ppermute | solution.py:620
  31.3 1.2 %collective-permute-start = (bf16[96,128]{1,0:T(8,128)(2,1)S(1)}, bf16[96,128]{1,0:T(8,128)(2,1)S(1)}, u32[]{:S(2)}, u32[]{:S(2)}) collective-permute-start(bf16[96,128]{1,0:T(8,128)(2,1)S(1)} %head.1.refs_0_), channel_id=1, source_target_pairs={{0,8},{8,0},{16,24},{24,16},{1,9},{9,1},{17,25},{25,17},{2,10},{10... | collective-permute-start | bytes 73736 | tf_op jit(solution)/shard_map/ppermute | solution.py:620
  32.5 1.4 %collective-permute-done.2.refs_3_ = bf16[96,128]{1,0:T(8,128)(2,1)S(1)} collective-permute-done((bf16[96,128]{1,0:T(8,128)(2,1)S(1)}, bf16[96,128]{1,0:T(8,128)(2,1)S(1)}, u32[]{:S(2)}, u32[]{:S(2)}) %collective-permute-start.2) | collective-permute-done | bytes 24608 | tf_op jit(solution)/shard_map/ppermute | solution.py:620
  33.9 0.7 %collective-permute-done.1.refs_2_ = bf16[96,128]{1,0:T(8,128)(2,1)S(1)} collective-permute-done((bf16[96,128]{1,0:T(8,128)(2,1)S(1)}, bf16[96,128]{1,0:T(8,128)(2,1)S(1)}, u32[]{:S(2)}, u32[]{:S(2)}) %collective-permute-start.1) | collective-permute-done | bytes 24608 | tf_op jit(solution)/shard_map/ppermute | solution.py:620
  34.5 0.0 collective-permute-done.refs_1_
  34.5 0.8 %place.1 = f32[8,3,2,256]{3,2,1,0:T(2,128)} custom-call(s32[8,128]{1,0:T(8,128)S(1)} %get-tuple-element.16.corner_ref, f32[4,48,256]{2,1,0:T(8,128)S(1)} %get-tuple-element.17.weights_ref, bf16[96,128]{1,0:T(8,128)(2,1)S(1)} %head.1.refs_0_, bf16[96,128]{1,0:T(8,128)(2,1)S(1)} %collective-permute-done.refs_1_, ...), custom_call_target="tpu_custom_call" | custom-call | tf_op jit(solution)/shard_map/place/pallas_call | solution.py:623
Async XLA Ops:
  1.4 15.1 %all-to-all-start = ((bf16[32,16,128]{2,1,0:T(8,128)(2,1)}), bf16[32,16,128]{2,1,0:T(8,128)(2,1)S(1)}, u32[]{:S(2)}, u32[]{:S(2)}) async-start(bf16[32,16,128]{2,1,0:T(8,128)(2,1)} %cut.1), calls=%async_computation | async-start | bytes 262144 | tf_op jit(solution)/shard_map/all_to_all | solution.py:551
  30.6 3.3 %collective-permute-start.2 = (bf16[96,128]{1,0:T(8,128)(2,1)S(1)}, bf16[96,128]{1,0:T(8,128)(2,1)S(1)}, u32[]{:S(2)}, u32[]{:S(2)}) collective-permute-start(bf16[96,128]{1,0:T(8,128)(2,1)S(1)} %head.1.refs_0_), channel_id=1, source_target_pairs={{0,24},{8,16},{16,8},{24,0},{1,25},{9,17},{17,9},{25,1},{2,26},{10... | collective-permute-start | bytes 73736 | tf_op jit(solution)/shard_map/ppermute | solution.py:620
  30.6 3.9 %collective-permute-start.1 = (bf16[96,128]{1,0:T(8,128)(2,1)S(1)}, bf16[96,128]{1,0:T(8,128)(2,1)S(1)}, u32[]{:S(2)}, u32[]{:S(2)}) collective-permute-start(bf16[96,128]{1,0:T(8,128)(2,1)S(1)} %head.1.refs_0_), channel_id=1, source_target_pairs={{0,16},{8,24},{16,0},{24,8},{1,17},{9,25},{17,1},{25,9},{2,18},{10... | collective-permute-start | bytes 73736 | tf_op jit(solution)/shard_map/ppermute | solution.py:620
  31.3 3.2 %collective-permute-start = (bf16[96,128]{1,0:T(8,128)(2,1)S(1)}, bf16[96,128]{1,0:T(8,128)(2,1)S(1)}, u32[]{:S(2)}, u32[]{:S(2)}) collective-permute-start(bf16[96,128]{1,0:T(8,128)(2,1)S(1)} %head.1.refs_0_), channel_id=1, source_target_pairs={{0,8},{8,0},{16,24},{24,16},{1,9},{9,1},{17,25},{25,17},{2,10},{10... | collective-permute-start | bytes 73736 | tf_op jit(solution)/shard_map/ppermute | solution.py:620

commit v7 on v6

--- a/solution.py
+++ b/solution.py
@@ -44,7 +44,7 @@
         shift = lax.rem(width - offsets_ref[1, item], width)
         window = pltpu.roll(rows, shift, 1)[:, :PX].astype(BF16)
         for space in range(spaces):
-            out_ref[item * spaces + space] = window
+            out_ref[space * items + item] = window
 
 
 def prep_kernel(
@@ -218,8 +218,10 @@
 def line_rows(start_z, gathered_ref, cells_ref, lines_ref, slab_rows, band_rows, spaces):
     block = slab_rows * band_rows
     pitch = block + 1
+    slabs = gathered_ref.shape[0] // spaces
     for device in range(gathered_ref.shape[0]):
-        cells_ref[device * pitch : device * pitch + block, :] = gathered_ref[device].astype(F32)
+        at = (device % slabs * spaces + device // slabs) * pitch
+        cells_ref[at : at + block, :] = gathered_ref[device].astype(F32)
     lane = iota((spaces, PX), 1)
     empty = jnp.zeros((spaces, PX), F32)
     edge = jnp.zeros((LINE, PX), F32)
@@ -411,35 +413,39 @@
     for g in range(groups):
         if g + 1 < groups:
             hidden(range(ends[g + 1], ends[g + 2]))
-        cells = wide_ref[g]
-        last = jnp.dot(cells, w2t_ref[...], preferred_element_type=F32)
-        pairs = [
-            jnp.dot(
-                cells[:, at : at + w2p_ref.shape[0]], w2p_ref[...], preferred_element_type=F32
+        spans = ((0, 4),) if g + 1 < groups else ((0, 2), (2, 4))
+        for low, high in spans:
+            cells = wide_ref[g, low * PX : high * PX, :]
+            last = jnp.dot(cells, w2t_ref[...], preferred_element_type=F32)
+            pairs = [
+                jnp.dot(
+                    cells[:, at : at + w2p_ref.shape[0]],
+                    w2p_ref[...],
+                    preferred_element_type=F32,
+                )
+                for at in (0, ZG // 2 * step)
+            ]
+            first, middle = (
+                jnp.concatenate([pair[:, at : at + half] for pair in pairs], axis=1)
+                for at in (0, half)
             )
-            for at in (0, ZG // 2 * step)
-        ]
-        first, middle = (
-            jnp.concatenate([pair[:, at : at + half] for pair in pairs], axis=1)
-            for at in (0, half)
-        )
-        for flip in range(2):
-            at = flip * 2 * PX
-            before, after = (last, first) if flip else (first, last)
-            value = (
-                middle[at : at + 2 * PX]
-                + jnp.where(x == 0, 0.0, pltpu.roll(before[at : at + 2 * PX], 1, 0))
-                + jnp.where(
-                    x == PX - 1, 0.0, pltpu.roll(after[at : at + 2 * PX], 2 * PX - 1, 0)
+            for pair in range(low, high, 2):
+                at = (pair - low) * PX
+                before, after = (last, first) if pair >= 2 else (first, last)
+                value = (
+                    middle[at : at + 2 * PX]
+                    + jnp.where(x == 0, 0.0, pltpu.roll(before[at : at + 2 * PX], 1, 0))
+                    + jnp.where(
+                        x == PX - 1, 0.0, pltpu.roll(after[at : at + 2 * PX], 2 * PX - 1, 0)
+                    )
                 )
-            )
-            conv_ref[g, at : at + 2 * PX, :] = value
-            for f in (2 * flip, 2 * flip + 1):
-                part = value[f * PX - at : (f + 1) * PX - at]
-                for kind, item in enumerate((part, part * part)):
-                    item = jnp.sum(item, axis=0, keepdims=True)
-                    old = totals[kind][f]
-                    totals[kind][f] = item if old is None else old + item
+                conv_ref[g, pair * PX : (pair + 2) * PX, :] = value
+                for f in (pair, pair + 1):
+                    part = value[(f - pair) * PX : (f - pair + 1) * PX]
+                    for kind, item in enumerate((part, part * part)):
+                        item = jnp.sum(item, axis=0, keepdims=True)
+                        old = totals[kind][f]
+                        totals[kind][f] = item if old is None else old + item
     sums = jnp.concatenate(totals[0] + totals[1], axis=0)
     lanes = 4 * channels
     sums = sum(sums[:, at : at + lanes] for at in range(0, out_lanes, lanes))
@@ -548,7 +554,7 @@
         scratch_shapes=[pltpu.VMEM((block, width), F32)],
         name="cut",
     )(corners, image)
-    gathered = lax.all_to_all(in_vmem(windows), ("patch", "space"), 0, 0, tiled=True)
+    gathered = lax.all_to_all(windows, ("space", "patch"), 0, 0, tiled=True)
 
     flat, full, w2t, w2p, params, heads, bias, weights, corner = pl.pallas_call(
         functools.partial(prep_kernel, spaces, slab_rows, band_rows),

time: 35.7 us -> 35.6 us (level)
  blocking collectives: 9.53 us -> 9.01 us
  waiting for transfers between devices: 8.31 us -> 8.77 us
    all_to_all x1, blocking collectives: 9.53 us -> 9.01 us  [local(): stats = lax.all_to_all(stats, 'space', 0, 0, tiled=True)]
    all_to_all x1, waiting for transfers between devices: 6.26 us -> 6.66 us  [local(): gathered = lax.all_to_all(windows, ('space', 'patch'), 0, 0, tiled=True)]
where the time goes in v7:
time: 35.6 us; the launch traced here: 35.3 us
  starting transfers between devices  9.22 us (26%)
  blocking collectives  9.01 us (25%)
  waiting for transfers between devices  8.77 us (25%)
  Pallas kernels  8.26 us (23%)
    all_to_all x1, blocking collectives, local(): stats = lax.all_to_all(stats, 'space', 0, 0, tiled=True)  9.01 us
    all_to_all x1, starting transfers between devices, local(): gathered = lax.all_to_all(windows, ('space', 'patch'), 0, 0, tiled=True)  7.33 us
    all_to_all x1, waiting for transfers between devices, local(): gathered = lax.all_to_all(windows, ('space', 'patch'), 0, 0, tiled=True)  6.66 us
    pallas_call x1, Pallas kernels, local(): pl.pallas_call(functools.partial(main_kernel, spaces, slab_rows, band_row...  3.79 us
    ppermute x3, waiting for transfers between devices, local(): lax.ppermute(averaged, 'patch', [(i, i ^ k) for i in range(groups)])  2.11 us
    ppermute x3, starting transfers between devices, local(): lax.ppermute(averaged, 'patch', [(i, i ^ k) for i in range(groups)])  1.9 us
    pallas_call x1, Pallas kernels, local(): pl.pallas_call(functools.partial(prep_kernel, spaces, slab_rows, band_row...  1.54 us
    pallas_call x1, Pallas kernels, local(): pl.pallas_call(cut_kernel, out_shape=pltpu.VMEM((groups * spaces, block,...  1.45 us
  transfers between devices with their start and end apart: 4, of which 3 were waited for; matrix products, arithmetic and copies ran while one was open for 0% of the time, Pallas kernels for 4%

profile of v7, /device:TPU:0, one launch (start us, length us, event | category | flops | bytes accessed | tf_op | source)
XLA Modules:
  0.0 35.3 jit_solution(9491229876628654554)
XLA Ops:
  0.0 1.4 %cut.1 = bf16[32,16,128]{2,1,0:T(8,128)(2,1)} custom-call(s32[2,4]{1,0:T(2,128)} %bitcast.7, bf16[8,2,256]{2,1,0:T(2,128)(2,1)} %image_ref.1), custom_call_target="tpu_custom_call" | custom-call | tf_op jit(solution)/shard_map/cut/pallas_call | solution.py:549
  1.4 7.3 %all-to-all-start = ((bf16[32,16,128]{2,1,0:T(8,128)(2,1)}), bf16[32,16,128]{2,1,0:T(8,128)(2,1)S(1)}, u32[]{:S(2)}, u32[]{:S(2)}) async-start(bf16[32,16,128]{2,1,0:T(8,128)(2,1)} %cut.1), calls=%async_computation | async-start | bytes 262144 | tf_op jit(solution)/shard_map/all_to_all | solution.py:557
  8.8 1.5 %prep.1 = (f32[48,512]{1,0:T(8,128)S(1)}, bf16[96,512]{1,0:T(8,128)(2,1)S(1)}, bf16[768,256]{1,0:T(8,128)(2,1)S(1)}, bf16[512,256]{1,0:T(8,128)(2,1)S(1)}, f32[8...) custom-call(s32[2,4]{1,0:T(2,128)} %bitcast.8, ...), custom_call_target="tpu_custom_call" | custom-call | tf_op jit(solution)/shard_map/prep/pallas_call | solution.py:559
  10.3 6.7 %all-to-all-done.gathered_ref = bf16[32,16,128]{2,1,0:T(8,128)(2,1)S(1)} async-done(((bf16[32,16,128]{2,1,0:T(8,128)(2,1)}), bf16[32,16,128]{2,1,0:T(8,128)(2,1)S(1)}, u32[]{:S(2)}, u32[]{:S(2)}) %all-to-all-start) | async-done | bytes 131104 | tf_op jit(solution)/shard_map/all_to_all | solution.py:557
  17.0 3.8 %main.1 = (f32[4,512,256]{2,1,0:T(8,128)S(1)}, f32[8,2,128]{2,1,0:T(2,128)S(1)}) custom-call(bf16[32,16,128]{2,1,0:T(8,128)(2,1)S(1)} %all-to-all-done.gathered_ref, s32[8,128]{1,0:T(8,128)S(1)} %get-tuple-element.16.corner_ref, f32[48,512]{1,0:T(8,128)S(1)} %get-tuple-element.18.flat_ref, bf16[96,512]{1,0:T(8,128)(2,1)S(1)} %get-tuple-element.19.full_ref, ...), custom_call_target="tpu_custom_call" | custom-call | tf_op jit(solution)/shard_map/main/pallas_call | solution.py:596
  20.8 9.0 %all_to_all.10.stats_ref = f32[8,2,128]{2,1,0:T(2,128)S(1)} all-to-all(f32[8,2,128]{2,1,0:T(2,128)S(1)} %get-tuple-element.24), channel_id=1, replica_groups=mesh['patch'=4,'space'=8] {'space'}, dimensions={0} | all-to-all | bytes 16384 | tf_op jit(solution)/shard_map/all_to_all | solution.py:616
  29.8 0.6 %head.1.refs_0_ = bf16[96,128]{1,0:T(8,128)(2,1)S(1)} custom-call(f32[4,512,256]{2,1,0:T(8,128)S(1)} %get-tuple-element.23.conv_ref, f32[8,2,128]{2,1,0:T(2,128)S(1)} %all_to_all.10.stats_ref, f32[8,512]{1,0:T(8,128)S(1)} %get-tuple-element.22.params_ref, bf16[2,24,256]{2,1,0:T(8,128)(2,1)S(1)} %get-tuple-element.25.heads_ref, ...), custom_call_target="tpu_custom_call" | custom-call | tf_op jit(solution)/shard_map/head/pallas_call | solution.py:617
  30.4 0.0 collective-permute-start.2
  30.5 0.8 %collective-permute-start.1 = (bf16[96,128]{1,0:T(8,128)(2,1)S(1)}, bf16[96,128]{1,0:T(8,128)(2,1)S(1)}, u32[]{:S(2)}, u32[]{:S(2)}) collective-permute-start(bf16[96,128]{1,0:T(8,128)(2,1)S(1)} %head.1.refs_0_), channel_id=1, source_target_pairs={{0,16},{8,24},{16,0},{24,8},{1,17},{9,25},{17,1},{25,9},{2,18},{10... | collective-permute-start | bytes 73736 | tf_op jit(solution)/shard_map/ppermute | solution.py:626
  31.3 1.0 %collective-permute-start = (bf16[96,128]{1,0:T(8,128)(2,1)S(1)}, bf16[96,128]{1,0:T(8,128)(2,1)S(1)}, u32[]{:S(2)}, u32[]{:S(2)}) collective-permute-start(bf16[96,128]{1,0:T(8,128)(2,1)S(1)} %head.1.refs_0_), channel_id=1, source_target_pairs={{0,8},{8,0},{16,24},{24,16},{1,9},{9,1},{17,25},{25,17},{2,10},{10... | collective-permute-start | bytes 73736 | tf_op jit(solution)/shard_map/ppermute | solution.py:626
  32.3 1.4 %collective-permute-done.2.refs_3_ = bf16[96,128]{1,0:T(8,128)(2,1)S(1)} collective-permute-done((bf16[96,128]{1,0:T(8,128)(2,1)S(1)}, bf16[96,128]{1,0:T(8,128)(2,1)S(1)}, u32[]{:S(2)}, u32[]{:S(2)}) %collective-permute-start.2) | collective-permute-done | bytes 24608 | tf_op jit(solution)/shard_map/ppermute | solution.py:626
  33.7 0.7 %collective-permute-done.1.refs_2_ = bf16[96,128]{1,0:T(8,128)(2,1)S(1)} collective-permute-done((bf16[96,128]{1,0:T(8,128)(2,1)S(1)}, bf16[96,128]{1,0:T(8,128)(2,1)S(1)}, u32[]{:S(2)}, u32[]{:S(2)}) %collective-permute-start.1) | collective-permute-done | bytes 24608 | tf_op jit(solution)/shard_map/ppermute | solution.py:626
  34.4 0.0 collective-permute-done.refs_1_
  34.5 0.8 %place.1 = f32[8,3,2,256]{3,2,1,0:T(2,128)} custom-call(s32[8,128]{1,0:T(8,128)S(1)} %get-tuple-element.16.corner_ref, f32[4,48,256]{2,1,0:T(8,128)S(1)} %get-tuple-element.17.weights_ref, bf16[96,128]{1,0:T(8,128)(2,1)S(1)} %head.1.refs_0_, bf16[96,128]{1,0:T(8,128)(2,1)S(1)} %collective-permute-done.refs_1_, ...), custom_call_target="tpu_custom_call" | custom-call | tf_op jit(solution)/shard_map/place/pallas_call | solution.py:629
Async XLA Ops:
  1.4 15.5 %all-to-all-start = ((bf16[32,16,128]{2,1,0:T(8,128)(2,1)}), bf16[32,16,128]{2,1,0:T(8,128)(2,1)S(1)}, u32[]{:S(2)}, u32[]{:S(2)}) async-start(bf16[32,16,128]{2,1,0:T(8,128)(2,1)} %cut.1), calls=%async_computation | async-start | bytes 262144 | tf_op jit(solution)/shard_map/all_to_all | solution.py:557
  30.4 3.3 %collective-permute-start.2 = (bf16[96,128]{1,0:T(8,128)(2,1)S(1)}, bf16[96,128]{1,0:T(8,128)(2,1)S(1)}, u32[]{:S(2)}, u32[]{:S(2)}) collective-permute-start(bf16[96,128]{1,0:T(8,128)(2,1)S(1)} %head.1.refs_0_), channel_id=1, source_target_pairs={{0,24},{8,16},{16,8},{24,0},{1,25},{9,17},{17,9},{25,1},{2,26},{10... | collective-permute-start | bytes 73736 | tf_op jit(solution)/shard_map/ppermute | solution.py:626
  30.5 4.0 %collective-permute-start.1 = (bf16[96,128]{1,0:T(8,128)(2,1)S(1)}, bf16[96,128]{1,0:T(8,128)(2,1)S(1)}, u32[]{:S(2)}, u32[]{:S(2)}) collective-permute-start(bf16[96,128]{1,0:T(8,128)(2,1)S(1)} %head.1.refs_0_), channel_id=1, source_target_pairs={{0,16},{8,24},{16,0},{24,8},{1,17},{9,25},{17,1},{25,9},{2,18},{10... | collective-permute-start | bytes 73736 | tf_op jit(solution)/shard_map/ppermute | solution.py:626
  31.3 3.2 %collective-permute-start = (bf16[96,128]{1,0:T(8,128)(2,1)S(1)}, bf16[96,128]{1,0:T(8,128)(2,1)S(1)}, u32[]{:S(2)}, u32[]{:S(2)}) collective-permute-start(bf16[96,128]{1,0:T(8,128)(2,1)S(1)} %head.1.refs_0_), channel_id=1, source_target_pairs={{0,8},{8,0},{16,24},{24,16},{1,9},{9,1},{17,25},{25,17},{2,10},{10... | collective-permute-start | bytes 73736 | tf_op jit(solution)/shard_map/ppermute | solution.py:626

commit v8 on v7

--- a/solution.py
+++ b/solution.py
@@ -616,7 +616,7 @@
     stats = lax.all_to_all(stats, "space", 0, 0, tiled=True)
     averaged = pl.pallas_call(
         functools.partial(head_kernel, float(PZ * rows * PX), channels),
-        out_shape=pltpu.VMEM((PZ * per_z, PX), BF16),
+        out_shape=pltpu.VMEM((PZ * per_z, PX), F32),
         in_specs=[VMEM] * 5,
         out_specs=VMEM,
         compiler_params=pltpu.CompilerParams(vmem_limit_bytes=8 << 20),

time: 35.6 us -> 36.2 us (1.017)
  waiting for transfers between devices: 8.77 us -> 9.36 us
    ppermute x3, waiting for transfers between devices: 2.11 us -> 2.71 us  [local(): lax.ppermute(averaged, 'patch', [(i, i ^ k) for i in range(groups)])]
where the time goes in v8:
time: 36.2 us; the launch traced here: 35.9 us
  waiting for transfers between devices  9.36 us (26%)
  starting transfers between devices  9.21 us (25%)
  blocking collectives  9.01 us (25%)
  Pallas kernels  8.26 us (23%)
    all_to_all x1, blocking collectives, local(): stats = lax.all_to_all(stats, 'space', 0, 0, tiled=True)  9.01 us
    all_to_all x1, starting transfers between devices, local(): gathered = lax.all_to_all(windows, ('space', 'patch'), 0, 0, tiled=True)  7.33 us
    all_to_all x1, waiting for transfers between devices, local(): gathered = lax.all_to_all(windows, ('space', 'patch'), 0, 0, tiled=True)  6.66 us
    pallas_call x1, Pallas kernels, local(): pl.pallas_call(functools.partial(main_kernel, spaces, slab_rows, band_row...  3.79 us
    ppermute x3, waiting for transfers between devices, local(): lax.ppermute(averaged, 'patch', [(i, i ^ k) for i in range(groups)])  2.71 us
    ppermute x3, starting transfers between devices, local(): lax.ppermute(averaged, 'patch', [(i, i ^ k) for i in range(groups)])  1.89 us
    pallas_call x1, Pallas kernels, local(): pl.pallas_call(functools.partial(prep_kernel, spaces, slab_rows, band_row...  1.54 us
    pallas_call x1, Pallas kernels, local(): pl.pallas_call(cut_kernel, out_shape=pltpu.VMEM((groups * spaces, block,...  1.45 us
  transfers between devices with their start and end apart: 4, of which 3 were waited for; matrix products, arithmetic and copies ran while one was open for 0% of the time, Pallas kernels for 4%

profile of v8, /device:TPU:0, one launch (start us, length us, event | category | flops | bytes accessed | tf_op | source)
XLA Modules:
  0.0 35.9 jit_solution(1346028947037484781)
XLA Ops:
  0.0 1.4 %cut.1 = bf16[32,16,128]{2,1,0:T(8,128)(2,1)} custom-call(s32[2,4]{1,0:T(2,128)} %bitcast.7, bf16[8,2,256]{2,1,0:T(2,128)(2,1)} %image_ref.1), custom_call_target="tpu_custom_call" | custom-call | tf_op jit(solution)/shard_map/cut/pallas_call | solution.py:549
  1.4 7.3 %all-to-all-start = ((bf16[32,16,128]{2,1,0:T(8,128)(2,1)}), bf16[32,16,128]{2,1,0:T(8,128)(2,1)S(1)}, u32[]{:S(2)}, u32[]{:S(2)}) async-start(bf16[32,16,128]{2,1,0:T(8,128)(2,1)} %cut.1), calls=%async_computation | async-start | bytes 262144 | tf_op jit(solution)/shard_map/all_to_all | solution.py:557
  8.8 1.5 %prep.1 = (f32[48,512]{1,0:T(8,128)S(1)}, bf16[96,512]{1,0:T(8,128)(2,1)S(1)}, bf16[768,256]{1,0:T(8,128)(2,1)S(1)}, bf16[512,256]{1,0:T(8,128)(2,1)S(1)}, f32[8...) custom-call(s32[2,4]{1,0:T(2,128)} %bitcast.8, ...), custom_call_target="tpu_custom_call" | custom-call | tf_op jit(solution)/shard_map/prep/pallas_call | solution.py:559
  10.3 6.7 %all-to-all-done.gathered_ref = bf16[32,16,128]{2,1,0:T(8,128)(2,1)S(1)} async-done(((bf16[32,16,128]{2,1,0:T(8,128)(2,1)}), bf16[32,16,128]{2,1,0:T(8,128)(2,1)S(1)}, u32[]{:S(2)}, u32[]{:S(2)}) %all-to-all-start) | async-done | bytes 131104 | tf_op jit(solution)/shard_map/all_to_all | solution.py:557
  17.0 3.8 %main.1 = (f32[4,512,256]{2,1,0:T(8,128)S(1)}, f32[8,2,128]{2,1,0:T(2,128)S(1)}) custom-call(bf16[32,16,128]{2,1,0:T(8,128)(2,1)S(1)} %all-to-all-done.gathered_ref, s32[8,128]{1,0:T(8,128)S(1)} %get-tuple-element.16.corner_ref, f32[48,512]{1,0:T(8,128)S(1)} %get-tuple-element.18.flat_ref, bf16[96,512]{1,0:T(8,128)(2,1)S(1)} %get-tuple-element.19.full_ref, ...), custom_call_target="tpu_custom_call" | custom-call | tf_op jit(solution)/shard_map/main/pallas_call | solution.py:596
  20.8 9.0 %all_to_all.10.stats_ref = f32[8,2,128]{2,1,0:T(2,128)S(1)} all-to-all(f32[8,2,128]{2,1,0:T(2,128)S(1)} %get-tuple-element.24), channel_id=1, replica_groups=mesh['patch'=4,'space'=8] {'space'}, dimensions={0} | all-to-all | bytes 16384 | tf_op jit(solution)/shard_map/all_to_all | solution.py:616
  29.8 0.6 %head.1.refs_0_ = f32[96,128]{1,0:T(8,128)S(1)} custom-call(f32[4,512,256]{2,1,0:T(8,128)S(1)} %get-tuple-element.23.conv_ref, f32[8,2,128]{2,1,0:T(2,128)S(1)} %all_to_all.10.stats_ref, f32[8,512]{1,0:T(8,128)S(1)} %get-tuple-element.22.params_ref, bf16[2,24,256]{2,1,0:T(8,128)(2,1)S(1)} %get-tuple-element.25.heads_ref, ...), custom_call_target="tpu_custom_call" | custom-call | tf_op jit(solution)/shard_map/head/pallas_call | solution.py:617
  30.4 0.0 collective-permute-start.2
  30.5 0.8 %collective-permute-start.1 = (f32[96,128]{1,0:T(8,128)S(1)}, f32[96,128]{1,0:T(8,128)S(1)}, u32[]{:S(2)}, u32[]{:S(2)}) collective-permute-start(f32[96,128]{1,0:T(8,128)S(1)} %head.1.refs_0_), channel_id=1, source_target_pairs={{0,16},{8,24},{16,0},{24,8},{1,17},{9,25},{17,1},{25,9},{2,18},{10... | collective-permute-start | bytes 147464 | tf_op jit(solution)/shard_map/ppermute | solution.py:626
  31.3 1.0 %collective-permute-start = (f32[96,128]{1,0:T(8,128)S(1)}, f32[96,128]{1,0:T(8,128)S(1)}, u32[]{:S(2)}, u32[]{:S(2)}) collective-permute-start(f32[96,128]{1,0:T(8,128)S(1)} %head.1.refs_0_), channel_id=1, source_target_pairs={{0,8},{8,0},{16,24},{24,16},{1,9},{9,1},{17,25},{25,17},{2,10},{10... | collective-permute-start | bytes 147464 | tf_op jit(solution)/shard_map/ppermute | solution.py:626
  32.3 1.7 %collective-permute-done.2.refs_3_ = f32[96,128]{1,0:T(8,128)S(1)} collective-permute-done((f32[96,128]{1,0:T(8,128)S(1)}, f32[96,128]{1,0:T(8,128)S(1)}, u32[]{:S(2)}, u32[]{:S(2)}) %collective-permute-start.2) | collective-permute-done | bytes 49184 | tf_op jit(solution)/shard_map/ppermute | solution.py:626
  34.0 1.1 %collective-permute-done.1.refs_2_ = f32[96,128]{1,0:T(8,128)S(1)} collective-permute-done((f32[96,128]{1,0:T(8,128)S(1)}, f32[96,128]{1,0:T(8,128)S(1)}, u32[]{:S(2)}, u32[]{:S(2)}) %collective-permute-start.1) | collective-permute-done | bytes 49184 | tf_op jit(solution)/shard_map/ppermute | solution.py:626
  35.0 0.0 collective-permute-done.refs_1_
  35.0 0.8 %place.1 = f32[8,3,2,256]{3,2,1,0:T(2,128)} custom-call(s32[8,128]{1,0:T(8,128)S(1)} %get-tuple-element.16.corner_ref, f32[4,48,256]{2,1,0:T(8,128)S(1)} %get-tuple-element.17.weights_ref, f32[96,128]{1,0:T(8,128)S(1)} %head.1.refs_0_, f32[96,128]{1,0:T(8,128)S(1)} %collective-permute-done.refs_1_, f32[96,128]{1,0:T(8,128)S(1)} %collective-permute-done.1.refs_2_, ...), custom_call_target="tpu_custom_call" | custom-call | tf_op jit(solution)/shard_map/place/pallas_call | solution.py:629
Async XLA Ops:
  1.4 15.5 %all-to-all-start = ((bf16[32,16,128]{2,1,0:T(8,128)(2,1)}), bf16[32,16,128]{2,1,0:T(8,128)(2,1)S(1)}, u32[]{:S(2)}, u32[]{:S(2)}) async-start(bf16[32,16,128]{2,1,0:T(8,128)(2,1)} %cut.1), calls=%async_computation | async-start | bytes 262144 | tf_op jit(solution)/shard_map/all_to_all | solution.py:557
  30.4 3.6 %collective-permute-start.2 = (f32[96,128]{1,0:T(8,128)S(1)}, f32[96,128]{1,0:T(8,128)S(1)}, u32[]{:S(2)}, u32[]{:S(2)}) collective-permute-start(f32[96,128]{1,0:T(8,128)S(1)} %head.1.refs_0_), channel_id=1, source_target_pairs={{0,24},{8,16},{16,8},{24,0},{1,25},{9,17},{17,9},{25,1},{2,26},{10... | collective-permute-start | bytes 147464 | tf_op jit(solution)/shard_map/ppermute | solution.py:626
  30.5 4.6 %collective-permute-start.1 = (f32[96,128]{1,0:T(8,128)S(1)}, f32[96,128]{1,0:T(8,128)S(1)}, u32[]{:S(2)}, u32[]{:S(2)}) collective-permute-start(f32[96,128]{1,0:T(8,128)S(1)} %head.1.refs_0_), channel_id=1, source_target_pairs={{0,16},{8,24},{16,0},{24,8},{1,17},{9,25},{17,1},{25,9},{2,18},{10... | collective-permute-start | bytes 147464 | tf_op jit(solution)/shard_map/ppermute | solution.py:626
  31.3 3.8 %collective-permute-start = (f32[96,128]{1,0:T(8,128)S(1)}, f32[96,128]{1,0:T(8,128)S(1)}, u32[]{:S(2)}, u32[]{:S(2)}) collective-permute-start(f32[96,128]{1,0:T(8,128)S(1)} %head.1.refs_0_), channel_id=1, source_target_pairs={{0,8},{8,0},{16,24},{24,16},{1,9},{9,1},{17,25},{25,17},{2,10},{10... | collective-permute-start | bytes 147464 | tf_op jit(solution)/shard_map/ppermute | solution.py:626

commit v9 on v6

--- a/solution.py
+++ b/solution.py
@@ -44,7 +44,7 @@
         shift = lax.rem(width - offsets_ref[1, item], width)
         window = pltpu.roll(rows, shift, 1)[:, :PX].astype(BF16)
         for space in range(spaces):
-            out_ref[item * spaces + space] = window
+            out_ref[space * items + item] = window
 
 
 def prep_kernel(
@@ -218,8 +218,10 @@
 def line_rows(start_z, gathered_ref, cells_ref, lines_ref, slab_rows, band_rows, spaces):
     block = slab_rows * band_rows
     pitch = block + 1
+    slabs = gathered_ref.shape[0] // spaces
     for device in range(gathered_ref.shape[0]):
-        cells_ref[device * pitch : device * pitch + block, :] = gathered_ref[device].astype(F32)
+        at = (device % slabs * spaces + device // slabs) * pitch
+        cells_ref[at : at + block, :] = gathered_ref[device].astype(F32)
     lane = iota((spaces, PX), 1)
     empty = jnp.zeros((spaces, PX), F32)
     edge = jnp.zeros((LINE, PX), F32)
@@ -406,12 +408,13 @@
 
     x = iota((2 * PX, out_lanes), 0) % PX
     totals = [[None] * 4, [None] * 4]
-    ends = [0] + [min(ZG * g + ZG + 1, PZ) for g in range(groups)]
+    blocks = ((0, 1), (1, 3), (3, groups))
+    ends = [0] + [min(ZG * after, PZ - 1) + 1 for _, after in blocks]
     hidden(range(ends[0], ends[1]))
-    for g in range(groups):
-        if g + 1 < groups:
-            hidden(range(ends[g + 1], ends[g + 2]))
-        cells = wide_ref[g]
+    for n, (start, after) in enumerate(blocks):
+        if n + 1 < len(blocks):
+            hidden(range(ends[n + 1], ends[n + 2]))
+        cells = wide_ref[start:after].reshape((after - start) * 4 * PX, wide_ref.shape[2])
         last = jnp.dot(cells, w2t_ref[...], preferred_element_type=F32)
         pairs = [
             jnp.dot(
@@ -423,19 +426,20 @@
             jnp.concatenate([pair[:, at : at + half] for pair in pairs], axis=1)
             for at in (0, half)
         )
-        for flip in range(2):
-            at = flip * 2 * PX
-            before, after = (last, first) if flip else (first, last)
+        for pair in range(2 * (after - start)):
+            at = pair * 2 * PX
+            g, low = start + pair // 2, pair % 2 * 2
+            before, behind = (last, first) if low else (first, last)
             value = (
                 middle[at : at + 2 * PX]
                 + jnp.where(x == 0, 0.0, pltpu.roll(before[at : at + 2 * PX], 1, 0))
                 + jnp.where(
-                    x == PX - 1, 0.0, pltpu.roll(after[at : at + 2 * PX], 2 * PX - 1, 0)
+                    x == PX - 1, 0.0, pltpu.roll(behind[at : at + 2 * PX], 2 * PX - 1, 0)
                 )
             )
-            conv_ref[g, at : at + 2 * PX, :] = value
-            for f in (2 * flip, 2 * flip + 1):
-                part = value[f * PX - at : (f + 1) * PX - at]
+            conv_ref[g, low * PX : (low + 2) * PX, :] = value
+            for f in (low, low + 1):
+                part = value[(f - low) * PX : (f - low + 1) * PX]
                 for kind, item in enumerate((part, part * part)):
                     item = jnp.sum(item, axis=0, keepdims=True)
                     old = totals[kind][f]
@@ -548,7 +552,7 @@
         scratch_shapes=[pltpu.VMEM((block, width), F32)],
         name="cut",
     )(corners, image)
-    gathered = lax.all_to_all(in_vmem(windows), ("patch", "space"), 0, 0, tiled=True)
+    gathered = lax.all_to_all(windows, ("space", "patch"), 0, 0, tiled=True)
 
     flat, full, w2t, w2p, params, heads, bias, weights, corner = pl.pallas_call(
         functools.partial(prep_kernel, spaces, slab_rows, band_rows),

time: 35.7 us -> 35.6 us (level)
  blocking collectives: 9.53 us -> 9.01 us
  waiting for transfers between devices: 8.31 us -> 8.77 us
    all_to_all x1, blocking collectives: 9.53 us -> 9.01 us  [local(): stats = lax.all_to_all(stats, 'space', 0, 0, tiled=True)]
    all_to_all x1, waiting for transfers between devices: 6.26 us -> 6.66 us  [local(): gathered = lax.all_to_all(windows, ('space', 'patch'), 0, 0, tiled=True)]
where the time goes in v9:
time: 35.6 us; the launch traced here: 35.3 us
  starting transfers between devices  9.22 us (26%)
  blocking collectives  9.01 us (25%)
  waiting for transfers between devices  8.77 us (25%)
  Pallas kernels  8.26 us (23%)
    all_to_all x1, blocking collectives, local(): stats = lax.all_to_all(stats, 'space', 0, 0, tiled=True)  9.01 us
    all_to_all x1, starting transfers between devices, local(): gathered = lax.all_to_all(windows, ('space', 'patch'), 0, 0, tiled=True)  7.33 us
    all_to_all x1, waiting for transfers between devices, local(): gathered = lax.all_to_all(windows, ('space', 'patch'), 0, 0, tiled=True)  6.66 us
    pallas_call x1, Pallas kernels, local(): pl.pallas_call(functools.partial(main_kernel, spaces, slab_rows, band_row...  3.79 us
    ppermute x3, waiting for transfers between devices, local(): lax.ppermute(averaged, 'patch', [(i, i ^ k) for i in range(groups)])  2.11 us
    ppermute x3, starting transfers between devices, local(): lax.ppermute(averaged, 'patch', [(i, i ^ k) for i in range(groups)])  1.9 us
    pallas_call x1, Pallas kernels, local(): pl.pallas_call(functools.partial(prep_kernel, spaces, slab_rows, band_row...  1.54 us
    pallas_call x1, Pallas kernels, local(): pl.pallas_call(cut_kernel, out_shape=pltpu.VMEM((groups * spaces, block,...  1.45 us
  transfers between devices with their start and end apart: 4, of which 3 were waited for; matrix products, arithmetic and copies ran while one was open for 0% of the time, Pallas kernels for 4%

profile of v9, /device:TPU:0, one launch (start us, length us, event | category | flops | bytes accessed | tf_op | source)
XLA Modules:
  0.0 35.3 jit_solution(5718952287678097760)
XLA Ops:
  0.0 1.4 %cut.1 = bf16[32,16,128]{2,1,0:T(8,128)(2,1)} custom-call(s32[2,4]{1,0:T(2,128)} %bitcast.7, bf16[8,2,256]{2,1,0:T(2,128)(2,1)} %image_ref.1), custom_call_target="tpu_custom_call" | custom-call | tf_op jit(solution)/shard_map/cut/pallas_call | solution.py:547
  1.4 7.3 %all-to-all-start = ((bf16[32,16,128]{2,1,0:T(8,128)(2,1)}), bf16[32,16,128]{2,1,0:T(8,128)(2,1)S(1)}, u32[]{:S(2)}, u32[]{:S(2)}) async-start(bf16[32,16,128]{2,1,0:T(8,128)(2,1)} %cut.1), calls=%async_computation | async-start | bytes 262144 | tf_op jit(solution)/shard_map/all_to_all | solution.py:555
  8.8 1.5 %prep.1 = (f32[48,512]{1,0:T(8,128)S(1)}, bf16[96,512]{1,0:T(8,128)(2,1)S(1)}, bf16[768,256]{1,0:T(8,128)(2,1)S(1)}, bf16[512,256]{1,0:T(8,128)(2,1)S(1)}, f32[8...) custom-call(s32[2,4]{1,0:T(2,128)} %bitcast.8, ...), custom_call_target="tpu_custom_call" | custom-call | tf_op jit(solution)/shard_map/prep/pallas_call | solution.py:557
  10.3 6.7 %all-to-all-done.gathered_ref = bf16[32,16,128]{2,1,0:T(8,128)(2,1)S(1)} async-done(((bf16[32,16,128]{2,1,0:T(8,128)(2,1)}), bf16[32,16,128]{2,1,0:T(8,128)(2,1)S(1)}, u32[]{:S(2)}, u32[]{:S(2)}) %all-to-all-start) | async-done | bytes 131104 | tf_op jit(solution)/shard_map/all_to_all | solution.py:555
  17.0 3.8 %main.1 = (f32[4,512,256]{2,1,0:T(8,128)S(1)}, f32[8,2,128]{2,1,0:T(2,128)S(1)}) custom-call(bf16[32,16,128]{2,1,0:T(8,128)(2,1)S(1)} %all-to-all-done.gathered_ref, s32[8,128]{1,0:T(8,128)S(1)} %get-tuple-element.16.corner_ref, f32[48,512]{1,0:T(8,128)S(1)} %get-tuple-element.18.flat_ref, bf16[96,512]{1,0:T(8,128)(2,1)S(1)} %get-tuple-element.19.full_ref, ...), custom_call_target="tpu_custom_call" | custom-call | tf_op jit(solution)/shard_map/main/pallas_call | solution.py:594
  20.8 9.0 %all_to_all.10.stats_ref = f32[8,2,128]{2,1,0:T(2,128)S(1)} all-to-all(f32[8,2,128]{2,1,0:T(2,128)S(1)} %get-tuple-element.24), channel_id=1, replica_groups=mesh['patch'=4,'space'=8] {'space'}, dimensions={0} | all-to-all | bytes 16384 | tf_op jit(solution)/shard_map/all_to_all | solution.py:614
  29.8 0.6 %head.1.refs_0_ = bf16[96,128]{1,0:T(8,128)(2,1)S(1)} custom-call(f32[4,512,256]{2,1,0:T(8,128)S(1)} %get-tuple-element.23.conv_ref, f32[8,2,128]{2,1,0:T(2,128)S(1)} %all_to_all.10.stats_ref, f32[8,512]{1,0:T(8,128)S(1)} %get-tuple-element.22.params_ref, bf16[2,24,256]{2,1,0:T(8,128)(2,1)S(1)} %get-tuple-element.25.heads_ref, ...), custom_call_target="tpu_custom_call" | custom-call | tf_op jit(solution)/shard_map/head/pallas_call | solution.py:615
  30.4 0.0 collective-permute-start.2
  30.5 0.8 %collective-permute-start.1 = (bf16[96,128]{1,0:T(8,128)(2,1)S(1)}, bf16[96,128]{1,0:T(8,128)(2,1)S(1)}, u32[]{:S(2)}, u32[]{:S(2)}) collective-permute-start(bf16[96,128]{1,0:T(8,128)(2,1)S(1)} %head.1.refs_0_), channel_id=1, source_target_pairs={{0,16},{8,24},{16,0},{24,8},{1,17},{9,25},{17,1},{25,9},{2,18},{10... | collective-permute-start | bytes 73736 | tf_op jit(solution)/shard_map/ppermute | solution.py:624
  31.3 1.0 %collective-permute-start = (bf16[96,128]{1,0:T(8,128)(2,1)S(1)}, bf16[96,128]{1,0:T(8,128)(2,1)S(1)}, u32[]{:S(2)}, u32[]{:S(2)}) collective-permute-start(bf16[96,128]{1,0:T(8,128)(2,1)S(1)} %head.1.refs_0_), channel_id=1, source_target_pairs={{0,8},{8,0},{16,24},{24,16},{1,9},{9,1},{17,25},{25,17},{2,10},{10... | collective-permute-start | bytes 73736 | tf_op jit(solution)/shard_map/ppermute | solution.py:624
  32.3 1.4 %collective-permute-done.2.refs_3_ = bf16[96,128]{1,0:T(8,128)(2,1)S(1)} collective-permute-done((bf16[96,128]{1,0:T(8,128)(2,1)S(1)}, bf16[96,128]{1,0:T(8,128)(2,1)S(1)}, u32[]{:S(2)}, u32[]{:S(2)}) %collective-permute-start.2) | collective-permute-done | bytes 24608 | tf_op jit(solution)/shard_map/ppermute | solution.py:624
  33.7 0.7 %collective-permute-done.1.refs_2_ = bf16[96,128]{1,0:T(8,128)(2,1)S(1)} collective-permute-done((bf16[96,128]{1,0:T(8,128)(2,1)S(1)}, bf16[96,128]{1,0:T(8,128)(2,1)S(1)}, u32[]{:S(2)}, u32[]{:S(2)}) %collective-permute-start.1) | collective-permute-done | bytes 24608 | tf_op jit(solution)/shard_map/ppermute | solution.py:624
  34.4 0.0 collective-permute-done.refs_1_
  34.5 0.8 %place.1 = f32[8,3,2,256]{3,2,1,0:T(2,128)} custom-call(s32[8,128]{1,0:T(8,128)S(1)} %get-tuple-element.16.corner_ref, f32[4,48,256]{2,1,0:T(8,128)S(1)} %get-tuple-element.17.weights_ref, bf16[96,128]{1,0:T(8,128)(2,1)S(1)} %head.1.refs_0_, bf16[96,128]{1,0:T(8,128)(2,1)S(1)} %collective-permute-done.refs_1_, ...), custom_call_target="tpu_custom_call" | custom-call | tf_op jit(solution)/shard_map/place/pallas_call | solution.py:627
Async XLA Ops:
  1.4 15.5 %all-to-all-start = ((bf16[32,16,128]{2,1,0:T(8,128)(2,1)}), bf16[32,16,128]{2,1,0:T(8,128)(2,1)S(1)}, u32[]{:S(2)}, u32[]{:S(2)}) async-start(bf16[32,16,128]{2,1,0:T(8,128)(2,1)} %cut.1), calls=%async_computation | async-start | bytes 262144 | tf_op jit(solution)/shard_map/all_to_all | solution.py:555
  30.4 3.3 %collective-permute-start.2 = (bf16[96,128]{1,0:T(8,128)(2,1)S(1)}, bf16[96,128]{1,0:T(8,128)(2,1)S(1)}, u32[]{:S(2)}, u32[]{:S(2)}) collective-permute-start(bf16[96,128]{1,0:T(8,128)(2,1)S(1)} %head.1.refs_0_), channel_id=1, source_target_pairs={{0,24},{8,16},{16,8},{24,0},{1,25},{9,17},{17,9},{25,1},{2,26},{10... | collective-permute-start | bytes 73736 | tf_op jit(solution)/shard_map/ppermute | solution.py:624
  30.5 4.0 %collective-permute-start.1 = (bf16[96,128]{1,0:T(8,128)(2,1)S(1)}, bf16[96,128]{1,0:T(8,128)(2,1)S(1)}, u32[]{:S(2)}, u32[]{:S(2)}) collective-permute-start(bf16[96,128]{1,0:T(8,128)(2,1)S(1)} %head.1.refs_0_), channel_id=1, source_target_pairs={{0,16},{8,24},{16,0},{24,8},{1,17},{9,25},{17,1},{25,9},{2,18},{10... | collective-permute-start | bytes 73736 | tf_op jit(solution)/shard_map/ppermute | solution.py:624
  31.3 3.2 %collective-permute-start = (bf16[96,128]{1,0:T(8,128)(2,1)S(1)}, bf16[96,128]{1,0:T(8,128)(2,1)S(1)}, u32[]{:S(2)}, u32[]{:S(2)}) collective-permute-start(bf16[96,128]{1,0:T(8,128)(2,1)S(1)} %head.1.refs_0_), channel_id=1, source_target_pairs={{0,8},{8,0},{16,24},{24,16},{1,9},{9,1},{17,25},{25,17},{2,10},{10... | collective-permute-start | bytes 73736 | tf_op jit(solution)/shard_map/ppermute | solution.py:624
